TPU v7x, 32 devices: a whole 2x2x4 slice. The times are simulated.
32 devices in a mesh: parts: 2 (over x), tiles: 16 (over z, y, core).
Axes of the slice: x: 2, y: 2, z: 4, core: 2. Of those that a mesh axis runs over, the one named last changes fastest.
Arguments:
- mask_params: float32 [4096, 1024], P(('parts', 'tiles')), parts along dimension 0, may hold values from -6 to 6
- target: int32 [4096, 1024], P(('parts', 'tiles')), parts along dimension 0, may hold values 0 or 1
- kernel_spectra: float32 [2, 16, 32, 128], replicated, may hold values from -0.0625 to 0.0625
- kernel_weights: float32 [16], replicated, may hold values from 0.05 to 1
Outputs:
- resist_image: float32 [4096, 1024], P(('parts', 'tiles')), parts along dimension 0
- mask_gradient: float32 [4096, 1024], P(('parts', 'tiles')), parts along dimension 0
There are 2 independent parts, one for each index of `parts`. A program takes and returns all parts, laid end to end along the dimension named above; an argument that names none is the same for every part. Nothing has to cross between parts.
All inputs are finite; a program needn't handle non-finite values. No bound on the sum of `target` on one device may be relied on, other than what follows from the above.
Results may differ from a plain program's by a relative error of at most 0.0003.
Values sent between devices are 32-bit elements; how exact they have to be, the bound alone decides.
No kernel may reach another device: no remote copies, remote signals or barrier semaphores. Data moves between devices by JAX's collectives and lax.ppermute only.
A program may use at most 64 MiB of HBM per device.

v0:
```python
import math

import jax
import jax.numpy as jnp
from jax import lax
from jax.sharding import PartitionSpec as P

MARGIN = 64


STEEPNESS = 8.0
THRESHOLD = 0.35
HIGHEST = lax.Precision.HIGHEST


def with_halo(block, sides, width):
    for axis, dim in sides:
        count = lax.axis_size(axis)
        forward = [(i, i + 1) for i in range(count - 1)]
        forward.append((count - 1, 0))
        backward = [(target, source) for source, target in forward]
        low = lax.ppermute(
            lax.slice_in_dim(block, block.shape[dim] - width, None, axis=dim), axis, forward
        )
        high = lax.ppermute(lax.slice_in_dim(block, 0, width, axis=dim), axis, backward)
        block = jnp.concatenate([low, block, high], axis=dim)
    return block


def matmul(left, right):
    return jnp.dot(left, right, precision=HIGHEST, preferred_element_type=jnp.float32)


def phase_table(frequencies, positions, length):
    cycles = jnp.remainder(frequencies[:, None] * positions[None, :], length).astype(jnp.float32)
    angles = cycles * (2.0 * math.pi / length)
    return (jnp.cos(angles), jnp.sin(angles))


def make_tables(strip_rows, margin, columns, freq_rows, freq_cols):
    window = strip_rows + 2 * margin
    col_freq = jnp.arange(freq_cols, dtype=jnp.int32) - freq_cols // 2
    row_freq = jnp.arange(freq_rows, dtype=jnp.int32) - freq_rows // 2
    col_cos, col_sin = phase_table(col_freq, jnp.arange(columns, dtype=jnp.int32), columns)
    row_cos, row_sin = phase_table(row_freq, jnp.arange(window, dtype=jnp.int32), window)
    factor = 1.0 / math.sqrt(window * columns)
    forward_cols = jnp.concatenate([col_cos.T, -col_sin.T], axis=1) * factor
    row_stack = jnp.concatenate([row_cos, row_sin], axis=0)
    own_rows = row_stack[:, margin : margin + strip_rows].T
    inverse_cols = jnp.concatenate(
        [jnp.concatenate([col_cos, col_sin], axis=1), jnp.concatenate([-col_sin, col_cos], axis=1)],
        axis=0,
    )
    return (forward_cols, row_stack, own_rows, inverse_cols)


def kernel_fields(window_spec, kernel_spectra, own_rows):
    half_rows = window_spec.shape[0] // 2
    half_cols = window_spec.shape[1] // 2
    spec_real = window_spec[:half_rows, :half_cols] + window_spec[half_rows:, half_cols:]
    spec_imag = window_spec[:half_rows, half_cols:] - window_spec[half_rows:, :half_cols]
    kern_real = kernel_spectra[0]
    kern_imag = kernel_spectra[1]
    prod_real = kern_real * spec_real - kern_imag * spec_imag
    prod_imag = kern_real * spec_imag + kern_imag * spec_real
    blocked = jnp.concatenate(
        [
            jnp.concatenate([prod_real, prod_imag], axis=2),
            jnp.concatenate([-prod_imag, prod_real], axis=2),
        ],
        axis=1,
    )
    return jnp.einsum("pr,krc->kpc", own_rows, blocked, precision=HIGHEST)


def window_adjoint(inner_grad, kernel_spectra, own_rows):
    half_rows = own_rows.shape[1] // 2
    half_cols = inner_grad.shape[2] // 2
    spec_grad = jnp.einsum("pr,kpc->krc", own_rows, inner_grad, precision=HIGHEST)
    grad_real = spec_grad[:, :half_rows, :half_cols] + spec_grad[:, half_rows:, half_cols:]
    grad_imag = spec_grad[:, :half_rows, half_cols:] - spec_grad[:, half_rows:, :half_cols]
    kern_real = kernel_spectra[0]
    kern_imag = kernel_spectra[1]
    win_real = jnp.sum(grad_real * kern_real + grad_imag * kern_imag, axis=0)
    win_imag = jnp.sum(grad_imag * kern_real - grad_real * kern_imag, axis=0)
    return jnp.concatenate(
        [
            jnp.concatenate([win_real, win_imag], axis=1),
            jnp.concatenate([-win_imag, win_real], axis=1),
        ],
        axis=0,
    )


def shards(mask_params, target, kernel_spectra, kernel_weights):
    strip_rows, columns = mask_params.shape
    margin = MARGIN
    freq_rows = kernel_spectra.shape[2]
    freq_cols = kernel_spectra.shape[3]
    kernels = kernel_spectra.shape[1]
    forward_cols, row_stack, own_rows, inverse_cols = make_tables(
        strip_rows, margin, columns, freq_rows, freq_cols
    )
    transmit = jnp.tanh(mask_params)
    padded = with_halo(transmit, (("tiles", 0),), margin)
    window_spec = matmul(row_stack, matmul(padded, forward_cols))
    inner = kernel_fields(window_spec, kernel_spectra, own_rows)
    blocks = kernels // 4
    shares = kernel_weights / jnp.sum(kernel_weights)
    inner_blocks = inner.reshape(blocks, 4, strip_rows, 2 * freq_cols)
    share_blocks = shares.reshape(blocks, 4)

    def add_power(totals, items):
        inner_block, share_block = items
        fields = jnp.einsum("kpc,cw->kpw", inner_block, inverse_cols, precision=HIGHEST)
        powers = fields[:, :, :columns] ** 2 + fields[:, :, columns:] ** 2
        return (totals + jnp.einsum("k,kpw->pw", share_block, powers, precision=HIGHEST), fields)

    intensity, field_blocks = lax.scan(
        add_power, jnp.zeros((strip_rows, columns), jnp.float32), (inner_blocks, share_blocks)
    )
    resist = jax.nn.sigmoid(STEEPNESS * (intensity - THRESHOLD))
    slopes = 2.0 * (resist - target.astype(jnp.float32)) * STEEPNESS * resist * (1.0 - resist)
    doubled = jnp.concatenate([slopes, slopes], axis=1)

    def adjoint_block(running, items):
        fields, share_block = items
        field_grad = (2.0 * share_block)[:, None, None] * doubled[None] * fields
        return (running, jnp.einsum("kpw,cw->kpc", field_grad, inverse_cols, precision=HIGHEST))

    _, inner_grad = lax.scan(
        adjoint_block, jnp.zeros((), jnp.float32), (field_blocks, share_blocks)
    )
    inner_grad = inner_grad.reshape(kernels, strip_rows, 2 * freq_cols)
    window_grad = window_adjoint(inner_grad, kernel_spectra, own_rows)
    framed_grad = with_halo(window_grad[None], (("tiles", 0),), 1)
    merged_grad = matmul(row_stack[:, margin : margin + strip_rows].T, window_grad)
    merged_grad = merged_grad.at[:margin].add(
        matmul(row_stack[:, margin + strip_rows :].T, framed_grad[0])
    )
    merged_grad = merged_grad.at[strip_rows - margin :].add(
        matmul(row_stack[:, :margin].T, framed_grad[2])
    )
    mask_grad = matmul(merged_grad, forward_cols.T)
    gradient = mask_grad * (1.0 - transmit * transmit)
    return (resist, gradient)


def solution(mesh):
    in_specs = (P(("parts", "tiles"), None), P(("parts", "tiles"), None), P(), P())
    out_specs = (P(("parts", "tiles"), None), P(("parts", "tiles"), None))
    return jax.shard_map(shards, mesh=mesh, in_specs=in_specs, out_specs=out_specs, check_vma=False)
```

profile of v0, /device:TPU:0, one launch (start us, length us, event | category | flops | bytes accessed | tf_op | source)
XLA Modules:
  0.0 110.3 jit_solution(16681351055351591656)
XLA Ops:
  3.1 5.0 %collective-permute-start.1 = (f32[64,1024]{1,0:T(8,128)S(1)}, f32[64,1024]{1,0:T(8,128)}, u32[]{:S(2)}, u32[]{:S(2)}) collective-permute-start(f32[64,1024]{1,0:T(8,128)S(1)} %get-tuple-element.155), channel_id=1, source_target_pairs={{1,0},{2,1},{3,2},{4,3},{5,4},{6,5},{7,6},{8,7},{9,8},{10,9},{11,1... | collective-permute-start | bytes 786440 | tf_op jit(solution)/shard_map/ppermute | solution.py:25
  8.3 3.1 %fusion.61 = (f32[128,1024]{1,0:T(8,128)S(1)}, f32[128,1024]{1,0:T(8,128)S(1)}, f32[128,1024]{1,0:T(8,128)}) fusion(s32[128]{0:T(128)S(1)} %iota_add_fusion), kind=kLoop, calls=%fused_computation.89 | loop fusion | flops 1966080 | bytes 1573376 | tf_op jit(solution)/shard_map/sin | solution.py:37
  14.2 2.1 %fusion.63 = (f32[1024,128]{1,0:T(8,128)S(1)}, f32[1024,128]{1,0:T(8,128)S(1)}) fusion(s32[128]{0:T(128)S(1)} %iota_add_fusion), kind=kLoop, calls=%fused_computation.91 | loop fusion | flops 1966080 | bytes 1049088 | tf_op jit(solution)/shard_map/cos | solution.py:37
  16.4 2.6 %fusion.27 = f32[256,256]{1,0:T(8,128)S(1)} fusion(f32[64,1024]{1,0:T(8,128)} %collective-permute-done.1, f32[128,1024]{1,0:T(8,128)} %copy-done.7, f32[64,1024]{1,0:T(8,128)} %collective-permute-done, f32[1024,128]{1,0:T(8,128)S(1)} %get-tuple-element.164, f32[1024,128]{1,0:T(8,128)S(1)} %get-tuple-element.163), kind=kOutput, calls=%fused_computation.34 | convolution fusion | flops 806354944 | bytes 2359296 | tf_op jit(solution)/shard_map/dot_general | solution.py:31
  19.3 4.8 %fusion.33 = f32[16,256,128]{2,1,0:T(8,128)} fusion(f32[16,32,128]{2,1,0:T(8,128)S(1)} %get-tuple-element.153, f32[16,32,128]{2,1,0:T(8,128)S(1)} %get-tuple-element.149, f32[16,32,128]{2,1,0:T(8,128)S(1)} %get-tuple-element.150, f32[32,256]{1,0:T(8,128)S(1)} %get-tuple-element.161, f32[32,256]{1,0:T(8,128)S(1)} %get-tuple-element.162), kind=kOutput, calls=%fused_computation.41 | convolution fusion | flops 403447808 | bytes 2949120 | tf_op jit(solution)/shard_map/pr,krc->kpc/dot_general | solution.py:73
  24.1 45.1 %while.26 = (s32[]{:T(128)}, f32[128,1024]{1,0:T(8,128)S(1)}, f32[4,4,128,2048]{3,2,1,0:T(8,128)}, f32[4,4]{1,0:T(4,128)S(1)}, f32[4,4,128,256]{2,3,1,0:T(8,128)...) while((s32[]{:T(128)}, f32[128,1024]{1,0:T(8,128)S(1)}, f32[4,4,128,2048]{3,2,1,0:T(8,128)}, ...), condition=%wide.region_2.3_spmd.clone, body=%wide.region_1.2_spmd.clone.sunk | while | flops 3229351936 | bytes 21497440 | solution.py:119
  24.1 6.1 %bitcast_dynamic-update-slice_fusion.2 = (f32[4,4,128,2048]{3,2,1,0:T(8,128)}, f32[4,128,2048]{2,1,0:T(8,128)S(1)}) fusion(f32[4,4,128,2048]{3,2,1,0:T(8,128)} %get-tuple-element.253, s32[]{:T(128)} %get-tuple-element.251, f32[256,2048]{1,0:T(8,128)S(1)} %get-tuple-element.264, f32[4,4,128,256]{2,3,1,0:T(8,128)} %get-tuple-element.263), kind=kOutput, calls=%fused_computation.13.clone.1 | convolution fusion | flops 3221225472 | bytes 11011072 | tf_op jit(solution)/shard_map/while/body/eval_jaxpr/kpc,cw->kpw/dot_general | solution.py:115
  30.9 4.3 %fusion.116 = f32[1,128,1024]{2,0,1:T(1,128)S(1)} fusion(f32[4,128,1024]{2,1,0:T(8,128)S(1)} %fusion.115, f32[4,4]{1,0:T(4,128)S(1)} %get-tuple-element.262, s32[]{:T(128)} %get-tuple-element.251), kind=kOutput, calls=%fused_computation.19.clone.1 | convolution fusion | flops 6291456 | bytes 2621956 | tf_op jit(solution)/shard_map/while/body/eval_jaxpr/k,kpw->pw/dot_general | solution.py:117
  35.4 6.1 %bitcast_dynamic-update-slice_fusion.2 = (f32[4,4,128,2048]{3,2,1,0:T(8,128)}, f32[4,128,2048]{2,1,0:T(8,128)S(1)}) fusion(f32[4,4,128,2048]{3,2,1,0:T(8,128)} %get-tuple-element.253, s32[]{:T(128)} %get-tuple-element.251, f32[256,2048]{1,0:T(8,128)S(1)} %get-tuple-element.264, f32[4,4,128,256]{2,3,1,0:T(8,128)} %get-tuple-element.263), kind=kOutput, calls=%fused_computation.13.clone.1 | convolution fusion | flops 3221225472 | bytes 11011072 | tf_op jit(solution)/shard_map/while/body/eval_jaxpr/kpc,cw->kpw/dot_general | solution.py:115
  42.2 4.3 %fusion.116 = f32[1,128,1024]{2,0,1:T(1,128)S(1)} fusion(f32[4,128,1024]{2,1,0:T(8,128)S(1)} %fusion.115, f32[4,4]{1,0:T(4,128)S(1)} %get-tuple-element.262, s32[]{:T(128)} %get-tuple-element.251), kind=kOutput, calls=%fused_computation.19.clone.1 | convolution fusion | flops 6291456 | bytes 2621956 | tf_op jit(solution)/shard_map/while/body/eval_jaxpr/k,kpw->pw/dot_general | solution.py:117
  46.7 6.1 %bitcast_dynamic-update-slice_fusion.2 = (f32[4,4,128,2048]{3,2,1,0:T(8,128)}, f32[4,128,2048]{2,1,0:T(8,128)S(1)}) fusion(f32[4,4,128,2048]{3,2,1,0:T(8,128)} %get-tuple-element.253, s32[]{:T(128)} %get-tuple-element.251, f32[256,2048]{1,0:T(8,128)S(1)} %get-tuple-element.264, f32[4,4,128,256]{2,3,1,0:T(8,128)} %get-tuple-element.263), kind=kOutput, calls=%fused_computation.13.clone.1 | convolution fusion | flops 3221225472 | bytes 11011072 | tf_op jit(solution)/shard_map/while/body/eval_jaxpr/kpc,cw->kpw/dot_general | solution.py:115
  53.5 4.3 %fusion.116 = f32[1,128,1024]{2,0,1:T(1,128)S(1)} fusion(f32[4,128,1024]{2,1,0:T(8,128)S(1)} %fusion.115, f32[4,4]{1,0:T(4,128)S(1)} %get-tuple-element.262, s32[]{:T(128)} %get-tuple-element.251), kind=kOutput, calls=%fused_computation.19.clone.1 | convolution fusion | flops 6291456 | bytes 2621956 | tf_op jit(solution)/shard_map/while/body/eval_jaxpr/k,kpw->pw/dot_general | solution.py:117
  58.0 6.1 %bitcast_dynamic-update-slice_fusion.2 = (f32[4,4,128,2048]{3,2,1,0:T(8,128)}, f32[4,128,2048]{2,1,0:T(8,128)S(1)}) fusion(f32[4,4,128,2048]{3,2,1,0:T(8,128)} %get-tuple-element.253, s32[]{:T(128)} %get-tuple-element.251, f32[256,2048]{1,0:T(8,128)S(1)} %get-tuple-element.264, f32[4,4,128,256]{2,3,1,0:T(8,128)} %get-tuple-element.263), kind=kOutput, calls=%fused_computation.13.clone.1 | convolution fusion | flops 3221225472 | bytes 11011072 | tf_op jit(solution)/shard_map/while/body/eval_jaxpr/kpc,cw->kpw/dot_general | solution.py:115
  64.7 4.3 %fusion.116 = f32[1,128,1024]{2,0,1:T(1,128)S(1)} fusion(f32[4,128,1024]{2,1,0:T(8,128)S(1)} %fusion.115, f32[4,4]{1,0:T(4,128)S(1)} %get-tuple-element.262, s32[]{:T(128)} %get-tuple-element.251), kind=kOutput, calls=%fused_computation.19.clone.1 | convolution fusion | flops 6291456 | bytes 2621956 | tf_op jit(solution)/shard_map/while/body/eval_jaxpr/k,kpw->pw/dot_general | solution.py:117
  69.3 2.1 %subtract_multiply_fusion = (f32[128,1024]{1,0:T(8,128)S(1)}, f32[128,1024]{1,0:T(8,128)}) fusion(s32[128,1024]{1,0:T(8,128)} %param.13, f32[128,1024]{1,0:T(8,128)S(1)} %get-tuple-element.91), kind=kLoop, calls=%fused_computation.62 | loop fusion | flops 1441792 | bytes 2097152 | tf_op jit(solution)/shard_map/mul | solution.py:123
  71.4 26.6 %while.25 = (s32[]{:T(128)}, f32[4,4,128,256]{3,2,1,0:T(8,128)}, f32[4,4]{1,0:T(4,128)S(1)}, f32[128,2048]{1,0:T(8,128)S(1)}, f32[4,4,128,2048]{3,2,1,0:T(8,128)}, /*index=5*/f32[256,2048]{1,0:T(8,128)S(1)}, s32[]{:T(128)}) while((s32[]{:T(128)}, f32[4,4,128,256]{3,2,1,0:T(8,128)}, f32[4,4]{1,0:T(4,128)S(1)}, f32[128,2048]{1,0:T(8,128)S(1)}, ...), condition=%wide.region_4.5_spmd, body=%wide.region_3.4_spmd.sunk | while | flops 3223322624 | bytes 7865473 | solution.py:131
  71.5 6.6 %fusion.112 = f32[4,4,128,256]{3,2,1,0:T(8,128)} fusion(f32[4,4,128,256]{3,2,1,0:T(8,128)} %get-tuple-element.275, s32[]{:T(128)} %get-tuple-element.274, f32[256,2048]{1,0:T(8,128)S(1)} %get-tuple-element.286, f32[4,4,128,2048]{3,2,1,0:T(8,128)} %get-tuple-element.285, f32[128,2048]{1,0:T(8,128)S(1)} %get-tuple-element.284, f32[4]{0:T(128)S(1)} %fusion.111), kind=kOutput, calls=%fused_computation.8.clone.1 | convolution fusion | flops 3223322624 | bytes 7865360 | tf_op jit(solution)/shard_map/while/body/eval_jaxpr/kpw,cw->kpc/dot_general | solution.py:129
  78.1 6.6 %fusion.112 = f32[4,4,128,256]{3,2,1,0:T(8,128)} fusion(f32[4,4,128,256]{3,2,1,0:T(8,128)} %get-tuple-element.275, s32[]{:T(128)} %get-tuple-element.274, f32[256,2048]{1,0:T(8,128)S(1)} %get-tuple-element.286, f32[4,4,128,2048]{3,2,1,0:T(8,128)} %get-tuple-element.285, f32[128,2048]{1,0:T(8,128)S(1)} %get-tuple-element.284, f32[4]{0:T(128)S(1)} %fusion.111), kind=kOutput, calls=%fused_computation.8.clone.1 | convolution fusion | flops 3223322624 | bytes 7865360 | tf_op jit(solution)/shard_map/while/body/eval_jaxpr/kpw,cw->kpc/dot_general | solution.py:129
  84.7 6.7 %fusion.112 = f32[4,4,128,256]{3,2,1,0:T(8,128)} fusion(f32[4,4,128,256]{3,2,1,0:T(8,128)} %get-tuple-element.275, s32[]{:T(128)} %get-tuple-element.274, f32[256,2048]{1,0:T(8,128)S(1)} %get-tuple-element.286, f32[4,4,128,2048]{3,2,1,0:T(8,128)} %get-tuple-element.285, f32[128,2048]{1,0:T(8,128)S(1)} %get-tuple-element.284, f32[4]{0:T(128)S(1)} %fusion.111), kind=kOutput, calls=%fused_computation.8.clone.1 | convolution fusion | flops 3223322624 | bytes 7865360 | tf_op jit(solution)/shard_map/while/body/eval_jaxpr/kpw,cw->kpc/dot_general | solution.py:129
  91.4 6.6 %fusion.112 = f32[4,4,128,256]{3,2,1,0:T(8,128)} fusion(f32[4,4,128,256]{3,2,1,0:T(8,128)} %get-tuple-element.275, s32[]{:T(128)} %get-tuple-element.274, f32[256,2048]{1,0:T(8,128)S(1)} %get-tuple-element.286, f32[4,4,128,2048]{3,2,1,0:T(8,128)} %get-tuple-element.285, f32[128,2048]{1,0:T(8,128)S(1)} %get-tuple-element.284, f32[4]{0:T(128)S(1)} %fusion.111), kind=kOutput, calls=%fused_computation.8.clone.1 | convolution fusion | flops 3223322624 | bytes 7865360 | tf_op jit(solution)/shard_map/while/body/eval_jaxpr/kpw,cw->kpc/dot_general | solution.py:129
  98.0 3.0 %convolution_bitcast_fusion = f32[16,64,256]{2,1,0:T(8,128)S(1)} fusion(f32[16,128,256]{2,1,0:T(8,128)} %bitcast.113, f32[32,256]{1,0:T(8,128)S(1)} %get-tuple-element.161, f32[32,256]{1,0:T(8,128)S(1)} %get-tuple-element.162), kind=kOutput, calls=%fused_computation.28 | convolution fusion | flops 402661376 | bytes 3211264 | tf_op jit(solution)/shard_map/pr,kpc->krc/dot_general | solution.py:79
  101.3 4.4 %collective-permute-start.3 = (f32[1,64,256]{2,1,0:T(8,128)S(1)}, f32[1,64,256]{2,1,0:T(8,128)S(1)}, u32[]{:S(2)}, u32[]{:S(2)}) collective-permute-start(f32[1,64,256]{2,1,0:T(8,128)S(1)} %fusion.68), channel_id=1, source_target_pairs={{1,0},{2,1},{3,2},{4,3},{5,4},{6,5},{7,6},{8,7},{9,8},{10,9},{11,1... | collective-permute-start | bytes 196616 | tf_op jit(solution)/shard_map/ppermute | solution.py:25
  106.1 1.6 %collective-permute-done.2 = f32[1,64,256]{2,1,0:T(8,128)S(1)} collective-permute-done((f32[1,64,256]{2,1,0:T(8,128)S(1)}, f32[1,64,256]{2,1,0:T(8,128)S(1)}, u32[]{:S(2)}, u32[]{:S(2)}) %collective-permute-start.2) | collective-permute-done | bytes 65568 | tf_op jit(solution)/shard_map/ppermute | solution.py:22
  108.3 1.9 %convolution_multiply_fusion = f32[128,1024]{1,0:T(8,128)} fusion(f32[128,256]{1,0:T(8,128)S(1)} %fusion.25, f32[1024,128]{1,0:T(8,128)S(1)} %copy-done.4, f32[1024,128]{1,0:T(8,128)S(1)} %copy-done.2, f32[128,1024]{1,0:T(8,128)S(1)} %copy-done), kind=kOutput, calls=%fused_computation.29 | convolution fusion | flops 403570688 | bytes 2228224 | tf_op jit(solution)/shard_map/dot_general | solution.py:31
  (57 shorter events, 10.4 us)
Async XLA Ops:
  0.6 10.8 %copy-start.8 = (f32[16]{0:T(128)S(1)}, f32[16]{0:T(128)}, u32[]{:S(2)}) copy-start(f32[16]{0:T(128)} %param.15) | copy-start | bytes 196
  1.8 6.3 %copy-start.7 = (f32[128,1024]{1,0:T(8,128)}, f32[128,1024]{1,0:T(8,128)S(1)}, u32[]{:S(2)}) copy-start(f32[128,1024]{1,0:T(8,128)S(1)} %tanh.3) | copy-start | bytes 1572868
  2.6 13.7 %collective-permute-start = (f32[64,1024]{1,0:T(8,128)}, f32[64,1024]{1,0:T(8,128)}, u32[]{:S(2)}, u32[]{:S(2)}) collective-permute-start(f32[64,1024]{1,0:T(8,128)} %get-tuple-element.154), channel_id=1, source_target_pairs={{0,1},{1,2},{2,3},{3,4},{4,5},{5,6},{6,7},{7,8},{8,9},{9,10},{10,1... | collective-permute-start | bytes 786440 | tf_op jit(solution)/shard_map/ppermute | solution.py:22
  3.1 13.3 %collective-permute-start.1 = (f32[64,1024]{1,0:T(8,128)S(1)}, f32[64,1024]{1,0:T(8,128)}, u32[]{:S(2)}, u32[]{:S(2)}) collective-permute-start(f32[64,1024]{1,0:T(8,128)S(1)} %get-tuple-element.155), channel_id=1, source_target_pairs={{1,0},{2,1},{3,2},{4,3},{5,4},{6,5},{7,6},{8,7},{9,8},{10,9},{11,1... | collective-permute-start | bytes 786440 | tf_op jit(solution)/shard_map/ppermute | solution.py:25
  14.2 5.0 %copy-start.5 = (f32[2,16,32,128]{3,2,1,0:T(8,128)S(1)}, f32[2,16,32,128]{3,2,1,0:T(8,128)}, u32[]{:S(2)}) copy-start(f32[2,16,32,128]{3,2,1,0:T(8,128)} %param.14) | copy-start | bytes 1572868
  16.3 3.0 %copy-start.1 = (f32[1024,128]{1,0:T(8,128)}, f32[1024,128]{1,0:T(8,128)S(1)}, u32[]{:S(2)}) copy-start(f32[1024,128]{1,0:T(8,128)S(1)} %get-tuple-element.163) | copy-start | bytes 1572868
  16.3 3.0 %copy-start.3 = (f32[1024,128]{1,0:T(8,128)}, f32[1024,128]{1,0:T(8,128)S(1)}, u32[]{:S(2)}) copy-start(f32[1024,128]{1,0:T(8,128)S(1)} %get-tuple-element.164) | copy-start | bytes 1572868
  98.0 3.1 %copy-start.6 = (f32[2,16,32,128]{3,2,1,0:T(8,128)S(1)}, f32[2,16,32,128]{3,2,1,0:T(8,128)}, u32[]{:S(2)}) copy-start(f32[2,16,32,128]{3,2,1,0:T(8,128)} %param.14) | copy-start | bytes 1572868
  98.0 10.3 %copy-start = (f32[128,1024]{1,0:T(8,128)S(1)}, f32[128,1024]{1,0:T(8,128)}, u32[]{:S(2)}) copy-start(f32[128,1024]{1,0:T(8,128)} %param.12) | copy-start | bytes 1572868
  98.0 10.3 %copy-start.2 = (f32[1024,128]{1,0:T(8,128)S(1)}, f32[1024,128]{1,0:T(8,128)}, u32[]{:S(2)}) copy-start(f32[1024,128]{1,0:T(8,128)} %copy-done.1) | copy-start | bytes 1572868
  98.0 10.3 %copy-start.4 = (f32[1024,128]{1,0:T(8,128)S(1)}, f32[1024,128]{1,0:T(8,128)}, u32[]{:S(2)}) copy-start(f32[1024,128]{1,0:T(8,128)} %copy-done.3) | copy-start | bytes 1572868
  101.2 6.4 %collective-permute-start.2 = (f32[1,64,256]{2,1,0:T(8,128)S(1)}, f32[1,64,256]{2,1,0:T(8,128)S(1)}, u32[]{:S(2)}, u32[]{:S(2)}) collective-permute-start(f32[1,64,256]{2,1,0:T(8,128)S(1)} %fusion.68), channel_id=1, source_target_pairs={{0,1},{1,2},{2,3},{3,4},{4,5},{5,6},{6,7},{7,8},{8,9},{9,10},{10,1... | collective-permute-start | bytes 196616 | tf_op jit(solution)/shard_map/ppermute | solution.py:22
  101.3 6.7 %collective-permute-start.3 = (f32[1,64,256]{2,1,0:T(8,128)S(1)}, f32[1,64,256]{2,1,0:T(8,128)S(1)}, u32[]{:S(2)}, u32[]{:S(2)}) collective-permute-start(f32[1,64,256]{2,1,0:T(8,128)S(1)} %fusion.68), channel_id=1, source_target_pairs={{1,0},{2,1},{3,2},{4,3},{5,4},{6,5},{7,6},{8,7},{9,8},{10,9},{11,1... | collective-permute-start | bytes 196616 | tf_op jit(solution)/shard_map/ppermute | solution.py:25
where the time goes:
time: 111 us; the launch traced here: 110 us
  matrix products  81.7 us (74%)
  other arithmetic  13.8 us (12%)
  starting transfers between devices  9.96 us (9%)
  local copies, waits for them, and re-layouts  2.06 us (2%)
  waiting for transfers between devices  1.56 us (1%)
    dot_general x4, matrix products, adjoint_block(): jnp.einsum('kpw,cw->kpc', field_grad, inverse_cols, precision=HIGHEST)  26.5 us
    dot_general x4, matrix products, add_power(): jnp.einsum('kpc,cw->kpw', inner_block, inverse_cols, precision=HIGHEST)  24.5 us
    dot_general x4, matrix products, add_power(): jnp.einsum('k,kpw->pw', share_block, powers, precision=HIGHEST)  17.2 us
    ppermute x2, starting transfers between devices, with_halo(): lax.ppermute(lax.slice_in_dim(block, 0, width, axis=dim), axis, backward)  9.41 us
    dot_general x6, matrix products, matmul(): jnp.dot(left, right, precision=HIGHEST, preferred_element_type=jnp.float32)  5.73 us
    dot_general x1, matrix products, kernel_fields(): return jnp.einsum('pr,krc->kpc', own_rows, blocked, precision=HIGHEST)  4.79 us
    sin x1, other arithmetic, phase_table(): return (jnp.cos(angles), jnp.sin(angles))  3.15 us
    dot_general x1, matrix products, window_adjoint(): jnp.einsum('pr,kpc->krc', own_rows, inner_grad, precision=HIGHEST)  3.04 us
  transfers between devices with their start and end apart: 4, of which 1 were waited for; matrix products, arithmetic and copies ran while one was open for 8% of the time, Pallas kernels for 0%

commit v1 on v0

v1 whole, which is shorter than its diff:
```python
import functools
import math

import jax
import jax.numpy as jnp
import numpy as np
from jax import lax
from jax.experimental import pallas as pl
from jax.experimental.pallas import tpu as pltpu
from jax.sharding import PartitionSpec as P

MARGIN = 64

STEEPNESS = 8.0
THRESHOLD = 0.35

BF16 = jnp.bfloat16
F32 = jnp.float32


def split_table(table):
    table = np.asarray(table, np.float32)
    high = table.astype(BF16)
    low = (table - high.astype(np.float32)).astype(BF16)
    return high, low


def stack_left(table):
    high, low = split_table(table)
    return np.concatenate([high, high, low], axis=1)


def angles(frequencies, positions, period):
    cycles = np.remainder(frequencies[:, None] * positions[None, :], period)
    return cycles * (2.0 * math.pi / period)


def interpolation(fine, coarse, bound, period):
    count = len(coarse)
    distance = fine[:, None] - coarse[None, :]
    total = np.ones_like(distance, dtype=np.float64)
    for frequency in range(1, bound):
        total += 2.0 * np.cos(np.remainder(frequency * distance, period) * (2.0 * math.pi / period))
    return total / count


def make_tables(strip_rows, margin, columns, freq_rows, freq_cols):
    window = strip_rows + 2 * margin
    row_freq = np.arange(freq_rows, dtype=np.float64) - freq_rows // 2
    col_freq = np.arange(freq_cols, dtype=np.float64) - freq_cols // 2
    rows_c, cols_c = 2 * freq_rows, 2 * freq_cols
    own = np.arange(margin, margin + strip_rows, dtype=np.float64)
    wide = np.arange(columns, dtype=np.float64)
    samples_r = np.arange(rows_c, dtype=np.float64) * (window / rows_c)
    samples_c = np.arange(cols_c, dtype=np.float64) * (columns / cols_c)
    factor = 1.0 / math.sqrt(window * columns)
    col_angle = angles(col_freq, wide, columns)
    forward = np.concatenate([np.cos(col_angle).T, -np.sin(col_angle).T], axis=1) * factor
    row_angle = angles(row_freq, own, window)
    cos_r, sin_r = np.cos(row_angle), np.sin(row_angle)
    half = strip_rows // 2
    none = np.zeros((freq_rows, half))
    first = np.concatenate([cos_r[:, :half], none, sin_r[:, :half], none], axis=1)
    second = np.concatenate([none, cos_r[:, half:], none, sin_r[:, half:]], axis=1)
    project = np.concatenate([first, second], axis=0)
    back_rows = np.concatenate([cos_r, sin_r], axis=0).T
    coarse_r = angles(row_freq, samples_r, window)
    field_rows = np.concatenate([np.cos(coarse_r), np.sin(coarse_r)], axis=0).T
    coarse_c = angles(col_freq, samples_c, columns)
    cos_c, sin_c = np.cos(coarse_c), np.sin(coarse_c)
    field_cols = np.concatenate(
        [np.concatenate([cos_c, sin_c], axis=1), np.concatenate([-sin_c, cos_c], axis=1)], axis=0
    )
    widen_rows = interpolation(own, samples_r, freq_rows, window)
    widen_cols = interpolation(wide, samples_c, freq_cols, columns).T
    return {
        "forward": split_table(forward),
        "project": split_table(project),
        "back_rows": stack_left(back_rows),
        "field_rows": stack_left(field_rows),
        "field_rows_t": stack_left(field_rows.T),
        "field_cols": split_table(field_cols),
        "widen_rows": stack_left(widen_rows),
        "widen_rows_t": stack_left(widen_rows.T),
        "widen_cols": split_table(widen_cols),
    }


def split(value):
    high = value.astype(BF16)
    return high, (value - high.astype(F32)).astype(BF16)


def stack_right(value):
    high, low = split(value)
    return jnp.concatenate([high, low, high], axis=0)


def dot(left, right):
    return jnp.dot(left, right, preferred_element_type=F32)


def dot_t(left, right):
    return lax.dot_general(left, right, (((1,), (1,)), ((), ())), preferred_element_type=F32)


def dot3(left, right):
    (lh, ll), (rh, rl) = left, right
    return dot(lh, rh) + dot(lh, rl) + dot(ll, rh)


def dot3_t(left, right):
    (lh, ll), (rh, rl) = left, right
    return dot_t(lh, rh) + dot_t(lh, rl) + dot_t(ll, rh)


def turn(pair, sign):
    half = pair.shape[1] // 2
    real, imag = pair[:, :half], pair[:, half:]
    if sign > 0:
        turned = jnp.concatenate([-imag, real], axis=1)
    else:
        turned = jnp.concatenate([imag, -real], axis=1)
    return jnp.concatenate([pair, turned], axis=0)


def alternate(shape):
    row = lax.broadcasted_iota(jnp.int32, shape, 0)
    return jnp.where(row % 2 == 0, 1.0, -1.0).astype(F32)


def project_kernel(mask, fwd_h, fwd_l, proj_h, proj_l, low_out, high_out, slope_out):
    transmit = jnp.tanh(mask[...])
    slope_out[...] = 1.0 - transmit * transmit
    spectra = dot3(split(transmit), (fwd_h[...], fwd_l[...]))
    parts = dot3((proj_h[...], proj_l[...]), split(turn(spectra, -1)))
    freq_rows = low_out.shape[0]
    low_out[...] = parts[:freq_rows]
    high_out[...] = parts[freq_rows:]


def image_kernel(
    low, high, before, after, spectra, target, rows_f, rows_t, cols_h, cols_l,
    wide_r, wide_rt, wide_h, wide_l, resist_out, grad_out, fields
):
    kernels, freq_rows, freq_cols = spectra.shape[1:]
    rows_c, cols_c = rows_f.shape[0], 2 * freq_cols
    sign = alternate(low.shape)
    window = low[...] + high[...] + sign * (before[...] + after[...])
    win_re, win_im = window[:, :freq_cols], window[:, freq_cols:]
    group = 4
    total = jnp.zeros((rows_c, cols_c), F32)
    for start in range(0, kernels, group):
        inners = []
        for k in range(start, start + group):
            kern_re, kern_im = spectra[0, k], spectra[1, k]
            prod = jnp.concatenate(
                [kern_re * win_re - kern_im * win_im, kern_re * win_im + kern_im * win_re], axis=1
            )
            inners.append(dot(rows_f[...], stack_right(turn(prod, 1))))
        inner = jnp.concatenate(inners, axis=0)
        field = dot3(split(inner), (cols_h[...], cols_l[...]))
        fields[pl.ds(start * rows_c, group * rows_c), :] = field
        power = field[:, :cols_c] ** 2 + field[:, cols_c:] ** 2
        for j in range(group):
            total = total + power[j * rows_c : (j + 1) * rows_c]
    tall = dot(wide_r[...], stack_right(total))
    intensity = dot3(split(tall), (wide_h[...], wide_l[...]))
    resist = jax.nn.sigmoid(STEEPNESS * (intensity - THRESHOLD))
    resist_out[...] = resist
    slopes = (4.0 * STEEPNESS) * (resist - target[...].astype(F32)) * resist * (1.0 - resist)
    narrow = dot3_t(split(slopes), (wide_h[...], wide_l[...]))
    weight = dot(wide_rt[...], stack_right(narrow))
    weight = jnp.concatenate([weight, weight], axis=1)
    grad_re = jnp.zeros((freq_rows, freq_cols), F32)
    grad_im = jnp.zeros((freq_rows, freq_cols), F32)
    for start in range(0, kernels, group):
        scaled = jnp.concatenate(
            [weight * fields[pl.ds(k * rows_c, rows_c), :] for k in range(start, start + group)],
            axis=0,
        )
        inner = dot3_t(split(scaled), (cols_h[...], cols_l[...]))
        for j in range(group):
            k = start + j
            spec = dot(rows_t[...], stack_right(inner[j * rows_c : (j + 1) * rows_c]))
            real = spec[:freq_rows, :freq_cols] + spec[freq_rows:, freq_cols:]
            imag = spec[:freq_rows, freq_cols:] - spec[freq_rows:, :freq_cols]
            kern_re, kern_im = spectra[0, k], spectra[1, k]
            grad_re = grad_re + real * kern_re + imag * kern_im
            grad_im = grad_im + imag * kern_re - real * kern_im
    grad_out[...] = jnp.concatenate([grad_re, grad_im], axis=1)


def gradient_kernel(own, before, after, slope, rows_b, fwd_h, fwd_l, out):
    half = out.shape[0] // 2
    sign = alternate(own.shape)
    low = stack_right(turn(own[...] + sign * before[...], 1))
    high = stack_right(turn(own[...] + sign * after[...], 1))
    merged = jnp.concatenate([dot(rows_b[:half], low), dot(rows_b[half:], high)], axis=0)
    out[...] = slope[...] * dot3_t(split(merged), (fwd_h[...], fwd_l[...]))


def call(kernel, outs, args, flops, scratch=(), limit=32 << 20):
    vmem = pl.BlockSpec(memory_space=pltpu.VMEM)
    shapes = [jax.ShapeDtypeStruct(shape, F32) for shape in outs]
    moved = sum(math.prod(a.shape) * a.dtype.itemsize for a in args)
    moved += sum(4 * math.prod(shape) for shape in outs)
    return pl.pallas_call(
        kernel,
        out_shape=shapes,
        in_specs=[vmem] * len(args),
        out_specs=[vmem] * len(outs),
        scratch_shapes=scratch,
        compiler_params=pltpu.CompilerParams(vmem_limit_bytes=limit),
        cost_estimate=pl.CostEstimate(flops=flops, bytes_accessed=moved, transcendentals=0),
    )(*args)


def shards(mask_params, target, kernel_spectra, kernel_weights):
    strip_rows, columns = mask_params.shape
    kernels, freq_rows, freq_cols = kernel_spectra.shape[1:]
    assert 2 * MARGIN == strip_rows
    tables = jax.tree.map(
        jnp.asarray, make_tables(strip_rows, MARGIN, columns, freq_rows, freq_cols)
    )
    count = lax.axis_size("tiles")
    forward = [(i, (i + 1) % count) for i in range(count)]
    backward = [(j, i) for i, j in forward]
    pair = (freq_rows, 2 * freq_cols)
    area = strip_rows * columns
    low, high, slope = call(
        project_kernel,
        [pair, pair, (strip_rows, columns)],
        [mask_params, *tables["forward"], *tables["project"]],
        flops=6 * area * 2 * freq_cols,
    )
    before = lax.ppermute(high, "tiles", forward)
    after = lax.ppermute(low, "tiles", backward)
    shares = jnp.sqrt(kernel_weights / jnp.sum(kernel_weights))
    spectra = kernel_spectra * shares[None, :, None, None]
    rows_c, cols_c = 2 * freq_rows, 2 * freq_cols
    resist, grad = call(
        image_kernel,
        [(strip_rows, columns), pair],
        [
            low, high, before, after, spectra, target,
            tables["field_rows"], tables["field_rows_t"], *tables["field_cols"],
            tables["widen_rows"], tables["widen_rows_t"], *tables["widen_cols"],
        ],
        flops=24 * kernels * rows_c * cols_c * cols_c,
        scratch=[pltpu.VMEM((kernels * rows_c, 2 * cols_c), F32)],
    )
    grad_before = lax.ppermute(grad, "tiles", forward)
    grad_after = lax.ppermute(grad, "tiles", backward)
    (gradient,) = call(
        gradient_kernel,
        [(strip_rows, columns)],
        [grad, grad_before, grad_after, slope, tables["back_rows"], *tables["forward"]],
        flops=6 * area * 2 * freq_cols,
    )
    return (resist, gradient)


def solution(mesh):
    in_specs = (P(("parts", "tiles"), None), P(("parts", "tiles"), None), P(), P())
    out_specs = (P(("parts", "tiles"), None), P(("parts", "tiles"), None))
    return jax.shard_map(shards, mesh=mesh, in_specs=in_specs, out_specs=out_specs, check_vma=False)
```

time: 111 us -> 32.6 us (0.29)
  matrix products: 81.7 us -> 0 us
  other arithmetic: 13.8 us -> 2.48 us
  Pallas kernels: 0 us -> 8.15 us
  waiting for transfers between devices: 1.56 us -> 9.5 us
  starting transfers between devices: 9.96 us -> 6.54 us
  local copies, waits for them, and re-layouts: 2.06 us -> 4.71 us
    dot_general x20 -> x0, matrix products: 81.7 us -> none  [the longest x4 26.5 us: adjoint_block(): jnp.einsum('kpw,cw->kpc', field_grad, inverse_cols, precision=HIGHEST)]
    pallas_call x0 -> x3, Pallas kernels: none -> 8.15 us  [call(): pl.pallas_call(kernel, out_shape=shapes, in_specs=[vmem] * len(args), out...]
    ppermute x4, waiting for transfers between devices: 1.56 us -> 9.5 us  [the longest x1 4.44 us: shards(): grad_before = lax.ppermute(grad, 'tiles', forward)]
    unnamed x18 -> x36, local copies, waits for them, and re-layouts: 0.04 us -> 4.71 us
    ppermute x4, starting transfers between devices: 9.96 us -> 6.54 us  [the longest x1 5.52 us: shards(): after = lax.ppermute(low, 'tiles', backward)]
    add x9 -> x0, other arithmetic: 3.31 us -> none  [the longest x4 2.52 us: add_power(): powers = fields[:, :, :columns] ** 2 + fields[:, :, columns:] ** 2]
    sin x1 -> x0, other arithmetic: 3.15 us -> none  [phase_table(): return (jnp.cos(angles), jnp.sin(angles))]
    cos x2 -> x0, other arithmetic: 2.29 us -> none  [phase_table(): return (jnp.cos(angles), jnp.sin(angles))]
  transfers between devices with their start and end apart: 4 -> 4, of which waited for: 1 -> 3; matrix products, arithmetic and copies ran while one was open for 8% -> 8% of each run, Pallas kernels for 0% -> 0%
where the time goes in v1:
time: 32.6 us; the launch traced here: 32.2 us
  waiting for transfers between devices  9.5 us (29%)
  Pallas kernels  8.15 us (25%)
  starting transfers between devices  6.54 us (20%)
  local copies, waits for them, and re-layouts  4.71 us (14%)
  other arithmetic  2.48 us (8%)
  between operations  0.81 us (2%)
    pallas_call x3, Pallas kernels, call(): pl.pallas_call(kernel, out_shape=shapes, in_specs=[vmem] * len(args), out...  8.15 us
    ppermute x1, starting transfers between devices, shards(): after = lax.ppermute(low, 'tiles', backward)  5.52 us
    unnamed x36, local copies, waits for them, and re-layouts  4.71 us
    ppermute x1, waiting for transfers between devices, shards(): grad_before = lax.ppermute(grad, 'tiles', forward)  4.44 us
    ppermute x1, waiting for transfers between devices, shards(): before = lax.ppermute(high, 'tiles', forward)  3.46 us
    ppermute x1, waiting for transfers between devices, shards(): grad_after = lax.ppermute(grad, 'tiles', backward)  1.59 us
    mul x1, other arithmetic, shards(): spectra = kernel_spectra * shares[None, :, None, None]  1.23 us
    ppermute x1, starting transfers between devices, shards(): grad_after = lax.ppermute(grad, 'tiles', backward)  1.01 us
  transfers between devices with their start and end apart: 4, of which 3 were waited for; matrix products, arithmetic and copies ran while one was open for 8% of the time, Pallas kernels for 0%

profile of v1, /device:TPU:0, one launch (start us, length us, event | category | flops | bytes accessed | tf_op | source)
XLA Modules:
  0.0 32.2 jit_solution(3674874633310722231)
XLA Ops:
  0.6 0.0 copy-start
  0.6 1.0 %copy-done = bf16[1024,256]{1,0:T(8,128)(2,1)S(1)} copy-done((bf16[1024,256]{1,0:T(8,128)(2,1)S(1)}, bf16[1024,256]{1,0:T(8,128)(2,1)}, u32[]{:S(2)}) %copy-start) | copy-done | bytes 524312
  1.7 1.0 %copy-done.2 = bf16[1024,256]{1,0:T(8,128)(2,1)S(1)} copy-done((bf16[1024,256]{1,0:T(8,128)(2,1)S(1)}, bf16[1024,256]{1,0:T(8,128)(2,1)}, u32[]{:S(2)}) %copy-start.2) | copy-done | bytes 524312
  2.7 1.0 %copy-done.4 = f32[128,1024]{1,0:T(8,128)S(1)} copy-done((f32[128,1024]{1,0:T(8,128)S(1)}, f32[128,1024]{1,0:T(8,128)}, u32[]{:S(2)}) %copy-start.4) | copy-done | bytes 524312
  3.8 0.8 %copy-done.6 = bf16[64,256]{1,0:T(8,128)(2,1)S(1)} copy-done((bf16[64,256]{1,0:T(8,128)(2,1)S(1)}, bf16[64,256]{1,0:T(8,128)(2,1)}, u32[]{:S(2)}) %copy-start.6) | copy-done | bytes 32792
  4.5 0.8 %copy-done.7 = bf16[64,256]{1,0:T(8,128)(2,1)S(1)} copy-done((bf16[64,256]{1,0:T(8,128)(2,1)S(1)}, bf16[64,256]{1,0:T(8,128)(2,1)}, u32[]{:S(2)}) %copy-start.7) | copy-done | bytes 32792
  5.3 0.0 copy-start.14
  5.3 0.0 copy-start.15
  5.3 0.0 copy-start.16
  5.3 0.6 %shard_map.176 = (f32[32,256]{1,0:T(8,128)S(1)}, f32[32,256]{1,0:T(8,128)S(1)}, f32[128,1024]{1,0:T(8,128)S(1)}) custom-call(f32[128,1024]{1,0:T(8,128)S(1)} %copy-done.4, bf16[1024,256]{1,0:T(8,128)(2,1)S(1)} %copy-done.2, bf16[1024,256]{1,0:T(8,128)(2,1)S(1)} %copy-done, bf16[64,256]{1,0:T(8,128)(2,1)S(1)} %copy-done.7, bf16[64,256]{1,0:T(8,128)(2,1)S(1)} %copy-done.6), custom_call_target="tpu_custom_call" | custom-call | flops 201326592 | bytes 2228224 | tf_op jit(solution)/shard_map/pallas_call | solution.py:208
  5.9 5.5 %collective-permute-start.1 = (f32[32,256]{1,0:T(8,128)S(1)}, f32[32,256]{1,0:T(8,128)S(1)}, u32[]{:S(2)}, u32[]{:S(2)}) collective-permute-start(f32[32,256]{1,0:T(8,128)S(1)} %get-tuple-element.7.low), channel_id=1, source_target_pairs={{1,0},{2,1},{3,2},{4,3},{5,4},{6,5},{7,6},{8,7},{9,8},{10,9},{11,1... | collective-permute-start | bytes 98312 | tf_op jit(solution)/shard_map/ppermute | solution.py:238
  11.5 0.6 %reduce_sum.9 = f32[]{:T(128)} reduce(f32[16]{0:T(128)S(1)} %copy-done.17, f32[]{:T(128)} %constant.13.clone.1), dimensions={0}, to_apply=%region_0.0 | reduce | flops 15 | bytes 72 | tf_op jit(solution)/shard_map/reduce_sum | solution.py:239
  12.1 0.7 %divide_sqrt_fusion = f32[16]{0:T(128)S(1)} fusion(f32[16]{0:T(128)S(1)} %copy-done.17, f32[]{:T(128)} %reduce_sum.9), kind=kLoop, calls=%fused_computation.1 | loop fusion | flops 16 | bytes 132 | tf_op jit(solution)/shard_map/sqrt | solution.py:239
  12.7 0.0 copy-start.9
  12.8 1.2 %broadcast_multiply_fusion.spectra = f32[2,16,32,128]{3,2,1,0:T(8,128)S(1)} fusion(f32[2,16,32,128]{3,2,1,0:T(8,128)} %param.19, f32[16]{0:T(128)S(1)} %divide_sqrt_fusion), kind=kLoop, calls=%fused_computation | loop fusion | flops 131072 | bytes 1048640 | tf_op jit(solution)/shard_map/mul | solution.py:240
  14.0 0.0 copy-start.1
  14.0 0.0 copy-start.3
  14.0 0.0 copy-start.5
  14.0 3.5 %collective-permute-done.before = f32[32,256]{1,0:T(8,128)S(1)} collective-permute-done((f32[32,256]{1,0:T(8,128)S(1)}, f32[32,256]{1,0:T(8,128)S(1)}, u32[]{:S(2)}, u32[]{:S(2)}) %collective-permute-start) | collective-permute-done | bytes 32800 | tf_op jit(solution)/shard_map/ppermute | solution.py:237
  17.6 6.0 %shard_map.177 = (f32[128,1024]{1,0:T(8,128)}, f32[32,256]{1,0:T(8,128)S(1)}) custom-call(f32[32,256]{1,0:T(8,128)S(1)} %get-tuple-element.7.low, f32[32,256]{1,0:T(8,128)S(1)} %get-tuple-element.8.high, f32[32,256]{1,0:T(8,128)S(1)} %collective-permute-done.before, f32[32,256]{1,0:T(8,128)S(1)} %collective-permute-done.1.after, ...), custom_call_target="tpu_custom_call" | custom-call | flops 1610612736 | bytes 3457024 | tf_op jit(solution)/shard_map/pallas_call | solution.py:208
  23.6 1.0 %collective-permute-start.3 = (f32[32,256]{1,0:T(8,128)S(1)}, f32[32,256]{1,0:T(8,128)S(1)}, u32[]{:S(2)}, u32[]{:S(2)}) collective-permute-start(f32[32,256]{1,0:T(8,128)S(1)} %get-tuple-element.10.own), channel_id=1, source_target_pairs={{1,0},{2,1},{3,2},{4,3},{5,4},{6,5},{7,6},{8,7},{9,8},{10,9},{11,1... | collective-permute-start | bytes 98312 | tf_op jit(solution)/shard_map/ppermute | solution.py:254
  24.6 1.6 %collective-permute-done.3.after = f32[32,256]{1,0:T(8,128)S(1)} collective-permute-done((f32[32,256]{1,0:T(8,128)S(1)}, f32[32,256]{1,0:T(8,128)S(1)}, u32[]{:S(2)}, u32[]{:S(2)}) %collective-permute-start.3) | collective-permute-done | bytes 32800 | tf_op jit(solution)/shard_map/ppermute | solution.py:254
  26.2 4.4 %collective-permute-done.2.before = f32[32,256]{1,0:T(8,128)S(1)} collective-permute-done((f32[32,256]{1,0:T(8,128)S(1)}, f32[32,256]{1,0:T(8,128)S(1)}, u32[]{:S(2)}, u32[]{:S(2)}) %collective-permute-start.2) | collective-permute-done | bytes 32800 | tf_op jit(solution)/shard_map/ppermute | solution.py:253
  30.7 1.5 %shard_map.178 = f32[128,1024]{1,0:T(8,128)} custom-call(f32[32,256]{1,0:T(8,128)S(1)} %get-tuple-element.10.own, f32[32,256]{1,0:T(8,128)S(1)} %collective-permute-done.2.before, f32[32,256]{1,0:T(8,128)S(1)} %collective-permute-done.3.after, f32[128,1024]{1,0:T(8,128)S(1)} %get-tuple-element.11.slope, bf16[128,192]{1,0:T(8,128)(2,1)S(1)} %copy-done.5, ...), custom_call_target="tpu_custom_call" | custom-call | flops 201326592 | bytes 2244608 | tf_op jit(solution)/shard_map/pallas_call | solution.py:208
  (26 shorter events, 0.1 us)
Async XLA Ops:
  0.6 1.0 %copy-start = (bf16[1024,256]{1,0:T(8,128)(2,1)S(1)}, bf16[1024,256]{1,0:T(8,128)(2,1)}, u32[]{:S(2)}) copy-start(bf16[1024,256]{1,0:T(8,128)(2,1)} %constant.34.clone.fwd_l) | copy-start | bytes 1572868
  1.7 1.0 %copy-start.2 = (bf16[1024,256]{1,0:T(8,128)(2,1)S(1)}, bf16[1024,256]{1,0:T(8,128)(2,1)}, u32[]{:S(2)}) copy-start(bf16[1024,256]{1,0:T(8,128)(2,1)} %constant.33.clone.fwd_h) | copy-start | bytes 1572868
  2.7 1.0 %copy-start.4 = (f32[128,1024]{1,0:T(8,128)S(1)}, f32[128,1024]{1,0:T(8,128)}, u32[]{:S(2)}) copy-start(f32[128,1024]{1,0:T(8,128)} %mask.1) | copy-start | bytes 1572868
  3.8 0.8 %copy-start.6 = (bf16[64,256]{1,0:T(8,128)(2,1)S(1)}, bf16[64,256]{1,0:T(8,128)(2,1)}, u32[]{:S(2)}) copy-start(bf16[64,256]{1,0:T(8,128)(2,1)} %constant.36.clone.proj_l) | copy-start | bytes 98308
  4.5 0.8 %copy-start.7 = (bf16[64,256]{1,0:T(8,128)(2,1)S(1)}, bf16[64,256]{1,0:T(8,128)(2,1)}, u32[]{:S(2)}) copy-start(bf16[64,256]{1,0:T(8,128)(2,1)} %constant.35.clone.proj_h) | copy-start | bytes 98308
  5.3 12.2 %copy-start.10 = (bf16[256,1024]{1,0:T(8,128)(2,1)S(1)}, bf16[256,1024]{1,0:T(8,128)(2,1)}, u32[]{:S(2)}) copy-start(bf16[256,1024]{1,0:T(8,128)(2,1)} %constant.37.clone.wide_h) | copy-start | bytes 1572868
  5.3 12.2 %copy-start.11 = (bf16[256,512]{1,0:T(8,128)(2,1)S(1)}, bf16[256,512]{1,0:T(8,128)(2,1)}, u32[]{:S(2)}) copy-start(bf16[256,512]{1,0:T(8,128)(2,1)} %constant.30.clone.cols_l) | copy-start | bytes 786436
  5.3 12.2 %copy-start.12 = (bf16[256,512]{1,0:T(8,128)(2,1)S(1)}, bf16[256,512]{1,0:T(8,128)(2,1)}, u32[]{:S(2)}) copy-start(bf16[256,512]{1,0:T(8,128)(2,1)} %constant.29.clone.cols_h) | copy-start | bytes 786436
  5.3 12.2 %copy-start.13 = (bf16[128,192]{1,0:T(8,128)(2,1)S(1)}, bf16[128,192]{1,0:T(8,128)(2,1)}, u32[]{:S(2)}) copy-start(bf16[128,192]{1,0:T(8,128)(2,1)} %constant.39.clone.wide_r) | copy-start | bytes 147460
  5.3 12.2 %copy-start.14 = (bf16[64,384]{1,0:T(8,128)(2,1)S(1)}, bf16[64,384]{1,0:T(8,128)(2,1)}, u32[]{:S(2)}) copy-start(bf16[64,384]{1,0:T(8,128)(2,1)} %constant.40.clone.wide_rt) | copy-start | bytes 147460
  5.3 12.2 %copy-start.15 = (bf16[64,192]{1,0:T(8,128)(2,1)S(1)}, bf16[64,192]{1,0:T(8,128)(2,1)}, u32[]{:S(2)}) copy-start(bf16[64,192]{1,0:T(8,128)(2,1)} %constant.32.clone.rows_t) | copy-start | bytes 73732
  5.3 12.2 %copy-start.16 = (bf16[64,192]{1,0:T(8,128)(2,1)S(1)}, bf16[64,192]{1,0:T(8,128)(2,1)}, u32[]{:S(2)}) copy-start(bf16[64,192]{1,0:T(8,128)(2,1)} %constant.31.clone.rows_f) | copy-start | bytes 73732
  5.9 5.5 %copy-start.17 = (f32[16]{0:T(128)S(1)}, f32[16]{0:T(128)}, u32[]{:S(2)}) copy-start(f32[16]{0:T(128)} %param.20) | copy-start | bytes 196
  5.9 8.1 %collective-permute-start.1 = (f32[32,256]{1,0:T(8,128)S(1)}, f32[32,256]{1,0:T(8,128)S(1)}, u32[]{:S(2)}, u32[]{:S(2)}) collective-permute-start(f32[32,256]{1,0:T(8,128)S(1)} %get-tuple-element.7.low), channel_id=1, source_target_pairs={{1,0},{2,1},{3,2},{4,3},{5,4},{6,5},{7,6},{8,7},{9,8},{10,9},{11,1... | collective-permute-start | bytes 98312 | tf_op jit(solution)/shard_map/ppermute | solution.py:238
  11.5 6.0 %collective-permute-start = (f32[32,256]{1,0:T(8,128)S(1)}, f32[32,256]{1,0:T(8,128)S(1)}, u32[]{:S(2)}, u32[]{:S(2)}) collective-permute-start(f32[32,256]{1,0:T(8,128)S(1)} %get-tuple-element.8.high), channel_id=1, source_target_pairs={{0,1},{1,2},{2,3},{3,4},{4,5},{5,6},{6,7},{7,8},{8,9},{9,10},{10,1... | collective-permute-start | bytes 98312 | tf_op jit(solution)/shard_map/ppermute | solution.py:237
  12.7 4.8 %copy-start.8 = (s32[128,1024]{1,0:T(8,128)S(1)}, s32[128,1024]{1,0:T(8,128)}, u32[]{:S(2)}) copy-start(s32[128,1024]{1,0:T(8,128)} %target.1) | copy-start | bytes 1572868
  12.7 4.8 %copy-start.9 = (bf16[256,1024]{1,0:T(8,128)(2,1)S(1)}, bf16[256,1024]{1,0:T(8,128)(2,1)}, u32[]{:S(2)}) copy-start(bf16[256,1024]{1,0:T(8,128)(2,1)} %constant.38.clone.wide_l) | copy-start | bytes 1572868
  14.0 16.7 %copy-start.1 = (bf16[1024,256]{1,0:T(8,128)(2,1)S(1)}, bf16[1024,256]{1,0:T(8,128)(2,1)}, u32[]{:S(2)}) copy-start(bf16[1024,256]{1,0:T(8,128)(2,1)} %constant.34.clone.fwd_l) | copy-start | bytes 1572868
  14.0 16.7 %copy-start.3 = (bf16[1024,256]{1,0:T(8,128)(2,1)S(1)}, bf16[1024,256]{1,0:T(8,128)(2,1)}, u32[]{:S(2)}) copy-start(bf16[1024,256]{1,0:T(8,128)(2,1)} %constant.33.clone.fwd_h) | copy-start | bytes 1572868
  14.0 16.7 %copy-start.5 = (bf16[128,192]{1,0:T(8,128)(2,1)S(1)}, bf16[128,192]{1,0:T(8,128)(2,1)}, u32[]{:S(2)}) copy-start(bf16[128,192]{1,0:T(8,128)(2,1)} %constant.28.clone.rows_b) | copy-start | bytes 147460
  23.6 2.6 %collective-permute-start.3 = (f32[32,256]{1,0:T(8,128)S(1)}, f32[32,256]{1,0:T(8,128)S(1)}, u32[]{:S(2)}, u32[]{:S(2)}) collective-permute-start(f32[32,256]{1,0:T(8,128)S(1)} %get-tuple-element.10.own), channel_id=1, source_target_pairs={{1,0},{2,1},{3,2},{4,3},{5,4},{6,5},{7,6},{8,7},{9,8},{10,9},{11,1... | collective-permute-start | bytes 98312 | tf_op jit(solution)/shard_map/ppermute | solution.py:254
  24.6 6.0 %collective-permute-start.2 = (f32[32,256]{1,0:T(8,128)S(1)}, f32[32,256]{1,0:T(8,128)S(1)}, u32[]{:S(2)}, u32[]{:S(2)}) collective-permute-start(f32[32,256]{1,0:T(8,128)S(1)} %get-tuple-element.10.own), channel_id=1, source_target_pairs={{0,1},{1,2},{2,3},{3,4},{4,5},{5,6},{6,7},{7,8},{8,9},{9,10},{10,1... | collective-permute-start | bytes 98312 | tf_op jit(solution)/shard_map/ppermute | solution.py:253

commit v2 on v1

--- a/solution.py
+++ b/solution.py
@@ -1,4 +1,3 @@
-import functools
 import math
 
 import jax
@@ -16,6 +15,7 @@
 
 BF16 = jnp.bfloat16
 F32 = jnp.float32
+CHUNKS = 4
 
 
 def split_table(table):
@@ -129,24 +129,65 @@
     return jnp.where(row % 2 == 0, 1.0, -1.0).astype(F32)
 
 
-def project_kernel(mask, fwd_h, fwd_l, proj_h, proj_l, low_out, high_out, slope_out):
-    transmit = jnp.tanh(mask[...])
-    slope_out[...] = 1.0 - transmit * transmit
-    spectra = dot3(split(transmit), (fwd_h[...], fwd_l[...]))
+def is_odd():
+    return lax.axis_index("tiles") % 2 == 1
+
+
+def column_chunks(ref, chunks):
+    width = ref.shape[1] // chunks
+    return [pl.ds(i * width, width) for i in range(chunks)]
+
+
+def project_kernel(
+    mask_hbm, fwd_h_hbm, fwd_l_hbm, proj_h_hbm, proj_l_hbm, far_out, near_out, sum_out, slope_out,
+    mask, fwd_h, fwd_l, proj_h, proj_l, sems
+):
+    chunks = column_chunks(mask, CHUNKS)
+    copies = []
+    for i, cols in enumerate(chunks):
+        copies.append([
+            pltpu.make_async_copy(mask_hbm.at[:, cols], mask.at[:, cols], sems.at[0, i]),
+            pltpu.make_async_copy(fwd_h_hbm.at[cols, :], fwd_h.at[cols, :], sems.at[1, i]),
+            pltpu.make_async_copy(fwd_l_hbm.at[cols, :], fwd_l.at[cols, :], sems.at[2, i]),
+        ])
+    last = [
+        pltpu.make_async_copy(proj_h_hbm, proj_h, sems.at[3, 0]),
+        pltpu.make_async_copy(proj_l_hbm, proj_l, sems.at[3, 1]),
+    ]
+    for group in copies:
+        for copy in group:
+            copy.start()
+    for copy in last:
+        copy.start()
+    spectra = None
+    for group, cols in zip(copies, chunks):
+        group[0].wait()
+        transmit = jnp.tanh(mask[:, cols])
+        slope_out[:, cols] = 1.0 - transmit * transmit
+        pieces = split(transmit)
+        group[1].wait()
+        group[2].wait()
+        term = dot3(pieces, (fwd_h[cols, :], fwd_l[cols, :]))
+        spectra = term if spectra is None else spectra + term
+    for copy in last:
+        copy.wait()
     parts = dot3((proj_h[...], proj_l[...]), split(turn(spectra, -1)))
-    freq_rows = low_out.shape[0]
-    low_out[...] = parts[:freq_rows]
-    high_out[...] = parts[freq_rows:]
+    freq_rows = far_out.shape[0]
+    low, high = parts[:freq_rows], parts[freq_rows:]
+    odd = is_odd()
+    far_out[...] = jnp.where(odd, high, low)
+    near_out[...] = jnp.where(odd, low, high)
+    sum_out[...] = low + high
 
 
 def image_kernel(
-    low, high, before, after, spectra, target, rows_f, rows_t, cols_h, cols_l,
-    wide_r, wide_rt, wide_h, wide_l, resist_out, grad_out, fields
+    own, far, near, spectra, target, rows_f, rows_t, cols_h, cols_l,
+    wide_r, wide_rt, wide_h, wide_l, resist_hbm, grad_out, fields, resist_out, sem
 ):
     kernels, freq_rows, freq_cols = spectra.shape[1:]
     rows_c, cols_c = rows_f.shape[0], 2 * freq_cols
-    sign = alternate(low.shape)
-    window = low[...] + high[...] + sign * (before[...] + after[...])
+    sign = alternate(own.shape)
+    window = own[...] + sign * (far[...] + near[...])
     win_re, win_im = window[:, :freq_cols], window[:, freq_cols:]
     group = 4
     total = jnp.zeros((rows_c, cols_c), F32)
@@ -168,6 +209,8 @@
     intensity = dot3(split(tall), (wide_h[...], wide_l[...]))
     resist = jax.nn.sigmoid(STEEPNESS * (intensity - THRESHOLD))
     resist_out[...] = resist
+    sent = pltpu.make_async_copy(resist_out, resist_hbm, sem)
+    sent.start()
     slopes = (4.0 * STEEPNESS) * (resist - target[...].astype(F32)) * resist * (1.0 - resist)
     narrow = dot3_t(split(slopes), (wide_h[...], wide_l[...]))
     weight = dot(wide_rt[...], stack_right(narrow))
@@ -189,27 +232,41 @@
             grad_re = grad_re + real * kern_re + imag * kern_im
             grad_im = grad_im + imag * kern_re - real * kern_im
     grad_out[...] = jnp.concatenate([grad_re, grad_im], axis=1)
-
-
-def gradient_kernel(own, before, after, slope, rows_b, fwd_h, fwd_l, out):
+    sent.wait()
+
+
+def gradient_kernel(own, far, near, slope, rows_b, fwd_h, fwd_l, out_hbm, out, sems):
     half = out.shape[0] // 2
     sign = alternate(own.shape)
-    low = stack_right(turn(own[...] + sign * before[...], 1))
-    high = stack_right(turn(own[...] + sign * after[...], 1))
+    odd = is_odd()
+    before = jnp.where(odd, near[...], far[...])
+    after = jnp.where(odd, far[...], near[...])
+    low = stack_right(turn(own[...] + sign * before, 1))
+    high = stack_right(turn(own[...] + sign * after, 1))
     merged = jnp.concatenate([dot(rows_b[:half], low), dot(rows_b[half:], high)], axis=0)
-    out[...] = slope[...] * dot3_t(split(merged), (fwd_h[...], fwd_l[...]))
-
-
-def call(kernel, outs, args, flops, scratch=(), limit=32 << 20):
-    vmem = pl.BlockSpec(memory_space=pltpu.VMEM)
+    merged = split(merged)
+    sent = []
+    for i, cols in enumerate(column_chunks(out, CHUNKS)):
+        out[:, cols] = slope[:, cols] * dot3_t(merged, (fwd_h[cols, :], fwd_l[cols, :]))
+        sent.append(pltpu.make_async_copy(out.at[:, cols], out_hbm.at[:, cols], sems.at[i]))
+        sent[-1].start()
+    for copy in sent:
+        copy.wait()
+
+
+VMEM = pl.BlockSpec(memory_space=pltpu.VMEM)
+HBM = pl.BlockSpec(memory_space=pltpu.HBM)
+
+
+def call(kernel, outs, args, flops, scratch, out_specs, in_specs=None, limit=32 << 20):
     shapes = [jax.ShapeDtypeStruct(shape, F32) for shape in outs]
     moved = sum(math.prod(a.shape) * a.dtype.itemsize for a in args)
     moved += sum(4 * math.prod(shape) for shape in outs)
     return pl.pallas_call(
         kernel,
         out_shape=shapes,
-        in_specs=[vmem] * len(args),
-        out_specs=[vmem] * len(outs),
+        in_specs=in_specs or [VMEM] * len(args),
+        out_specs=out_specs,
         scratch_shapes=scratch,
         compiler_params=pltpu.CompilerParams(vmem_limit_bytes=limit),
         cost_estimate=pl.CostEstimate(flops=flops, bytes_accessed=moved, transcendentals=0),
@@ -219,23 +276,29 @@
 def shards(mask_params, target, kernel_spectra, kernel_weights):
     strip_rows, columns = mask_params.shape
     kernels, freq_rows, freq_cols = kernel_spectra.shape[1:]
-    assert 2 * MARGIN == strip_rows
     tables = jax.tree.map(
         jnp.asarray, make_tables(strip_rows, MARGIN, columns, freq_rows, freq_cols)
     )
     count = lax.axis_size("tiles")
-    forward = [(i, (i + 1) % count) for i in range(count)]
-    backward = [(j, i) for i, j in forward]
+    assert 2 * MARGIN == strip_rows and count % 2 == 0
+    near_pairs = [(i, i ^ 1) for i in range(count)]
+    far_pairs = [(i, (i + 1 if i % 2 else i - 1) % count) for i in range(count)]
     pair = (freq_rows, 2 * freq_cols)
     area = strip_rows * columns
-    low, high, slope = call(
+    args = [mask_params, *tables["forward"], *tables["project"]]
+    args = [pltpu.with_memory_space_constraint(a, pltpu.HBM) for a in args]
+    send_far, send_near, own, slope = call(
         project_kernel,
-        [pair, pair, (strip_rows, columns)],
-        [mask_params, *tables["forward"], *tables["project"]],
+        [pair, pair, pair, (strip_rows, columns)],
+        args,
         flops=6 * area * 2 * freq_cols,
-    )
-    before = lax.ppermute(high, "tiles", forward)
-    after = lax.ppermute(low, "tiles", backward)
+        scratch=[pltpu.VMEM(a.shape, a.dtype) for a in args]
+        + [pltpu.SemaphoreType.DMA((4, CHUNKS))],
+        in_specs=[HBM] * len(args),
+        out_specs=[VMEM] * 4,
+    )
+    far = lax.ppermute(send_far, "tiles", far_pairs)
+    near = lax.ppermute(send_near, "tiles", near_pairs)
     shares = jnp.sqrt(kernel_weights / jnp.sum(kernel_weights))
     spectra = kernel_spectra * shares[None, :, None, None]
     rows_c, cols_c = 2 * freq_rows, 2 * freq_cols
@@ -243,20 +306,27 @@
         image_kernel,
         [(strip_rows, columns), pair],
         [
-            low, high, before, after, spectra, target,
+            own, far, near, spectra, target,
             tables["field_rows"], tables["field_rows_t"], *tables["field_cols"],
             tables["widen_rows"], tables["widen_rows_t"], *tables["widen_cols"],
         ],
         flops=24 * kernels * rows_c * cols_c * cols_c,
-        scratch=[pltpu.VMEM((kernels * rows_c, 2 * cols_c), F32)],
-    )
-    grad_before = lax.ppermute(grad, "tiles", forward)
-    grad_after = lax.ppermute(grad, "tiles", backward)
+        scratch=[
+            pltpu.VMEM((kernels * rows_c, 2 * cols_c), F32),
+            pltpu.VMEM((strip_rows, columns), F32),
+            pltpu.SemaphoreType.DMA,
+        ],
+        out_specs=[HBM, VMEM],
+    )
+    grad_far = lax.ppermute(grad, "tiles", far_pairs)
+    grad_near = lax.ppermute(grad, "tiles", near_pairs)
     (gradient,) = call(
         gradient_kernel,
         [(strip_rows, columns)],
-        [grad, grad_before, grad_after, slope, tables["back_rows"], *tables["forward"]],
+        [grad, grad_far, grad_near, slope, tables["back_rows"], *tables["forward"]],
         flops=6 * area * 2 * freq_cols,
+        scratch=[pltpu.VMEM((strip_rows, columns), F32), pltpu.SemaphoreType.DMA((CHUNKS,))],
+        out_specs=[HBM],
     )
     return (resist, gradient)
 

time: 32.6 us -> 25.5 us (0.78)
  waiting for transfers between devices: 9.5 us -> 2.99 us
  local copies, waits for them, and re-layouts: 4.71 us -> 0.09 us
  starting transfers between devices: 6.54 us -> 9.16 us
  Pallas kernels: 8.15 us -> 9.73 us
    ppermute x4, waiting for transfers between devices: 9.5 us -> 2.99 us  [the longest x1 2.99 us: shards(): grad_far = lax.ppermute(grad, 'tiles', far_pairs)]
    unnamed x36 -> x26, local copies, waits for them, and re-layouts: 4.71 us -> 0.09 us
    ppermute x4, starting transfers between devices: 6.54 us -> 9.16 us  [the longest x1 5.54 us: shards(): far = lax.ppermute(send_far, 'tiles', far_pairs)]
    pallas_call x3, Pallas kernels: 8.15 us -> 9.73 us  [call(): pl.pallas_call(kernel, out_shape=shapes, in_specs=in_specs or [VMEM] * le...]
  transfers between devices with their start and end apart: 4 -> 4, of which waited for: 3 -> 1; matrix products, arithmetic and copies ran while one was open for 8% -> 10% of each run, Pallas kernels for 0% -> 0%
where the time goes in v2:
time: 25.5 us; the launch traced here: 25.3 us
  Pallas kernels  9.73 us (38%)
  starting transfers between devices  9.16 us (36%)
  waiting for transfers between devices  2.99 us (12%)
  other arithmetic  2.48 us (10%)
  between operations  0.86 us (3%)
    pallas_call x3, Pallas kernels, call(): pl.pallas_call(kernel, out_shape=shapes, in_specs=in_specs or [VMEM] * le...  9.73 us
    ppermute x1, starting transfers between devices, shards(): far = lax.ppermute(send_far, 'tiles', far_pairs)  5.54 us
    ppermute x1, starting transfers between devices, shards(): grad_far = lax.ppermute(grad, 'tiles', far_pairs)  3.05 us
    ppermute x1, waiting for transfers between devices, shards(): grad_far = lax.ppermute(grad, 'tiles', far_pairs)  2.99 us
    mul x1, other arithmetic, shards(): spectra = kernel_spectra * shares[None, :, None, None]  1.23 us
    sqrt x1, other arithmetic, shards(): shares = jnp.sqrt(kernel_weights / jnp.sum(kernel_weights))  0.65 us
    reduce_sum x1, other arithmetic, shards(): shares = jnp.sqrt(kernel_weights / jnp.sum(kernel_weights))  0.6 us
    ppermute x1, starting transfers between devices, shards(): grad_near = lax.ppermute(grad, 'tiles', near_pairs)  0.58 us
  transfers between devices with their start and end apart: 4, of which 1 were waited for; matrix products, arithmetic and copies ran while one was open for 10% of the time, Pallas kernels for 0%

profile of v2, /device:TPU:0, one launch (start us, length us, event | category | flops | bytes accessed | tf_op | source)
XLA Modules:
  0.0 25.3 jit_solution(3080458652619638380)
XLA Ops:
  0.6 0.0 copy-start.5
  0.6 0.0 copy-start.6
  0.7 0.0 copy-start.7
  0.7 0.0 copy-start.8
  0.7 0.0 copy-start.9
  0.7 0.0 copy-start.10
  0.7 0.0 copy-start.11
  0.7 2.4 %shard_map.176 = (f32[32,256]{1,0:T(8,128)S(1)}, f32[32,256]{1,0:T(8,128)S(1)}, f32[32,256]{1,0:T(8,128)S(1)}, f32[128,1024]{1,0:T(8,128)S(1)}) custom-call(f32[128,1024]{1,0:T(8,128)} %mask_hbm.1, bf16[1024,256]{1,0:T(8,128)(2,1)} %constant.33.clone.fwd_h_hbm.fwd_h, bf16[1024,256]{1,0:T(8,128)(2,1)} %constant.34.clone.fwd_l_hbm.fwd_l, ...), custom_call_target="tpu_custom_call" | custom-call | flops 201326592 | bytes 2260992 | tf_op jit(solution)/shard_map/pallas_call | solution.py:265
  3.1 0.0 copy-start.12
  3.1 5.5 %collective-permute-start = (f32[32,256]{1,0:T(8,128)S(1)}, f32[32,256]{1,0:T(8,128)S(1)}, u32[]{:S(2)}, u32[]{:S(2)}) collective-permute-start(f32[32,256]{1,0:T(8,128)S(1)} %get-tuple-element.9), channel_id=1, source_target_pairs={{0,15},{1,2},{2,1},{3,4},{4,3},{5,6},{6,5},{7,8},{8,7},{9,10},{10,... | collective-permute-start | bytes 98312 | tf_op jit(solution)/shard_map/ppermute | solution.py:300
  8.6 0.0 collective-permute-start.1
  8.6 0.6 %reduce_sum.9 = f32[]{:T(128)} reduce(f32[16]{0:T(128)S(1)} %copy-done.12, f32[]{:T(128)} %constant.13.clone.1), dimensions={0}, to_apply=%region_0.0 | reduce | flops 15 | bytes 72 | tf_op jit(solution)/shard_map/reduce_sum | solution.py:302
  9.2 0.7 %divide_sqrt_fusion = f32[16]{0:T(128)S(1)} fusion(f32[16]{0:T(128)S(1)} %copy-done.12, f32[]{:T(128)} %reduce_sum.9), kind=kLoop, calls=%fused_computation.1 | loop fusion | flops 16 | bytes 132 | tf_op jit(solution)/shard_map/sqrt | solution.py:302
  9.9 0.0 copy-start.3
  9.9 0.0 copy-start.4
  9.9 1.2 %broadcast_multiply_fusion.spectra = f32[2,16,32,128]{3,2,1,0:T(8,128)S(1)} fusion(f32[2,16,32,128]{3,2,1,0:T(8,128)} %param.19, f32[16]{0:T(128)S(1)} %divide_sqrt_fusion), kind=kLoop, calls=%fused_computation | loop fusion | flops 131072 | bytes 1048640 | tf_op jit(solution)/shard_map/mul | solution.py:303
  11.3 0.0 copy-start
  11.3 0.0 copy-start.1
  11.3 0.0 copy-start.2
  11.3 5.9 %shard_map.177 = (f32[128,1024]{1,0:T(8,128)}, f32[32,256]{1,0:T(8,128)S(1)}) custom-call(f32[32,256]{1,0:T(8,128)S(1)} %get-tuple-element.8.own, f32[32,256]{1,0:T(8,128)S(1)} %collective-permute-done.far, f32[32,256]{1,0:T(8,128)S(1)} %collective-permute-done.1.near, f32[2,16,32,128]{3,2,1,0:T(8,128)S(1)} %broadcast_multiply_fusion.spectra, ...), custom_call_target="tpu_custom_call" | custom-call | flops 1610612736 | bytes 3424256 | tf_op jit(solution)/shard_map/pallas_call | solution.py:265
  17.2 0.6 %collective-permute-start.3 = (f32[32,256]{1,0:T(8,128)S(1)}, f32[32,256]{1,0:T(8,128)S(1)}, u32[]{:S(2)}, u32[]{:S(2)}) collective-permute-start(f32[32,256]{1,0:T(8,128)S(1)} %get-tuple-element.12.own), channel_id=1, source_target_pairs={{0,1},{1,0},{2,3},{3,2},{4,5},{5,4},{6,7},{7,6},{8,9},{9,8},{10,11... | collective-permute-start | bytes 98312 | tf_op jit(solution)/shard_map/ppermute | solution.py:322
  17.8 3.0 %collective-permute-start.2 = (f32[32,256]{1,0:T(8,128)S(1)}, f32[32,256]{1,0:T(8,128)S(1)}, u32[]{:S(2)}, u32[]{:S(2)}) collective-permute-start(f32[32,256]{1,0:T(8,128)S(1)} %get-tuple-element.12.own), channel_id=1, source_target_pairs={{0,15},{1,2},{2,1},{3,4},{4,3},{5,6},{6,5},{7,8},{8,7},{9,10},{10,... | collective-permute-start | bytes 98312 | tf_op jit(solution)/shard_map/ppermute | solution.py:321
  20.8 3.0 %collective-permute-done.2.far = f32[32,256]{1,0:T(8,128)S(1)} collective-permute-done((f32[32,256]{1,0:T(8,128)S(1)}, f32[32,256]{1,0:T(8,128)S(1)}, u32[]{:S(2)}, u32[]{:S(2)}) %collective-permute-start.2) | collective-permute-done | bytes 32800 | tf_op jit(solution)/shard_map/ppermute | solution.py:321
  23.8 1.5 %shard_map.178 = f32[128,1024]{1,0:T(8,128)} custom-call(f32[32,256]{1,0:T(8,128)S(1)} %get-tuple-element.12.own, f32[32,256]{1,0:T(8,128)S(1)} %collective-permute-done.2.far, f32[32,256]{1,0:T(8,128)S(1)} %collective-permute-done.3.near, f32[128,1024]{1,0:T(8,128)S(1)} %get-tuple-element.13.slope, bf16[128,192]{1,0:T(8,128)(2,1)S(1)} %copy-done.2, ...), custom_call_target="tpu_custom_call" | custom-call | flops 201326592 | bytes 2244608 | tf_op jit(solution)/shard_map/pallas_call | solution.py:265
  (16 shorter events, 0.0 us)
Async XLA Ops:
  0.6 10.6 %copy-start.5 = (bf16[256,1024]{1,0:T(8,128)(2,1)S(1)}, bf16[256,1024]{1,0:T(8,128)(2,1)}, u32[]{:S(2)}) copy-start(bf16[256,1024]{1,0:T(8,128)(2,1)} %constant.37.clone.wide_h) | copy-start | bytes 1572868
  0.6 10.6 %copy-start.6 = (bf16[256,512]{1,0:T(8,128)(2,1)S(1)}, bf16[256,512]{1,0:T(8,128)(2,1)}, u32[]{:S(2)}) copy-start(bf16[256,512]{1,0:T(8,128)(2,1)} %constant.30.clone.cols_l) | copy-start | bytes 786436
  0.7 10.6 %copy-start.7 = (bf16[256,512]{1,0:T(8,128)(2,1)S(1)}, bf16[256,512]{1,0:T(8,128)(2,1)}, u32[]{:S(2)}) copy-start(bf16[256,512]{1,0:T(8,128)(2,1)} %constant.29.clone.cols_h) | copy-start | bytes 786436
  0.7 10.6 %copy-start.8 = (bf16[128,192]{1,0:T(8,128)(2,1)S(1)}, bf16[128,192]{1,0:T(8,128)(2,1)}, u32[]{:S(2)}) copy-start(bf16[128,192]{1,0:T(8,128)(2,1)} %constant.39.clone.wide_r) | copy-start | bytes 147460
  0.7 10.6 %copy-start.9 = (bf16[64,384]{1,0:T(8,128)(2,1)S(1)}, bf16[64,384]{1,0:T(8,128)(2,1)}, u32[]{:S(2)}) copy-start(bf16[64,384]{1,0:T(8,128)(2,1)} %constant.40.clone.wide_rt) | copy-start | bytes 147460
  0.7 10.5 %copy-start.10 = (bf16[64,192]{1,0:T(8,128)(2,1)S(1)}, bf16[64,192]{1,0:T(8,128)(2,1)}, u32[]{:S(2)}) copy-start(bf16[64,192]{1,0:T(8,128)(2,1)} %constant.32.clone.rows_t) | copy-start | bytes 73732
  0.7 10.5 %copy-start.11 = (bf16[64,192]{1,0:T(8,128)(2,1)S(1)}, bf16[64,192]{1,0:T(8,128)(2,1)}, u32[]{:S(2)}) copy-start(bf16[64,192]{1,0:T(8,128)(2,1)} %constant.31.clone.rows_f) | copy-start | bytes 73732
  3.1 5.6 %copy-start.12 = (f32[16]{0:T(128)S(1)}, f32[16]{0:T(128)}, u32[]{:S(2)}) copy-start(f32[16]{0:T(128)} %param.20) | copy-start | bytes 196
  3.1 8.1 %collective-permute-start = (f32[32,256]{1,0:T(8,128)S(1)}, f32[32,256]{1,0:T(8,128)S(1)}, u32[]{:S(2)}, u32[]{:S(2)}) collective-permute-start(f32[32,256]{1,0:T(8,128)S(1)} %get-tuple-element.9), channel_id=1, source_target_pairs={{0,15},{1,2},{2,1},{3,4},{4,3},{5,6},{6,5},{7,8},{8,7},{9,10},{10,... | collective-permute-start | bytes 98312 | tf_op jit(solution)/shard_map/ppermute | solution.py:300
  8.6 2.5 %collective-permute-start.1 = (f32[32,256]{1,0:T(8,128)S(1)}, f32[32,256]{1,0:T(8,128)S(1)}, u32[]{:S(2)}, u32[]{:S(2)}) collective-permute-start(f32[32,256]{1,0:T(8,128)S(1)} %get-tuple-element.10), channel_id=1, source_target_pairs={{0,1},{1,0},{2,3},{3,2},{4,5},{5,4},{6,7},{7,6},{8,9},{9,8},{10,11... | collective-permute-start | bytes 98312 | tf_op jit(solution)/shard_map/ppermute | solution.py:301
  9.9 1.4 %copy-start.3 = (s32[128,1024]{1,0:T(8,128)S(1)}, s32[128,1024]{1,0:T(8,128)}, u32[]{:S(2)}) copy-start(s32[128,1024]{1,0:T(8,128)} %target.1) | copy-start | bytes 1572868
  9.9 1.4 %copy-start.4 = (bf16[256,1024]{1,0:T(8,128)(2,1)S(1)}, bf16[256,1024]{1,0:T(8,128)(2,1)}, u32[]{:S(2)}) copy-start(bf16[256,1024]{1,0:T(8,128)(2,1)} %constant.38.clone.wide_l) | copy-start | bytes 1572868
  11.3 12.6 %copy-start = (bf16[1024,256]{1,0:T(8,128)(2,1)S(1)}, bf16[1024,256]{1,0:T(8,128)(2,1)}, u32[]{:S(2)}) copy-start(bf16[1024,256]{1,0:T(8,128)(2,1)} %constant.34.clone.fwd_l_hbm.fwd_l) | copy-start | bytes 1572868
  11.3 12.5 %copy-start.1 = (bf16[1024,256]{1,0:T(8,128)(2,1)S(1)}, bf16[1024,256]{1,0:T(8,128)(2,1)}, u32[]{:S(2)}) copy-start(bf16[1024,256]{1,0:T(8,128)(2,1)} %constant.33.clone.fwd_h_hbm.fwd_h) | copy-start | bytes 1572868
  11.3 12.5 %copy-start.2 = (bf16[128,192]{1,0:T(8,128)(2,1)S(1)}, bf16[128,192]{1,0:T(8,128)(2,1)}, u32[]{:S(2)}) copy-start(bf16[128,192]{1,0:T(8,128)(2,1)} %constant.28.clone.rows_b) | copy-start | bytes 147460
  17.2 3.6 %collective-permute-start.3 = (f32[32,256]{1,0:T(8,128)S(1)}, f32[32,256]{1,0:T(8,128)S(1)}, u32[]{:S(2)}, u32[]{:S(2)}) collective-permute-start(f32[32,256]{1,0:T(8,128)S(1)} %get-tuple-element.12.own), channel_id=1, source_target_pairs={{0,1},{1,0},{2,3},{3,2},{4,5},{5,4},{6,7},{7,6},{8,9},{9,8},{10,11... | collective-permute-start | bytes 98312 | tf_op jit(solution)/shard_map/ppermute | solution.py:322
  17.8 6.0 %collective-permute-start.2 = (f32[32,256]{1,0:T(8,128)S(1)}, f32[32,256]{1,0:T(8,128)S(1)}, u32[]{:S(2)}, u32[]{:S(2)}) collective-permute-start(f32[32,256]{1,0:T(8,128)S(1)} %get-tuple-element.12.own), channel_id=1, source_target_pairs={{0,15},{1,2},{2,1},{3,4},{4,3},{5,6},{6,5},{7,8},{8,7},{9,10},{10,... | collective-permute-start | bytes 98312 | tf_op jit(solution)/shard_map/ppermute | solution.py:321

commit v3 on v1

v3 whole, which is shorter than its diff:
```python
import math

import jax
import jax.numpy as jnp
import numpy as np
from jax import lax
from jax.experimental import pallas as pl
from jax.experimental.pallas import tpu as pltpu
from jax.sharding import PartitionSpec as P


MARGIN = 64

STEEPNESS = 8.0
THRESHOLD = 0.35

BF16 = jnp.bfloat16
F32 = jnp.float32
QUARTERS = 4
GROUP = 8
LIMIT = 32 << 20


def split_table(table):
    table = np.asarray(table, np.float32)
    high = table.astype(BF16)
    low = (table - high.astype(np.float32)).astype(BF16)
    return high, low


def stack_left(table):
    high, low = split_table(table)
    return np.concatenate([high, high, low], axis=1)


def angles(frequencies, positions, period):
    cycles = np.remainder(frequencies[:, None] * positions[None, :], period)
    return cycles * (2.0 * math.pi / period)


def interpolation(fine, coarse, bound, period):
    count = len(coarse)
    distance = fine[:, None] - coarse[None, :]
    total = np.ones_like(distance, dtype=np.float64)
    for frequency in range(1, bound):
        total += 2.0 * np.cos(np.remainder(frequency * distance, period) * (2.0 * math.pi / period))
    return total / count


def make_tables(strip_rows, margin, columns, freq_rows, freq_cols):
    window = strip_rows + 2 * margin
    row_freq = np.arange(freq_rows, dtype=np.float64) - freq_rows // 2
    col_freq = np.arange(freq_cols, dtype=np.float64) - freq_cols // 2
    rows_c, cols_c = 2 * freq_rows, 2 * freq_cols
    own = np.arange(margin, margin + strip_rows, dtype=np.float64)
    wide = np.arange(columns, dtype=np.float64)
    samples_r = np.arange(rows_c, dtype=np.float64) * (window / rows_c)
    samples_c = np.arange(cols_c, dtype=np.float64) * (columns / cols_c)
    factor = 1.0 / math.sqrt(window * columns)
    col_angle = angles(col_freq, wide[: columns // QUARTERS], columns)
    forward = np.concatenate([np.cos(col_angle).T, -np.sin(col_angle).T], axis=1) * factor
    row_angle = angles(row_freq, own, window)
    cos_r, sin_r = np.cos(row_angle), np.sin(row_angle)
    half = strip_rows // 2
    none = np.zeros((freq_rows, half))
    first = np.concatenate([cos_r[:, :half], none, sin_r[:, :half], none], axis=1)
    second = np.concatenate([none, cos_r[:, half:], none, sin_r[:, half:]], axis=1)
    project = np.concatenate([first, second], axis=0)
    back_rows = np.concatenate([cos_r, sin_r], axis=0).T
    coarse_r = angles(row_freq, samples_r, window)
    field_rows = np.concatenate([np.cos(coarse_r), np.sin(coarse_r)], axis=0).T
    coarse_c = angles(col_freq, samples_c, columns)
    cos_c, sin_c = np.cos(coarse_c), np.sin(coarse_c)
    field_cols = np.concatenate(
        [np.concatenate([cos_c, sin_c], axis=1), np.concatenate([-sin_c, cos_c], axis=1)], axis=0
    )
    widen_rows = interpolation(own, samples_r, freq_rows, window)
    widen_cols = interpolation(wide, samples_c, freq_cols, columns).T
    return {
        "forward": split_table(forward),
        "project": split_table(project),
        "back_rows": stack_left(back_rows),
        "field_rows": stack_left(field_rows),
        "field_rows_t": stack_left(field_rows.T),
        "field_cols": split_table(field_cols),
        "widen_rows": stack_left(widen_rows),
        "widen_rows_t": stack_left(widen_rows.T),
        "widen_cols": split_table(widen_cols),
    }


def split(value):
    high = value.astype(BF16)
    return high, (value - high.astype(F32)).astype(BF16)


def stack_right(value):
    high, low = split(value)
    return jnp.concatenate([high, low, high], axis=0)


def stack_turned(pair):
    high, low = (turn(piece, 1) for piece in split(pair))
    return jnp.concatenate([high, low, high], axis=0)


def dot(left, right):
    return jnp.dot(left, right, preferred_element_type=F32)


def dot_t(left, right):
    return lax.dot_general(left, right, (((1,), (1,)), ((), ())), preferred_element_type=F32)


def dot3(left, right):
    (lh, ll), (rh, rl) = left, right
    return dot(lh, rh) + dot(lh, rl) + dot(ll, rh)


def dot3_t(left, right):
    (lh, ll), (rh, rl) = left, right
    return dot_t(lh, rh) + dot_t(lh, rl) + dot_t(ll, rh)


def turn(pair, sign):
    half = pair.shape[1] // 2
    real, imag = pair[:, :half], pair[:, half:]
    if sign > 0:
        turned = jnp.concatenate([-imag, real], axis=1)
    else:
        turned = jnp.concatenate([imag, -real], axis=1)
    return jnp.concatenate([pair, turned], axis=0)


def alternate(shape):
    row = lax.broadcasted_iota(jnp.int32, shape, 0)
    return jnp.where(row % 2 == 0, 1.0, -1.0).astype(F32)


def is_first():
    return lax.axis_index("tiles") == 0


def is_last():
    return lax.axis_index("tiles") == lax.axis_size("tiles") - 1


def quarters(ref):
    width = ref.shape[1] // QUARTERS
    return [pl.ds(i * width, width) for i in range(QUARTERS)]


def quarter_turn(pair, count):
    half = pair.shape[1] // 2
    real, imag = pair[:, :half], pair[:, half:]
    lane = lax.broadcasted_iota(jnp.int32, (1, half), 1) - half // 2
    phase = (lane * count) & 3
    cosine = (phase == 0).astype(F32) - (phase == 2).astype(F32)
    sine = (phase == 1).astype(F32) - (phase == 3).astype(F32)
    return jnp.concatenate(
        [real * cosine - imag * sine, real * sine + imag * cosine], axis=1
    )


def project(
    mask_hbm, fwd_h_hbm, fwd_l_hbm, proj_h_hbm, proj_l_hbm, weights_hbm, slope_out, share_out, scratch
):
    mask, fwd_h, fwd_l, proj_h, proj_l, weights, sems = scratch
    columns = quarters(mask)
    masks = [
        pltpu.make_async_copy(mask_hbm.at[:, cols], mask.at[:, cols], sems.at[0, i])
        for i, cols in enumerate(columns)
    ]
    tables = [
        pltpu.make_async_copy(fwd_h_hbm, fwd_h, sems.at[1, 0]),
        pltpu.make_async_copy(fwd_l_hbm, fwd_l, sems.at[1, 1]),
    ]
    last = [
        pltpu.make_async_copy(weights_hbm, weights, sems.at[2, 2]),
        pltpu.make_async_copy(proj_h_hbm, proj_h, sems.at[2, 0]),
        pltpu.make_async_copy(proj_l_hbm, proj_l, sems.at[2, 1]),
    ]
    for copy in [masks[0], *tables, *masks[1:], *last]:
        copy.start()
    spectra = None
    for i, cols in enumerate(columns):
        masks[i].wait()
        transmit = jnp.tanh(mask[:, cols])
        slope_out[:, cols] = 1.0 - transmit * transmit
        pieces = split(transmit)
        if i == 0:
            for copy in tables:
                copy.wait()
        term = quarter_turn(dot3(pieces, (fwd_h[...], fwd_l[...])), -i)
        spectra = term if spectra is None else spectra + term
    for copy in last:
        copy.wait()
    kernels, width = share_out.shape
    whole = weights[0]
    for k in range(1, kernels):
        whole = whole + weights[k]
    rows = [jnp.full((1, width), weights[k], F32) for k in range(kernels)]
    share_out[...] = jnp.concatenate(rows, axis=0) / jnp.full((kernels, width), whole, F32)
    parts = dot3((proj_h[...], proj_l[...]), split(turn(spectra, -1)))
    half = parts.shape[0] // 2
    return parts[:half], parts[half:]


def project_first(*refs):
    args, (down, up, own, share, slope), scratch = refs[:6], refs[6:11], refs[11:]

    @pl.when(jnp.logical_not(is_last()))
    def _():
        low, high = project(*args, slope, share, scratch)
        down[...], up[...], own[...] = low, high, low + high


def project_second(*refs):
    args, taken, refs = refs[:6], refs[6:9], refs[10:]
    (near, up, own, share, slope), scratch = refs[:5], refs[5:]

    @pl.when(is_last())
    def _():
        low, high = project(*args, slope, share, scratch)
        near[...], up[...], own[...] = low, high, low + high

    @pl.when(jnp.logical_not(is_last()))
    def _():
        up[...], own[...], share[...] = (ref[...] for ref in taken)


def image(
    own, before, after, after_near, spectra, shares, target, rows_f, rows_t, cols_h, cols_l,
    wide_r, wide_rt, wide_h, wide_l, resist_hbm, grad_out, fields, resist_out, sem
):
    kernels, freq_rows, freq_cols = spectra.shape[1:]
    rows_c, cols_c = rows_f.shape[0], 2 * freq_cols
    group = math.gcd(kernels, GROUP)
    sign = alternate(own.shape)
    is_near = lax.axis_index("tiles") == lax.axis_size("tiles") - 2
    sides = before[...] + jnp.where(is_near, after_near[...], after[...])
    window = own[...] + sign * sides
    win_re, win_im = window[:, :freq_cols], window[:, freq_cols:]

    def forward(step, total):
        start = step * group
        inners = []
        for j in range(group):
            kern_re, kern_im = spectra[0, start + j], spectra[1, start + j]
            prod = jnp.concatenate(
                [kern_re * win_re - kern_im * win_im, kern_re * win_im + kern_im * win_re], axis=1
            )
            inners.append(dot(rows_f[...], stack_turned(prod)))
        inner = jnp.concatenate(inners, axis=0)
        field = dot3(split(inner), (cols_h[...], cols_l[...]))
        fields[pl.ds(pl.multiple_of(start * rows_c, rows_c), group * rows_c), :] = field
        power = field[:, :cols_c] ** 2 + field[:, cols_c:] ** 2
        for j in range(group):
            share = shares[pl.ds(start + j, 1), :]
            total = total + share * power[j * rows_c : (j + 1) * rows_c]
        return total

    total = lax.fori_loop(0, kernels // group, forward, jnp.zeros((rows_c, cols_c), F32))
    tall = dot(wide_r[...], stack_right(total))
    intensity = dot3(split(tall), (wide_h[...], wide_l[...]))
    resist = jax.nn.sigmoid(STEEPNESS * (intensity - THRESHOLD))
    resist_out[...] = resist
    sent = pltpu.make_async_copy(resist_out, resist_hbm, sem)
    sent.start()
    slopes = (4.0 * STEEPNESS) * (resist - target[...].astype(F32)) * resist * (1.0 - resist)
    narrow = dot3_t(split(slopes), (wide_h[...], wide_l[...]))
    weight = dot(wide_rt[...], stack_right(narrow))
    weight = jnp.concatenate([weight, weight], axis=1)

    def backward(step, sums):
        grad_re, grad_im = sums
        start = step * group
        scaled = jnp.concatenate(
            [
                weight * fields[pl.ds(pl.multiple_of((start + j) * rows_c, rows_c), rows_c), :]
                for j in range(group)
            ],
            axis=0,
        )
        inner = dot3_t(split(scaled), (cols_h[...], cols_l[...]))
        for j in range(group):
            spec = dot(rows_t[...], stack_right(inner[j * rows_c : (j + 1) * rows_c]))
            spec = shares[pl.ds(start + j, 1), :] * spec
            real = spec[:freq_rows, :freq_cols] + spec[freq_rows:, freq_cols:]
            imag = spec[:freq_rows, freq_cols:] - spec[freq_rows:, :freq_cols]
            kern_re, kern_im = spectra[0, start + j], spectra[1, start + j]
            grad_re = grad_re + real * kern_re + imag * kern_im
            grad_im = grad_im + imag * kern_re - real * kern_im
        return grad_re, grad_im

    none = jnp.zeros((freq_rows, freq_cols), F32)
    grad_re, grad_im = lax.fori_loop(0, kernels // group, backward, (none, none))
    grad_out[...] = jnp.concatenate([grad_re, grad_im], axis=1)
    sent.wait()


def image_first(*refs):
    @pl.when(jnp.logical_not(is_first()))
    def _():
        image(*refs)


def image_second(*refs):
    args, (_, grad_in), refs = refs[:15], refs[15:17], refs[17:]

    @pl.when(is_first())
    def _():
        image(*args, *refs)

    @pl.when(jnp.logical_not(is_first()))
    def _():
        refs[1][...] = grad_in[...]


def gradient_kernel(
    own, before, before_near, after, slope, rows_b, fwd_h, fwd_l, out_hbm, out, sems
):
    half = out.shape[0] // 2
    sign = alternate(own.shape)
    is_near = lax.axis_index("tiles") == 1
    low = stack_turned(own[...] + sign * jnp.where(is_near, before_near[...], before[...]))
    high = stack_turned(own[...] + sign * after[...])
    merged = jnp.concatenate([dot(rows_b[:half], low), dot(rows_b[half:], high)], axis=0)
    sent = []
    for i, cols in enumerate(quarters(out)):
        pieces = split(quarter_turn(merged, i))
        out[:, cols] = slope[:, cols] * dot3_t(pieces, (fwd_h[...], fwd_l[...]))
        sent.append(pltpu.make_async_copy(out.at[:, cols], out_hbm.at[:, cols], sems.at[i]))
        sent[-1].start()
    for copy in sent:
        copy.wait()


VMEM = pl.BlockSpec(memory_space=pltpu.VMEM)
HBM = pl.BlockSpec(memory_space=pltpu.HBM)


def call(kernel, outs, args, flops, scratch, out_specs, in_specs=None, aliases=None):
    shapes = [jax.ShapeDtypeStruct(shape, F32) for shape in outs]
    moved = sum(math.prod(a.shape) * a.dtype.itemsize for a in args)
    moved += sum(4 * math.prod(shape) for shape in outs)
    return pl.pallas_call(
        kernel,
        out_shape=shapes,
        in_specs=in_specs or [VMEM] * len(args),
        out_specs=out_specs,
        scratch_shapes=scratch,
        input_output_aliases=aliases or {},
        compiler_params=pltpu.CompilerParams(vmem_limit_bytes=LIMIT),
        cost_estimate=pl.CostEstimate(flops=flops, bytes_accessed=moved, transcendentals=0),
    )(*args)


def permute(value, pairs):
    return lax.ppermute(value, "tiles", pairs)


def shards(mask_params, target, kernel_spectra, kernel_weights):
    strip_rows, columns = mask_params.shape
    kernels, freq_rows, freq_cols = kernel_spectra.shape[1:]
    tables = jax.tree.map(
        jnp.asarray, make_tables(strip_rows, MARGIN, columns, freq_rows, freq_cols)
    )
    count = lax.axis_size("tiles")
    assert 2 * MARGIN == strip_rows and count % 2 == 0 and count > 2
    near_pairs = [(i, i ^ 1) for i in range(count)]
    up_pairs = [(i, (i + 1) % count) for i in range(count)]
    down_pairs = [(j, i) for i, j in up_pairs]
    pair, full, wide = (freq_rows, 2 * freq_cols), (strip_rows, columns), (kernels, 2 * freq_cols)
    area = strip_rows * columns

    args = [mask_params, *tables["forward"], *tables["project"]]
    held = [pltpu.VMEM(a.shape, a.dtype) for a in args]
    held += [pltpu.SMEM((kernels,), F32), pltpu.SemaphoreType.DMA((3, QUARTERS))]
    args.append(kernel_weights)
    args = [pltpu.with_memory_space_constraint(a, pltpu.HBM) for a in args]
    work = 60 * area * 2 * freq_cols
    send_down, send_up, own, share, slope = call(
        project_first, [pair, pair, pair, wide, full], args, work, held,
        in_specs=[HBM] * 6, out_specs=[VMEM] * 5,
    )
    after = permute(send_down, down_pairs)
    send_near, send_up, own, share, slope = call(
        project_second, [pair, pair, pair, wide, full], [*args, send_up, own, share, slope],
        work, held, in_specs=[HBM] * 6 + [VMEM] * 4, out_specs=[VMEM] * 5, aliases={9: 4},
    )
    before = permute(send_up, up_pairs)
    after_near = permute(send_near, near_pairs)

    rows_c, cols_c = 2 * freq_rows, 2 * freq_cols
    held = [
        pltpu.VMEM((kernels * rows_c, 2 * cols_c), F32),
        pltpu.VMEM(full, F32),
        pltpu.SemaphoreType.DMA,
    ]
    rest = [
        kernel_spectra, share, target,
        tables["field_rows"], tables["field_rows_t"], *tables["field_cols"],
        tables["widen_rows"], tables["widen_rows_t"], *tables["widen_cols"],
    ]
    specs = [VMEM] * 15
    work = 24 * kernels * rows_c * cols_c * cols_c
    resist, grad = call(
        image_first, [full, pair], [own, before, after, after_near, *rest], work, held,
        in_specs=specs, out_specs=[HBM, VMEM],
    )
    grad_before = permute(grad, up_pairs)
    resist, grad = call(
        image_second, [full, pair], [own, before, after, after_near, *rest, resist, grad], work, held,
        in_specs=specs + [HBM, VMEM], out_specs=[HBM, VMEM], aliases={15: 0},
    )
    grad_after = permute(grad, down_pairs)
    grad_before_near = permute(grad, near_pairs)
    (gradient,) = call(
        gradient_kernel,
        [full],
        [grad, grad_before, grad_before_near, grad_after, slope, tables["back_rows"], *tables["forward"]],
        6 * area * 2 * freq_cols,
        [pltpu.VMEM(full, F32), pltpu.SemaphoreType.DMA((QUARTERS,))],
        out_specs=[HBM],
    )
    return (resist, gradient)


def solution(mesh):
    in_specs = (P(("parts", "tiles"), None), P(("parts", "tiles"), None), P(), P())
    out_specs = (P(("parts", "tiles"), None), P(("parts", "tiles"), None))
    return jax.shard_map(shards, mesh=mesh, in_specs=in_specs, out_specs=out_specs, check_vma=False)
```

time: 32.6 us -> 28.1 us (0.86)
  starting transfers between devices: 6.54 us -> 11.3 us
  local copies, waits for them, and re-layouts: 4.71 us -> 0.09 us
  other arithmetic: 2.48 us -> 0 us
  waiting for transfers between devices: 9.5 us -> 7.12 us
  Pallas kernels: 8.15 us -> 8.66 us
    ppermute x4 -> x6, starting transfers between devices: 6.54 us -> 11.3 us  [permute(): return lax.ppermute(value, 'tiles', pairs)]
    unnamed x36 -> x26, local copies, waits for them, and re-layouts: 4.71 us -> 0.09 us
    ppermute x4 -> x6, waiting for transfers between devices: 9.5 us -> 7.12 us  [permute(): return lax.ppermute(value, 'tiles', pairs)]
    mul x1 -> x0, other arithmetic: 1.23 us -> none  [shards(): spectra = kernel_spectra * shares[None, :, None, None]]
    sqrt x1 -> x0, other arithmetic: 0.65 us -> none  [shards(): shares = jnp.sqrt(kernel_weights / jnp.sum(kernel_weights))]
    reduce_sum x1 -> x0, other arithmetic: 0.6 us -> none  [shards(): shares = jnp.sqrt(kernel_weights / jnp.sum(kernel_weights))]
    pallas_call x3 -> x5, Pallas kernels: 8.15 us -> 8.66 us  [call(): pl.pallas_call(kernel, out_shape=shapes, in_specs=in_specs or [VMEM] * le...]
  transfers between devices with their start and end apart: 4 -> 6, of which waited for: 3 -> 4; matrix products, arithmetic and copies ran while one was open for 8% -> 0% of each run, Pallas kernels for 0% -> 0%
where the time goes in v3:
time: 28.1 us; the launch traced here: 28 us
  starting transfers between devices  11.3 us (40%)
  Pallas kernels  8.66 us (31%)
  waiting for transfers between devices  7.12 us (25%)
  between operations  0.83 us (3%)
    ppermute x6, starting transfers between devices, permute(): return lax.ppermute(value, 'tiles', pairs)  11.3 us
    pallas_call x5, Pallas kernels, call(): pl.pallas_call(kernel, out_shape=shapes, in_specs=in_specs or [VMEM] * le...  8.66 us
    ppermute x6, waiting for transfers between devices, permute(): return lax.ppermute(value, 'tiles', pairs)  7.12 us
  transfers between devices with their start and end apart: 6, of which 4 were waited for; matrix products, arithmetic and copies ran while one was open for 0% of the time, Pallas kernels for 0%

profile of v3, /device:TPU:0, one launch (start us, length us, event | category | flops | bytes accessed | tf_op | source)
XLA Modules:
  0.0 28.0 jit_solution(17928778360622933736)
XLA Ops:
  0.6 2.4 %shard_map.176 = (f32[32,256]{1,0:T(8,128)S(1)}, f32[32,256]{1,0:T(8,128)S(1)}, f32[32,256]{1,0:T(8,128)S(1)}, f32[16,256]{1,0:T(8,128)S(1)}, f32[128,1024]{1,0:T(8,128)S(1)}) custom-call(f32[128,1024]{1,0:T(8,128)} %refs_0_.3, bf16[256,256]{1,0:T(8,128)(2,1)} %constant.31.clone.refs_1_.fwd_h, bf16[256,256]{1,0:T(8,128)(2,1)} %constant.32.clone.refs_2_.fwd_l, ...), custom_call_target="tpu_custom_call" | custom-call | flops 2013265920 | bytes 1491008 | tf_op jit(solution)/shard_map/pallas_call | solution.py:347
  3.1 0.0 copy-start.5
  3.1 0.0 copy-start.6
  3.1 0.0 copy-start.7
  3.1 0.0 copy-start.8
  3.1 0.0 copy-start.9
  3.1 0.0 copy-start.10
  3.1 0.0 copy-start.11
  3.1 0.0 copy-start.12
  3.2 0.1 shard_map.177
  3.3 0.5 %collective-permute-start = (f32[32,256]{1,0:T(8,128)S(1)}, f32[32,256]{1,0:T(8,128)S(1)}, u32[]{:S(2)}, u32[]{:S(2)}) collective-permute-start(f32[32,256]{1,0:T(8,128)S(1)} %get-tuple-element.21), channel_id=1, source_target_pairs={{0,1},{1,2},{2,3},{3,4},{4,5},{5,6},{6,7},{7,8},{8,9},{9,10},{10,1... | collective-permute-start | bytes 98312 | tf_op jit(solution)/shard_map/ppermute | solution.py:360
  3.8 2.6 %collective-permute-start.2 = (f32[32,256]{1,0:T(8,128)S(1)}, f32[32,256]{1,0:T(8,128)S(1)}, u32[]{:S(2)}, u32[]{:S(2)}) collective-permute-start(f32[32,256]{1,0:T(8,128)S(1)} %get-tuple-element.23), channel_id=1, source_target_pairs={{0,1},{1,0},{2,3},{3,2},{4,5},{5,4},{6,7},{7,6},{8,9},{9,8},{10,11... | collective-permute-start | bytes 98312 | tf_op jit(solution)/shard_map/ppermute | solution.py:360
  6.5 3.1 %collective-permute-start.1 = (f32[32,256]{1,0:T(8,128)S(1)}, f32[32,256]{1,0:T(8,128)S(1)}, u32[]{:S(2)}, u32[]{:S(2)}) collective-permute-start(f32[32,256]{1,0:T(8,128)S(1)} %get-tuple-element.22), channel_id=1, source_target_pairs={{1,0},{2,1},{3,2},{4,3},{5,4},{6,5},{7,6},{8,7},{9,8},{10,9},{11,1... | collective-permute-start | bytes 98312 | tf_op jit(solution)/shard_map/ppermute | solution.py:360
  9.6 1.0 %collective-permute-done.refs_1_ = f32[32,256]{1,0:T(8,128)S(1)} collective-permute-done((f32[32,256]{1,0:T(8,128)S(1)}, f32[32,256]{1,0:T(8,128)S(1)}, u32[]{:S(2)}, u32[]{:S(2)}) %collective-permute-start) | collective-permute-done | bytes 32800 | tf_op jit(solution)/shard_map/ppermute | solution.py:360
  10.6 0.6 %collective-permute-done.1.refs_2_ = f32[32,256]{1,0:T(8,128)S(1)} collective-permute-done((f32[32,256]{1,0:T(8,128)S(1)}, f32[32,256]{1,0:T(8,128)S(1)}, u32[]{:S(2)}, u32[]{:S(2)}) %collective-permute-start.1) | collective-permute-done | bytes 32800 | tf_op jit(solution)/shard_map/ppermute | solution.py:360
  11.3 0.0 copy-start
  11.3 0.0 copy-start.1
  11.3 0.0 copy-start.2
  11.3 4.6 %shard_map.179 = (f32[128,1024]{1,0:T(8,128)}, f32[32,256]{1,0:T(8,128)S(1)}) custom-call(f32[32,256]{1,0:T(8,128)S(1)} %get-tuple-element.20.refs_0_, f32[32,256]{1,0:T(8,128)S(1)} %collective-permute-done.refs_1_, f32[32,256]{1,0:T(8,128)S(1)} %collective-permute-done.1.refs_2_, ...), custom_call_target="tpu_custom_call", output_to_operand_aliasing={{0}: (15, {})} | custom-call | flops 1610612736 | bytes 4030464 | tf_op jit(solution)/shard_map/pallas_call | solution.py:347
  16.0 4.5 %collective-permute-start.5 = (f32[32,256]{1,0:T(8,128)S(1)}, f32[32,256]{1,0:T(8,128)S(1)}, u32[]{:S(2)}, u32[]{:S(2)}) collective-permute-start(f32[32,256]{1,0:T(8,128)S(1)} %get-tuple-element.28.own), channel_id=1, source_target_pairs={{1,0},{2,1},{3,2},{4,3},{5,4},{6,5},{7,6},{8,7},{9,8},{10,9},{11,1... | collective-permute-start | bytes 98312 | tf_op jit(solution)/shard_map/ppermute | solution.py:360
  20.5 0.5 %collective-permute-start.3 = (f32[32,256]{1,0:T(8,128)S(1)}, f32[32,256]{1,0:T(8,128)S(1)}, u32[]{:S(2)}, u32[]{:S(2)}) collective-permute-start(f32[32,256]{1,0:T(8,128)S(1)} %get-tuple-element.26.refs_16_), channel_id=1, source_target_pairs={{0,1},{1,2},{2,3},{3,4},{4,5},{5,6},{6,7},{7,8},{8,9},{9,10},{10,1... | collective-permute-start | bytes 98312 | tf_op jit(solution)/shard_map/ppermute | solution.py:360
  21.0 1.1 %collective-permute-done.5.after = f32[32,256]{1,0:T(8,128)S(1)} collective-permute-done((f32[32,256]{1,0:T(8,128)S(1)}, f32[32,256]{1,0:T(8,128)S(1)}, u32[]{:S(2)}, u32[]{:S(2)}) %collective-permute-start.5) | collective-permute-done | bytes 32800 | tf_op jit(solution)/shard_map/ppermute | solution.py:360
  22.1 4.4 %collective-permute-done.3.before = f32[32,256]{1,0:T(8,128)S(1)} collective-permute-done((f32[32,256]{1,0:T(8,128)S(1)}, f32[32,256]{1,0:T(8,128)S(1)}, u32[]{:S(2)}, u32[]{:S(2)}) %collective-permute-start.3) | collective-permute-done | bytes 32800 | tf_op jit(solution)/shard_map/ppermute | solution.py:360
  26.5 1.5 %shard_map.180 = f32[128,1024]{1,0:T(8,128)} custom-call(f32[32,256]{1,0:T(8,128)S(1)} %get-tuple-element.28.own, f32[32,256]{1,0:T(8,128)S(1)} %collective-permute-done.3.before, f32[32,256]{1,0:T(8,128)S(1)} %collective-permute-done.4.before_near, f32[32,256]{1,0:T(8,128)S(1)} %collective-permute-done.5.after, f32[128,1024]{1,0:T(8,128)S(1)} %get-tuple-element.29.slope, ...), custom_call_target="tpu_custom_call" | custom-call | flops 201326592 | bytes 1490944 | tf_op jit(solution)/shard_map/pallas_call | solution.py:347
  (19 shorter events, 0.1 us)
Async XLA Ops:
  3.0 8.1 %copy-start.3 = (f32[2,16,32,128]{3,2,1,0:T(8,128)S(1)}, f32[2,16,32,128]{3,2,1,0:T(8,128)}, u32[]{:S(2)}) copy-start(f32[2,16,32,128]{3,2,1,0:T(8,128)} %refs_4_.5) | copy-start | bytes 1572868
  3.0 8.1 %copy-start.4 = (s32[128,1024]{1,0:T(8,128)S(1)}, s32[128,1024]{1,0:T(8,128)}, u32[]{:S(2)}) copy-start(s32[128,1024]{1,0:T(8,128)} %refs_6_.3) | copy-start | bytes 1572868
  3.1 8.1 %copy-start.5 = (bf16[256,1024]{1,0:T(8,128)(2,1)S(1)}, bf16[256,1024]{1,0:T(8,128)(2,1)}, u32[]{:S(2)}) copy-start(bf16[256,1024]{1,0:T(8,128)(2,1)} %constant.36.clone.refs_14_) | copy-start | bytes 1572868
  3.1 8.1 %copy-start.6 = (bf16[256,1024]{1,0:T(8,128)(2,1)S(1)}, bf16[256,1024]{1,0:T(8,128)(2,1)}, u32[]{:S(2)}) copy-start(bf16[256,1024]{1,0:T(8,128)(2,1)} %constant.35.clone.refs_13_) | copy-start | bytes 1572868
  3.1 8.1 %copy-start.7 = (bf16[256,512]{1,0:T(8,128)(2,1)S(1)}, bf16[256,512]{1,0:T(8,128)(2,1)}, u32[]{:S(2)}) copy-start(bf16[256,512]{1,0:T(8,128)(2,1)} %constant.28.clone.refs_10_) | copy-start | bytes 786436
  3.1 8.1 %copy-start.8 = (bf16[256,512]{1,0:T(8,128)(2,1)S(1)}, bf16[256,512]{1,0:T(8,128)(2,1)}, u32[]{:S(2)}) copy-start(bf16[256,512]{1,0:T(8,128)(2,1)} %constant.27.clone.refs_9_) | copy-start | bytes 786436
  3.1 8.1 %copy-start.9 = (bf16[128,192]{1,0:T(8,128)(2,1)S(1)}, bf16[128,192]{1,0:T(8,128)(2,1)}, u32[]{:S(2)}) copy-start(bf16[128,192]{1,0:T(8,128)(2,1)} %constant.37.clone.refs_11_) | copy-start | bytes 147460
  3.1 8.1 %copy-start.10 = (bf16[64,384]{1,0:T(8,128)(2,1)S(1)}, bf16[64,384]{1,0:T(8,128)(2,1)}, u32[]{:S(2)}) copy-start(bf16[64,384]{1,0:T(8,128)(2,1)} %constant.38.clone.refs_12_) | copy-start | bytes 147460
  3.1 8.1 %copy-start.11 = (bf16[64,192]{1,0:T(8,128)(2,1)S(1)}, bf16[64,192]{1,0:T(8,128)(2,1)}, u32[]{:S(2)}) copy-start(bf16[64,192]{1,0:T(8,128)(2,1)} %constant.30.clone.refs_8_) | copy-start | bytes 73732
  3.1 8.1 %copy-start.12 = (bf16[64,192]{1,0:T(8,128)(2,1)S(1)}, bf16[64,192]{1,0:T(8,128)(2,1)}, u32[]{:S(2)}) copy-start(bf16[64,192]{1,0:T(8,128)(2,1)} %constant.29.clone.refs_7_) | copy-start | bytes 73732
  3.3 7.3 %collective-permute-start = (f32[32,256]{1,0:T(8,128)S(1)}, f32[32,256]{1,0:T(8,128)S(1)}, u32[]{:S(2)}, u32[]{:S(2)}) collective-permute-start(f32[32,256]{1,0:T(8,128)S(1)} %get-tuple-element.21), channel_id=1, source_target_pairs={{0,1},{1,2},{2,3},{3,4},{4,5},{5,6},{6,7},{7,8},{8,9},{9,10},{10,1... | collective-permute-start | bytes 98312 | tf_op jit(solution)/shard_map/ppermute | solution.py:360
  3.8 6.7 %collective-permute-start.2 = (f32[32,256]{1,0:T(8,128)S(1)}, f32[32,256]{1,0:T(8,128)S(1)}, u32[]{:S(2)}, u32[]{:S(2)}) collective-permute-start(f32[32,256]{1,0:T(8,128)S(1)} %get-tuple-element.23), channel_id=1, source_target_pairs={{0,1},{1,0},{2,3},{3,2},{4,5},{5,4},{6,7},{7,6},{8,9},{9,8},{10,11... | collective-permute-start | bytes 98312 | tf_op jit(solution)/shard_map/ppermute | solution.py:360
  6.5 4.7 %collective-permute-start.1 = (f32[32,256]{1,0:T(8,128)S(1)}, f32[32,256]{1,0:T(8,128)S(1)}, u32[]{:S(2)}, u32[]{:S(2)}) collective-permute-start(f32[32,256]{1,0:T(8,128)S(1)} %get-tuple-element.22), channel_id=1, source_target_pairs={{1,0},{2,1},{3,2},{4,3},{5,4},{6,5},{7,6},{8,7},{9,8},{10,9},{11,1... | collective-permute-start | bytes 98312 | tf_op jit(solution)/shard_map/ppermute | solution.py:360
  11.3 15.2 %copy-start = (bf16[256,256]{1,0:T(8,128)(2,1)S(1)}, bf16[256,256]{1,0:T(8,128)(2,1)}, u32[]{:S(2)}) copy-start(bf16[256,256]{1,0:T(8,128)(2,1)} %constant.32.clone.refs_2_.fwd_l) | copy-start | bytes 393220
  11.3 15.2 %copy-start.1 = (bf16[256,256]{1,0:T(8,128)(2,1)S(1)}, bf16[256,256]{1,0:T(8,128)(2,1)}, u32[]{:S(2)}) copy-start(bf16[256,256]{1,0:T(8,128)(2,1)} %constant.31.clone.refs_1_.fwd_h) | copy-start | bytes 393220
  11.3 15.2 %copy-start.2 = (bf16[128,192]{1,0:T(8,128)(2,1)S(1)}, bf16[128,192]{1,0:T(8,128)(2,1)}, u32[]{:S(2)}) copy-start(bf16[128,192]{1,0:T(8,128)(2,1)} %constant.26.clone.rows_b) | copy-start | bytes 147460
  16.0 6.1 %collective-permute-start.5 = (f32[32,256]{1,0:T(8,128)S(1)}, f32[32,256]{1,0:T(8,128)S(1)}, u32[]{:S(2)}, u32[]{:S(2)}) collective-permute-start(f32[32,256]{1,0:T(8,128)S(1)} %get-tuple-element.28.own), channel_id=1, source_target_pairs={{1,0},{2,1},{3,2},{4,3},{5,4},{6,5},{7,6},{8,7},{9,8},{10,9},{11,1... | collective-permute-start | bytes 98312 | tf_op jit(solution)/shard_map/ppermute | solution.py:360
  20.5 1.6 %collective-permute-start.4 = (f32[32,256]{1,0:T(8,128)S(1)}, f32[32,256]{1,0:T(8,128)S(1)}, u32[]{:S(2)}, u32[]{:S(2)}) collective-permute-start(f32[32,256]{1,0:T(8,128)S(1)} %get-tuple-element.28.own), channel_id=1, source_target_pairs={{0,1},{1,0},{2,3},{3,2},{4,5},{5,4},{6,7},{7,6},{8,9},{9,8},{10,11... | collective-permute-start | bytes 98312 | tf_op jit(solution)/shard_map/ppermute | solution.py:360
  20.5 6.0 %collective-permute-start.3 = (f32[32,256]{1,0:T(8,128)S(1)}, f32[32,256]{1,0:T(8,128)S(1)}, u32[]{:S(2)}, u32[]{:S(2)}) collective-permute-start(f32[32,256]{1,0:T(8,128)S(1)} %get-tuple-element.26.refs_16_), channel_id=1, source_target_pairs={{0,1},{1,2},{2,3},{3,4},{4,5},{5,6},{6,7},{7,8},{8,9},{9,10},{10,1... | collective-permute-start | bytes 98312 | tf_op jit(solution)/shard_map/ppermute | solution.py:360

commit v4 on v3

--- a/solution.py
+++ b/solution.py
@@ -143,6 +143,10 @@
 
 def is_last():
     return lax.axis_index("tiles") == lax.axis_size("tiles") - 1
+
+
+def is_odd():
+    return lax.axis_index("tiles") % 2 == 1
 
 
 def quarters(ref):
@@ -207,39 +211,40 @@
 
 
 def project_first(*refs):
-    args, (down, up, own, share, slope), scratch = refs[:6], refs[6:11], refs[11:]
+    args, (far, near, own, share, slope), scratch = refs[:6], refs[6:11], refs[11:]
 
     @pl.when(jnp.logical_not(is_last()))
     def _():
         low, high = project(*args, slope, share, scratch)
-        down[...], up[...], own[...] = low, high, low + high
+        odd = is_odd()
+        far[...] = jnp.where(odd, high, low)
+        near[...] = jnp.where(odd, low, high)
+        own[...] = low + high
 
 
 def project_second(*refs):
-    args, taken, refs = refs[:6], refs[6:9], refs[10:]
-    (near, up, own, share, slope), scratch = refs[:5], refs[5:]
+    args, taken, refs = refs[:6], refs[6:10], refs[11:]
+    (far, near, own, share, slope), scratch = refs[:5], refs[5:]
 
     @pl.when(is_last())
     def _():
         low, high = project(*args, slope, share, scratch)
-        near[...], up[...], own[...] = low, high, low + high
+        far[...], near[...], own[...] = high, low, low + high
 
     @pl.when(jnp.logical_not(is_last()))
     def _():
-        up[...], own[...], share[...] = (ref[...] for ref in taken)
+        far[...], near[...], own[...], share[...] = (ref[...] for ref in taken)
 
 
 def image(
-    own, before, after, after_near, spectra, shares, target, rows_f, rows_t, cols_h, cols_l,
+    own, far, near, spectra, shares, target, rows_f, rows_t, cols_h, cols_l,
     wide_r, wide_rt, wide_h, wide_l, resist_hbm, grad_out, fields, resist_out, sem
 ):
     kernels, freq_rows, freq_cols = spectra.shape[1:]
     rows_c, cols_c = rows_f.shape[0], 2 * freq_cols
     group = math.gcd(kernels, GROUP)
     sign = alternate(own.shape)
-    is_near = lax.axis_index("tiles") == lax.axis_size("tiles") - 2
-    sides = before[...] + jnp.where(is_near, after_near[...], after[...])
-    window = own[...] + sign * sides
+    window = own[...] + sign * (far[...] + near[...])
     win_re, win_im = window[:, :freq_cols], window[:, freq_cols:]
 
     def forward(step, total):
@@ -306,7 +311,7 @@
 
 
 def image_second(*refs):
-    args, (_, grad_in), refs = refs[:15], refs[15:17], refs[17:]
+    args, (_, grad_in), refs = refs[:14], refs[14:16], refs[16:]
 
     @pl.when(is_first())
     def _():
@@ -318,12 +323,12 @@
 
 
 def gradient_kernel(
-    own, before, before_near, after, slope, rows_b, fwd_h, fwd_l, out_hbm, out, sems
+    own, before_even, before_odd, after, slope, rows_b, fwd_h, fwd_l, out_hbm, out, sems
 ):
     half = out.shape[0] // 2
     sign = alternate(own.shape)
-    is_near = lax.axis_index("tiles") == 1
-    low = stack_turned(own[...] + sign * jnp.where(is_near, before_near[...], before[...]))
+    before = jnp.where(is_odd(), before_odd[...], before_even[...])
+    low = stack_turned(own[...] + sign * before)
     high = stack_turned(own[...] + sign * after[...])
     merged = jnp.concatenate([dot(rows_b[:half], low), dot(rows_b[half:], high)], axis=0)
     sent = []
@@ -367,10 +372,14 @@
         jnp.asarray, make_tables(strip_rows, MARGIN, columns, freq_rows, freq_cols)
     )
     count = lax.axis_size("tiles")
-    assert 2 * MARGIN == strip_rows and count % 2 == 0 and count > 2
+    assert 2 * MARGIN == strip_rows and count % 2 == 0 and count >= 6
     near_pairs = [(i, i ^ 1) for i in range(count)]
-    up_pairs = [(i, (i + 1) % count) for i in range(count)]
-    down_pairs = [(j, i) for i, j in up_pairs]
+    far_pairs = [(i, (i + 1 if i % 2 else i - 1) % count) for i in range(count)]
+    last = count - 1
+    ends = [(last, 0), (0, last - 1), (last - 1, last), (1, 2), (2, 3), (3, 1)]
+    wrap1_pairs = ends + near_pairs[4 : last - 1]
+    wrap2_pairs = [(last, 0), (0, 1), (1, 2), (2, last)] + far_pairs[3:last]
+    down_pairs = [(i, (i - 1) % count) for i in range(count)]
     pair, full, wide = (freq_rows, 2 * freq_cols), (strip_rows, columns), (kernels, 2 * freq_cols)
     area = strip_rows * columns
 
@@ -380,17 +389,18 @@
     args.append(kernel_weights)
     args = [pltpu.with_memory_space_constraint(a, pltpu.HBM) for a in args]
     work = 60 * area * 2 * freq_cols
-    send_down, send_up, own, share, slope = call(
+    send_far, send_near, own, share, slope = call(
         project_first, [pair, pair, pair, wide, full], args, work, held,
         in_specs=[HBM] * 6, out_specs=[VMEM] * 5,
     )
-    after = permute(send_down, down_pairs)
-    send_near, send_up, own, share, slope = call(
-        project_second, [pair, pair, pair, wide, full], [*args, send_up, own, share, slope],
-        work, held, in_specs=[HBM] * 6 + [VMEM] * 4, out_specs=[VMEM] * 5, aliases={9: 4},
-    )
-    before = permute(send_up, up_pairs)
-    after_near = permute(send_near, near_pairs)
+    far = permute(send_far, far_pairs)
+    send_far, send_near, own, share, slope = call(
+        project_second, [pair, pair, pair, wide, full],
+        [*args, send_far, send_near, own, share, slope],
+        work, held, in_specs=[HBM] * 6 + [VMEM] * 5, out_specs=[VMEM] * 5, aliases={10: 4},
+    )
+    near = permute(send_near, near_pairs)
+    far_first = permute(send_far, wrap1_pairs)
 
     rows_c, cols_c = 2 * freq_rows, 2 * freq_cols
     held = [
@@ -403,23 +413,26 @@
         tables["field_rows"], tables["field_rows_t"], *tables["field_cols"],
         tables["widen_rows"], tables["widen_rows_t"], *tables["widen_cols"],
     ]
-    specs = [VMEM] * 15
+    specs = [VMEM] * 14
     work = 24 * kernels * rows_c * cols_c * cols_c
     resist, grad = call(
-        image_first, [full, pair], [own, before, after, after_near, *rest], work, held,
+        image_first, [full, pair], [own, far, near, *rest], work, held,
         in_specs=specs, out_specs=[HBM, VMEM],
     )
-    grad_before = permute(grad, up_pairs)
+    grad_before_even = permute(grad, wrap2_pairs)
     resist, grad = call(
-        image_second, [full, pair], [own, before, after, after_near, *rest, resist, grad], work, held,
-        in_specs=specs + [HBM, VMEM], out_specs=[HBM, VMEM], aliases={15: 0},
+        image_second, [full, pair], [own, far_first, near, *rest, resist, grad], work, held,
+        in_specs=specs + [HBM, VMEM], out_specs=[HBM, VMEM], aliases={14: 0},
     )
     grad_after = permute(grad, down_pairs)
-    grad_before_near = permute(grad, near_pairs)
+    grad_before_odd = permute(grad, near_pairs)
     (gradient,) = call(
         gradient_kernel,
         [full],
-        [grad, grad_before, grad_before_near, grad_after, slope, tables["back_rows"], *tables["forward"]],
+        [
+            grad, grad_before_even, grad_before_odd, grad_after, slope,
+            tables["back_rows"], *tables["forward"],
+        ],
         6 * area * 2 * freq_cols,
         [pltpu.VMEM(full, F32), pltpu.SemaphoreType.DMA((QUARTERS,))],
         out_specs=[HBM],

time: 28.1 us -> 28.4 us (1.011)
  waiting for transfers between devices: 7.12 us -> 11.3 us
  starting transfers between devices: 11.3 us -> 7.47 us
    ppermute x6, waiting for transfers between devices: 7.12 us -> 11.3 us  [permute(): return lax.ppermute(value, 'tiles', pairs)]
    ppermute x6, starting transfers between devices: 11.3 us -> 7.47 us  [permute(): return lax.ppermute(value, 'tiles', pairs)]
where the time goes in v4:
time: 28.4 us; the launch traced here: 28.3 us
  waiting for transfers between devices  11.3 us (40%)
  Pallas kernels  8.64 us (30%)
  starting transfers between devices  7.47 us (26%)
  between operations  0.81 us (3%)
    ppermute x6, waiting for transfers between devices, permute(): return lax.ppermute(value, 'tiles', pairs)  11.3 us
    pallas_call x5, Pallas kernels, call(): pl.pallas_call(kernel, out_shape=shapes, in_specs=in_specs or [VMEM] * le...  8.64 us
    ppermute x6, starting transfers between devices, permute(): return lax.ppermute(value, 'tiles', pairs)  7.47 us
  transfers between devices with their start and end apart: 6, of which 4 were waited for; matrix products, arithmetic and copies ran while one was open for 0% of the time, Pallas kernels for 0%

profile of v4, /device:TPU:0, one launch (start us, length us, event | category | flops | bytes accessed | tf_op | source)
XLA Modules:
  0.0 28.3 jit_solution(6383447940113044575)
XLA Ops:
  0.6 2.4 %shard_map.176 = (f32[32,256]{1,0:T(8,128)S(1)}, f32[32,256]{1,0:T(8,128)S(1)}, f32[32,256]{1,0:T(8,128)S(1)}, f32[16,256]{1,0:T(8,128)S(1)}, f32[128,1024]{1,0:T(8,128)S(1)}) custom-call(f32[128,1024]{1,0:T(8,128)} %refs_0_.3, bf16[256,256]{1,0:T(8,128)(2,1)} %constant.31.clone.refs_1_.fwd_h, bf16[256,256]{1,0:T(8,128)(2,1)} %constant.32.clone.refs_2_.fwd_l, ...), custom_call_target="tpu_custom_call" | custom-call | flops 2013265920 | bytes 1491008 | tf_op jit(solution)/shard_map/pallas_call | solution.py:352
  3.0 0.0 copy-start.3
  3.0 0.0 copy-start.4
  3.1 0.0 copy-start.5
  3.1 0.0 copy-start.6
  3.1 0.0 copy-start.7
  3.1 0.0 copy-start.8
  3.1 0.0 copy-start.9
  3.1 0.0 copy-start.10
  3.1 0.0 copy-start.11
  3.1 0.0 copy-start.12
  3.2 0.1 shard_map.177
  3.3 0.6 %collective-permute-start.1 = (f32[32,256]{1,0:T(8,128)S(1)}, f32[32,256]{1,0:T(8,128)S(1)}, u32[]{:S(2)}, u32[]{:S(2)}) collective-permute-start(f32[32,256]{1,0:T(8,128)S(1)} %get-tuple-element.23), channel_id=1, source_target_pairs={{0,1},{1,0},{2,3},{3,2},{4,5},{5,4},{6,7},{7,6},{8,9},{9,8},{10,11... | collective-permute-start | bytes 98312 | tf_op jit(solution)/shard_map/ppermute | solution.py:365
  3.9 5.7 %collective-permute-start.2 = (f32[32,256]{1,0:T(8,128)S(1)}, f32[32,256]{1,0:T(8,128)S(1)}, u32[]{:S(2)}, u32[]{:S(2)}) collective-permute-start(f32[32,256]{1,0:T(8,128)S(1)} %get-tuple-element.16.refs_6_), channel_id=1, source_target_pairs={{0,15},{1,2},{2,1},{3,4},{4,3},{5,6},{6,5},{7,8},{8,7},{9,10},{10,... | collective-permute-start | bytes 98312 | tf_op jit(solution)/shard_map/ppermute | solution.py:365
  9.5 0.5 %collective-permute-start = (f32[32,256]{1,0:T(8,128)S(1)}, f32[32,256]{1,0:T(8,128)S(1)}, u32[]{:S(2)}, u32[]{:S(2)}) collective-permute-start(f32[32,256]{1,0:T(8,128)S(1)} %get-tuple-element.22), channel_id=1, source_target_pairs={{15,0},{0,14},{14,15},{1,2},{2,3},{3,1},{4,5},{5,4},{6,7},{7,6},{8... | collective-permute-start | bytes 98312 | tf_op jit(solution)/shard_map/ppermute | solution.py:365
  10.0 1.1 %collective-permute-done.2.refs_1_ = f32[32,256]{1,0:T(8,128)S(1)} collective-permute-done((f32[32,256]{1,0:T(8,128)S(1)}, f32[32,256]{1,0:T(8,128)S(1)}, u32[]{:S(2)}, u32[]{:S(2)}) %collective-permute-start.2) | collective-permute-done | bytes 32800 | tf_op jit(solution)/shard_map/ppermute | solution.py:365
  11.2 4.3 %collective-permute-done.refs_1_ = f32[32,256]{1,0:T(8,128)S(1)} collective-permute-done((f32[32,256]{1,0:T(8,128)S(1)}, f32[32,256]{1,0:T(8,128)S(1)}, u32[]{:S(2)}, u32[]{:S(2)}) %collective-permute-start) | collective-permute-done | bytes 32800 | tf_op jit(solution)/shard_map/ppermute | solution.py:365
  15.6 4.6 %shard_map.179 = (f32[128,1024]{1,0:T(8,128)}, f32[32,256]{1,0:T(8,128)S(1)}) custom-call(f32[32,256]{1,0:T(8,128)S(1)} %get-tuple-element.21.refs_0_, f32[32,256]{1,0:T(8,128)S(1)} %collective-permute-done.refs_1_, f32[32,256]{1,0:T(8,128)S(1)} %collective-permute-done.1.refs_2_, ...), custom_call_target="tpu_custom_call", output_to_operand_aliasing={{0}: (14, {})} | custom-call | flops 1610612736 | bytes 3997696 | tf_op jit(solution)/shard_map/pallas_call | solution.py:352
  20.2 0.2 collective-permute-start.5
  20.4 0.3 %collective-permute-start.4 = (f32[32,256]{1,0:T(8,128)S(1)}, f32[32,256]{1,0:T(8,128)S(1)}, u32[]{:S(2)}, u32[]{:S(2)}) collective-permute-start(f32[32,256]{1,0:T(8,128)S(1)} %get-tuple-element.28.own), channel_id=1, source_target_pairs={{0,1},{1,0},{2,3},{3,2},{4,5},{5,4},{6,7},{7,6},{8,9},{9,8},{10,11... | collective-permute-start | bytes 98312 | tf_op jit(solution)/shard_map/ppermute | solution.py:365
  20.7 0.2 collective-permute-start.3
  20.9 1.1 %collective-permute-done.5.after = f32[32,256]{1,0:T(8,128)S(1)} collective-permute-done((f32[32,256]{1,0:T(8,128)S(1)}, f32[32,256]{1,0:T(8,128)S(1)}, u32[]{:S(2)}, u32[]{:S(2)}) %collective-permute-start.5) | collective-permute-done | bytes 32800 | tf_op jit(solution)/shard_map/ppermute | solution.py:365
  22.0 4.8 %collective-permute-done.3.before_even = f32[32,256]{1,0:T(8,128)S(1)} collective-permute-done((f32[32,256]{1,0:T(8,128)S(1)}, f32[32,256]{1,0:T(8,128)S(1)}, u32[]{:S(2)}, u32[]{:S(2)}) %collective-permute-start.3) | collective-permute-done | bytes 32800 | tf_op jit(solution)/shard_map/ppermute | solution.py:365
  26.8 1.5 %shard_map.180 = f32[128,1024]{1,0:T(8,128)} custom-call(f32[32,256]{1,0:T(8,128)S(1)} %get-tuple-element.28.own, f32[32,256]{1,0:T(8,128)S(1)} %collective-permute-done.3.before_even, f32[32,256]{1,0:T(8,128)S(1)} %collective-permute-done.4.before_odd, f32[32,256]{1,0:T(8,128)S(1)} %collective-permute-done.5.after, ...), custom_call_target="tpu_custom_call" | custom-call | flops 201326592 | bytes 1490944 | tf_op jit(solution)/shard_map/pallas_call | solution.py:352
  (19 shorter events, 0.1 us)
Async XLA Ops:
  3.0 8.1 %copy-start.3 = (f32[2,16,32,128]{3,2,1,0:T(8,128)S(1)}, f32[2,16,32,128]{3,2,1,0:T(8,128)}, u32[]{:S(2)}) copy-start(f32[2,16,32,128]{3,2,1,0:T(8,128)} %refs_3_.5) | copy-start | bytes 1572868
  3.0 8.1 %copy-start.4 = (s32[128,1024]{1,0:T(8,128)S(1)}, s32[128,1024]{1,0:T(8,128)}, u32[]{:S(2)}) copy-start(s32[128,1024]{1,0:T(8,128)} %refs_5_.7) | copy-start | bytes 1572868
  3.1 8.1 %copy-start.5 = (bf16[256,1024]{1,0:T(8,128)(2,1)S(1)}, bf16[256,1024]{1,0:T(8,128)(2,1)}, u32[]{:S(2)}) copy-start(bf16[256,1024]{1,0:T(8,128)(2,1)} %constant.36.clone.refs_13_) | copy-start | bytes 1572868
  3.1 8.1 %copy-start.6 = (bf16[256,1024]{1,0:T(8,128)(2,1)S(1)}, bf16[256,1024]{1,0:T(8,128)(2,1)}, u32[]{:S(2)}) copy-start(bf16[256,1024]{1,0:T(8,128)(2,1)} %constant.35.clone.refs_12_) | copy-start | bytes 1572868
  3.1 8.1 %copy-start.7 = (bf16[256,512]{1,0:T(8,128)(2,1)S(1)}, bf16[256,512]{1,0:T(8,128)(2,1)}, u32[]{:S(2)}) copy-start(bf16[256,512]{1,0:T(8,128)(2,1)} %constant.28.clone.refs_9_) | copy-start | bytes 786436
  3.1 8.0 %copy-start.8 = (bf16[256,512]{1,0:T(8,128)(2,1)S(1)}, bf16[256,512]{1,0:T(8,128)(2,1)}, u32[]{:S(2)}) copy-start(bf16[256,512]{1,0:T(8,128)(2,1)} %constant.27.clone.refs_8_) | copy-start | bytes 786436
  3.1 8.0 %copy-start.9 = (bf16[128,192]{1,0:T(8,128)(2,1)S(1)}, bf16[128,192]{1,0:T(8,128)(2,1)}, u32[]{:S(2)}) copy-start(bf16[128,192]{1,0:T(8,128)(2,1)} %constant.37.clone.refs_10_) | copy-start | bytes 147460
  3.1 8.0 %copy-start.10 = (bf16[64,384]{1,0:T(8,128)(2,1)S(1)}, bf16[64,384]{1,0:T(8,128)(2,1)}, u32[]{:S(2)}) copy-start(bf16[64,384]{1,0:T(8,128)(2,1)} %constant.38.clone.refs_11_) | copy-start | bytes 147460
  3.1 8.0 %copy-start.11 = (bf16[64,192]{1,0:T(8,128)(2,1)S(1)}, bf16[64,192]{1,0:T(8,128)(2,1)}, u32[]{:S(2)}) copy-start(bf16[64,192]{1,0:T(8,128)(2,1)} %constant.30.clone.refs_7_) | copy-start | bytes 73732
  3.1 8.0 %copy-start.12 = (bf16[64,192]{1,0:T(8,128)(2,1)S(1)}, bf16[64,192]{1,0:T(8,128)(2,1)}, u32[]{:S(2)}) copy-start(bf16[64,192]{1,0:T(8,128)(2,1)} %constant.29.clone.refs_6_) | copy-start | bytes 73732
  3.3 6.7 %collective-permute-start.1 = (f32[32,256]{1,0:T(8,128)S(1)}, f32[32,256]{1,0:T(8,128)S(1)}, u32[]{:S(2)}, u32[]{:S(2)}) collective-permute-start(f32[32,256]{1,0:T(8,128)S(1)} %get-tuple-element.23), channel_id=1, source_target_pairs={{0,1},{1,0},{2,3},{3,2},{4,5},{5,4},{6,7},{7,6},{8,9},{9,8},{10,11... | collective-permute-start | bytes 98312 | tf_op jit(solution)/shard_map/ppermute | solution.py:365
  3.9 7.3 %collective-permute-start.2 = (f32[32,256]{1,0:T(8,128)S(1)}, f32[32,256]{1,0:T(8,128)S(1)}, u32[]{:S(2)}, u32[]{:S(2)}) collective-permute-start(f32[32,256]{1,0:T(8,128)S(1)} %get-tuple-element.16.refs_6_), channel_id=1, source_target_pairs={{0,15},{1,2},{2,1},{3,4},{4,3},{5,6},{6,5},{7,8},{8,7},{9,10},{10,... | collective-permute-start | bytes 98312 | tf_op jit(solution)/shard_map/ppermute | solution.py:365
  9.5 6.0 %collective-permute-start = (f32[32,256]{1,0:T(8,128)S(1)}, f32[32,256]{1,0:T(8,128)S(1)}, u32[]{:S(2)}, u32[]{:S(2)}) collective-permute-start(f32[32,256]{1,0:T(8,128)S(1)} %get-tuple-element.22), channel_id=1, source_target_pairs={{15,0},{0,14},{14,15},{1,2},{2,3},{3,1},{4,5},{5,4},{6,7},{7,6},{8... | collective-permute-start | bytes 98312 | tf_op jit(solution)/shard_map/ppermute | solution.py:365
  15.5 11.2 %copy-start = (bf16[256,256]{1,0:T(8,128)(2,1)S(1)}, bf16[256,256]{1,0:T(8,128)(2,1)}, u32[]{:S(2)}) copy-start(bf16[256,256]{1,0:T(8,128)(2,1)} %constant.32.clone.refs_2_.fwd_l) | copy-start | bytes 393220
  15.5 11.2 %copy-start.1 = (bf16[256,256]{1,0:T(8,128)(2,1)S(1)}, bf16[256,256]{1,0:T(8,128)(2,1)}, u32[]{:S(2)}) copy-start(bf16[256,256]{1,0:T(8,128)(2,1)} %constant.31.clone.refs_1_.fwd_h) | copy-start | bytes 393220
  15.6 11.2 %copy-start.2 = (bf16[128,192]{1,0:T(8,128)(2,1)S(1)}, bf16[128,192]{1,0:T(8,128)(2,1)}, u32[]{:S(2)}) copy-start(bf16[128,192]{1,0:T(8,128)(2,1)} %constant.26.clone.rows_b) | copy-start | bytes 147460
  20.2 1.8 %collective-permute-start.5 = (f32[32,256]{1,0:T(8,128)S(1)}, f32[32,256]{1,0:T(8,128)S(1)}, u32[]{:S(2)}, u32[]{:S(2)}) collective-permute-start(f32[32,256]{1,0:T(8,128)S(1)} %get-tuple-element.28.own), channel_id=1, source_target_pairs={{0,15},{1,0},{2,1},{3,2},{4,3},{5,4},{6,5},{7,6},{8,7},{9,8},{10,9... | collective-permute-start | bytes 98312 | tf_op jit(solution)/shard_map/ppermute | solution.py:365
  20.4 1.6 %collective-permute-start.4 = (f32[32,256]{1,0:T(8,128)S(1)}, f32[32,256]{1,0:T(8,128)S(1)}, u32[]{:S(2)}, u32[]{:S(2)}) collective-permute-start(f32[32,256]{1,0:T(8,128)S(1)} %get-tuple-element.28.own), channel_id=1, source_target_pairs={{0,1},{1,0},{2,3},{3,2},{4,5},{5,4},{6,7},{7,6},{8,9},{9,8},{10,11... | collective-permute-start | bytes 98312 | tf_op jit(solution)/shard_map/ppermute | solution.py:365
  20.7 6.0 %collective-permute-start.3 = (f32[32,256]{1,0:T(8,128)S(1)}, f32[32,256]{1,0:T(8,128)S(1)}, u32[]{:S(2)}, u32[]{:S(2)}) collective-permute-start(f32[32,256]{1,0:T(8,128)S(1)} %get-tuple-element.26.refs_15_), channel_id=1, source_target_pairs={{15,0},{0,1},{1,2},{2,15},{3,4},{4,3},{5,6},{6,5},{7,8},{8,7},{9,1... | collective-permute-start | bytes 98312 | tf_op jit(solution)/shard_map/ppermute | solution.py:365

commit v5 on v4

--- a/solution.py
+++ b/solution.py
@@ -31,6 +31,13 @@
 def stack_left(table):
     high, low = split_table(table)
     return np.concatenate([high, high, low], axis=1)
+
+
+def stack_both(table):
+    high, low = split_table(table)
+    return np.concatenate(
+        [np.concatenate([high, high], axis=1), np.concatenate([low, 0 * low], axis=1)], axis=0
+    )
 
 
 def angles(frequencies, positions, period):
@@ -68,7 +75,10 @@
     project = np.concatenate([first, second], axis=0)
     back_rows = np.concatenate([cos_r, sin_r], axis=0).T
     coarse_r = angles(row_freq, samples_r, window)
-    field_rows = np.concatenate([np.cos(coarse_r), np.sin(coarse_r)], axis=0).T
+    cos_f, sin_f = np.cos(coarse_r).T, np.sin(coarse_r).T
+    field_rows = np.concatenate(
+        [np.concatenate([cos_f, -sin_f], axis=1), np.concatenate([sin_f, cos_f], axis=1)], axis=0
+    )
     coarse_c = angles(col_freq, samples_c, columns)
     cos_c, sin_c = np.cos(coarse_c), np.sin(coarse_c)
     field_cols = np.concatenate(
@@ -81,7 +91,7 @@
         "project": split_table(project),
         "back_rows": stack_left(back_rows),
         "field_rows": stack_left(field_rows),
-        "field_rows_t": stack_left(field_rows.T),
+        "field_rows_t": stack_both(field_rows.T),
         "field_cols": split_table(field_cols),
         "widen_rows": stack_left(widen_rows),
         "widen_rows_t": stack_left(widen_rows.T),
@@ -241,7 +251,7 @@
     wide_r, wide_rt, wide_h, wide_l, resist_hbm, grad_out, fields, resist_out, sem
 ):
     kernels, freq_rows, freq_cols = spectra.shape[1:]
-    rows_c, cols_c = rows_f.shape[0], 2 * freq_cols
+    rows_c, cols_c = rows_f.shape[0] // 2, 2 * freq_cols
     group = math.gcd(kernels, GROUP)
     sign = alternate(own.shape)
     window = own[...] + sign * (far[...] + near[...])
@@ -249,20 +259,20 @@
 
     def forward(step, total):
         start = step * group
-        inners = []
+        prods = []
         for j in range(group):
             kern_re, kern_im = spectra[0, start + j], spectra[1, start + j]
-            prod = jnp.concatenate(
+            prods.append(jnp.concatenate(
                 [kern_re * win_re - kern_im * win_im, kern_re * win_im + kern_im * win_re], axis=1
-            )
-            inners.append(dot(rows_f[...], stack_turned(prod)))
-        inner = jnp.concatenate(inners, axis=0)
-        field = dot3(split(inner), (cols_h[...], cols_l[...]))
-        fields[pl.ds(pl.multiple_of(start * rows_c, rows_c), group * rows_c), :] = field
-        power = field[:, :cols_c] ** 2 + field[:, cols_c:] ** 2
+            ))
+        inner = dot3(split(jnp.concatenate(prods, axis=0)), (cols_h[...], cols_l[...]))
         for j in range(group):
-            share = shares[pl.ds(start + j, 1), :]
-            total = total + share * power[j * rows_c : (j + 1) * rows_c]
+            part = inner[j * freq_rows : (j + 1) * freq_rows]
+            part = jnp.concatenate([part[:, :cols_c], part[:, cols_c:]], axis=0)
+            field = dot(rows_f[...], stack_right(part))
+            fields[start + j] = field
+            power = field[:rows_c] ** 2 + field[rows_c:] ** 2
+            total = total + shares[pl.ds(start + j, 1), :] * power
         return total
 
     total = lax.fori_loop(0, kernels // group, forward, jnp.zeros((rows_c, cols_c), F32))
@@ -275,24 +285,21 @@
     slopes = (4.0 * STEEPNESS) * (resist - target[...].astype(F32)) * resist * (1.0 - resist)
     narrow = dot3_t(split(slopes), (wide_h[...], wide_l[...]))
     weight = dot(wide_rt[...], stack_right(narrow))
-    weight = jnp.concatenate([weight, weight], axis=1)
+    weight = jnp.concatenate([weight, weight], axis=0)
 
     def backward(step, sums):
         grad_re, grad_im = sums
         start = step * group
-        scaled = jnp.concatenate(
-            [
-                weight * fields[pl.ds(pl.multiple_of((start + j) * rows_c, rows_c), rows_c), :]
-                for j in range(group)
-            ],
-            axis=0,
-        )
-        inner = dot3_t(split(scaled), (cols_h[...], cols_l[...]))
+        inners = []
         for j in range(group):
-            spec = dot(rows_t[...], stack_right(inner[j * rows_c : (j + 1) * rows_c]))
-            spec = shares[pl.ds(start + j, 1), :] * spec
-            real = spec[:freq_rows, :freq_cols] + spec[freq_rows:, freq_cols:]
-            imag = spec[:freq_rows, freq_cols:] - spec[freq_rows:, :freq_cols]
+            pieces = jnp.concatenate(split(weight * fields[start + j]), axis=0)
+            part = dot(rows_t[...], pieces)
+            part = part[: 2 * freq_rows] + part[2 * freq_rows :]
+            inners.append(jnp.concatenate([part[:freq_rows], part[freq_rows:]], axis=1))
+        spec = dot3_t(split(jnp.concatenate(inners, axis=0)), (cols_h[...], cols_l[...]))
+        for j in range(group):
+            part = shares[pl.ds(start + j, 1), :] * spec[j * freq_rows : (j + 1) * freq_rows]
+            real, imag = part[:, :freq_cols], part[:, freq_cols:]
             kern_re, kern_im = spectra[0, start + j], spectra[1, start + j]
             grad_re = grad_re + real * kern_re + imag * kern_im
             grad_im = grad_im + imag * kern_re - real * kern_im
@@ -404,7 +411,7 @@
 
     rows_c, cols_c = 2 * freq_rows, 2 * freq_cols
     held = [
-        pltpu.VMEM((kernels * rows_c, 2 * cols_c), F32),
+        pltpu.VMEM((kernels, 2 * rows_c, cols_c), F32),
         pltpu.VMEM(full, F32),
         pltpu.SemaphoreType.DMA,
     ]

time: 28.4 us -> 27.6 us (0.972)
  Pallas kernels: 8.64 us -> 7.83 us
    pallas_call x5, Pallas kernels: 8.64 us -> 7.83 us  [call(): pl.pallas_call(kernel, out_shape=shapes, in_specs=in_specs or [VMEM] * le...]
where the time goes in v5:
time: 27.6 us; the launch traced here: 27.5 us
  waiting for transfers between devices  11.3 us (41%)
  Pallas kernels  7.83 us (28%)
  starting transfers between devices  7.43 us (27%)
  between operations  0.81 us (3%)
    ppermute x6, waiting for transfers between devices, permute(): return lax.ppermute(value, 'tiles', pairs)  11.3 us
    pallas_call x5, Pallas kernels, call(): pl.pallas_call(kernel, out_shape=shapes, in_specs=in_specs or [VMEM] * le...  7.83 us
    ppermute x6, starting transfers between devices, permute(): return lax.ppermute(value, 'tiles', pairs)  7.43 us
  transfers between devices with their start and end apart: 6, of which 4 were waited for; matrix products, arithmetic and copies ran while one was open for 0% of the time, Pallas kernels for 0%

profile of v5, /device:TPU:0, one launch (start us, length us, event | category | flops | bytes accessed | tf_op | source)
XLA Modules:
  0.0 27.5 jit_solution(12729112640833662145)
XLA Ops:
  0.6 2.4 %shard_map.176 = (f32[32,256]{1,0:T(8,128)S(1)}, f32[32,256]{1,0:T(8,128)S(1)}, f32[32,256]{1,0:T(8,128)S(1)}, f32[16,256]{1,0:T(8,128)S(1)}, f32[128,1024]{1,0:T(8,128)S(1)}) custom-call(f32[128,1024]{1,0:T(8,128)} %refs_0_.3, bf16[256,256]{1,0:T(8,128)(2,1)} %constant.31.clone.refs_1_.fwd_h, bf16[256,256]{1,0:T(8,128)(2,1)} %constant.32.clone.refs_2_.fwd_l, ...), custom_call_target="tpu_custom_call" | custom-call | flops 2013265920 | bytes 1491008 | tf_op jit(solution)/shard_map/pallas_call | solution.py:359
  3.0 0.0 copy-start.3
  3.0 0.0 copy-start.4
  3.1 0.0 copy-start.5
  3.1 0.0 copy-start.6
  3.1 0.0 copy-start.7
  3.1 0.0 copy-start.8
  3.1 0.0 copy-start.9
  3.1 0.0 copy-start.10
  3.1 0.0 copy-start.11
  3.1 0.0 copy-start.12
  3.2 0.1 shard_map.177
  3.3 0.6 %collective-permute-start.1 = (f32[32,256]{1,0:T(8,128)S(1)}, f32[32,256]{1,0:T(8,128)S(1)}, u32[]{:S(2)}, u32[]{:S(2)}) collective-permute-start(f32[32,256]{1,0:T(8,128)S(1)} %get-tuple-element.23), channel_id=1, source_target_pairs={{0,1},{1,0},{2,3},{3,2},{4,5},{5,4},{6,7},{7,6},{8,9},{9,8},{10,11... | collective-permute-start | bytes 98312 | tf_op jit(solution)/shard_map/ppermute | solution.py:372
  3.9 5.7 %collective-permute-start.2 = (f32[32,256]{1,0:T(8,128)S(1)}, f32[32,256]{1,0:T(8,128)S(1)}, u32[]{:S(2)}, u32[]{:S(2)}) collective-permute-start(f32[32,256]{1,0:T(8,128)S(1)} %get-tuple-element.16.refs_6_), channel_id=1, source_target_pairs={{0,15},{1,2},{2,1},{3,4},{4,3},{5,6},{6,5},{7,8},{8,7},{9,10},{10,... | collective-permute-start | bytes 98312 | tf_op jit(solution)/shard_map/ppermute | solution.py:372
  9.5 0.5 %collective-permute-start = (f32[32,256]{1,0:T(8,128)S(1)}, f32[32,256]{1,0:T(8,128)S(1)}, u32[]{:S(2)}, u32[]{:S(2)}) collective-permute-start(f32[32,256]{1,0:T(8,128)S(1)} %get-tuple-element.22), channel_id=1, source_target_pairs={{15,0},{0,14},{14,15},{1,2},{2,3},{3,1},{4,5},{5,4},{6,7},{7,6},{8... | collective-permute-start | bytes 98312 | tf_op jit(solution)/shard_map/ppermute | solution.py:372
  10.0 1.1 %collective-permute-done.2.refs_1_ = f32[32,256]{1,0:T(8,128)S(1)} collective-permute-done((f32[32,256]{1,0:T(8,128)S(1)}, f32[32,256]{1,0:T(8,128)S(1)}, u32[]{:S(2)}, u32[]{:S(2)}) %collective-permute-start.2) | collective-permute-done | bytes 32800 | tf_op jit(solution)/shard_map/ppermute | solution.py:372
  11.2 4.3 %collective-permute-done.refs_1_ = f32[32,256]{1,0:T(8,128)S(1)} collective-permute-done((f32[32,256]{1,0:T(8,128)S(1)}, f32[32,256]{1,0:T(8,128)S(1)}, u32[]{:S(2)}, u32[]{:S(2)}) %collective-permute-start) | collective-permute-done | bytes 32800 | tf_op jit(solution)/shard_map/ppermute | solution.py:372
  15.6 3.8 %shard_map.179 = (f32[128,1024]{1,0:T(8,128)}, f32[32,256]{1,0:T(8,128)S(1)}) custom-call(f32[32,256]{1,0:T(8,128)S(1)} %get-tuple-element.21.refs_0_, f32[32,256]{1,0:T(8,128)S(1)} %collective-permute-done.refs_1_, f32[32,256]{1,0:T(8,128)S(1)} %collective-permute-done.1.refs_2_, ...), custom_call_target="tpu_custom_call", output_to_operand_aliasing={{0}: (14, {})} | custom-call | flops 1610612736 | bytes 4063232 | tf_op jit(solution)/shard_map/pallas_call | solution.py:359
  19.4 0.2 collective-permute-start.5
  19.6 0.4 %collective-permute-start.4 = (f32[32,256]{1,0:T(8,128)S(1)}, f32[32,256]{1,0:T(8,128)S(1)}, u32[]{:S(2)}, u32[]{:S(2)}) collective-permute-start(f32[32,256]{1,0:T(8,128)S(1)} %get-tuple-element.28.own), channel_id=1, source_target_pairs={{0,1},{1,0},{2,3},{3,2},{4,5},{5,4},{6,7},{7,6},{8,9},{9,8},{10,11... | collective-permute-start | bytes 98312 | tf_op jit(solution)/shard_map/ppermute | solution.py:372
  19.9 0.1 collective-permute-start.3
  20.1 1.1 %collective-permute-done.5.after = f32[32,256]{1,0:T(8,128)S(1)} collective-permute-done((f32[32,256]{1,0:T(8,128)S(1)}, f32[32,256]{1,0:T(8,128)S(1)}, u32[]{:S(2)}, u32[]{:S(2)}) %collective-permute-start.5) | collective-permute-done | bytes 32800 | tf_op jit(solution)/shard_map/ppermute | solution.py:372
  21.2 4.8 %collective-permute-done.3.before_even = f32[32,256]{1,0:T(8,128)S(1)} collective-permute-done((f32[32,256]{1,0:T(8,128)S(1)}, f32[32,256]{1,0:T(8,128)S(1)}, u32[]{:S(2)}, u32[]{:S(2)}) %collective-permute-start.3) | collective-permute-done | bytes 32800 | tf_op jit(solution)/shard_map/ppermute | solution.py:372
  26.0 1.5 %shard_map.180 = f32[128,1024]{1,0:T(8,128)} custom-call(f32[32,256]{1,0:T(8,128)S(1)} %get-tuple-element.28.own, f32[32,256]{1,0:T(8,128)S(1)} %collective-permute-done.3.before_even, f32[32,256]{1,0:T(8,128)S(1)} %collective-permute-done.4.before_odd, f32[32,256]{1,0:T(8,128)S(1)} %collective-permute-done.5.after, ...), custom_call_target="tpu_custom_call" | custom-call | flops 201326592 | bytes 1490944 | tf_op jit(solution)/shard_map/pallas_call | solution.py:359
  (19 shorter events, 0.1 us)
Async XLA Ops:
  3.0 8.1 %copy-start.3 = (f32[2,16,32,128]{3,2,1,0:T(8,128)S(1)}, f32[2,16,32,128]{3,2,1,0:T(8,128)}, u32[]{:S(2)}) copy-start(f32[2,16,32,128]{3,2,1,0:T(8,128)} %refs_3_.5) | copy-start | bytes 1572868
  3.0 8.1 %copy-start.4 = (s32[128,1024]{1,0:T(8,128)S(1)}, s32[128,1024]{1,0:T(8,128)}, u32[]{:S(2)}) copy-start(s32[128,1024]{1,0:T(8,128)} %refs_5_.7) | copy-start | bytes 1572868
  3.1 8.1 %copy-start.5 = (bf16[256,1024]{1,0:T(8,128)(2,1)S(1)}, bf16[256,1024]{1,0:T(8,128)(2,1)}, u32[]{:S(2)}) copy-start(bf16[256,1024]{1,0:T(8,128)(2,1)} %constant.36.clone.refs_13_) | copy-start | bytes 1572868
  3.1 8.1 %copy-start.6 = (bf16[256,1024]{1,0:T(8,128)(2,1)S(1)}, bf16[256,1024]{1,0:T(8,128)(2,1)}, u32[]{:S(2)}) copy-start(bf16[256,1024]{1,0:T(8,128)(2,1)} %constant.35.clone.refs_12_) | copy-start | bytes 1572868
  3.1 8.1 %copy-start.7 = (bf16[256,512]{1,0:T(8,128)(2,1)S(1)}, bf16[256,512]{1,0:T(8,128)(2,1)}, u32[]{:S(2)}) copy-start(bf16[256,512]{1,0:T(8,128)(2,1)} %constant.28.clone.refs_9_) | copy-start | bytes 786436
  3.1 8.0 %copy-start.8 = (bf16[256,512]{1,0:T(8,128)(2,1)S(1)}, bf16[256,512]{1,0:T(8,128)(2,1)}, u32[]{:S(2)}) copy-start(bf16[256,512]{1,0:T(8,128)(2,1)} %constant.27.clone.refs_8_) | copy-start | bytes 786436
  3.1 8.0 %copy-start.9 = (bf16[128,192]{1,0:T(8,128)(2,1)S(1)}, bf16[128,192]{1,0:T(8,128)(2,1)}, u32[]{:S(2)}) copy-start(bf16[128,192]{1,0:T(8,128)(2,1)} %constant.37.clone.refs_10_) | copy-start | bytes 147460
  3.1 8.0 %copy-start.10 = (bf16[128,256]{1,0:T(8,128)(2,1)S(1)}, bf16[128,256]{1,0:T(8,128)(2,1)}, u32[]{:S(2)}) copy-start(bf16[128,256]{1,0:T(8,128)(2,1)} %constant.30.clone.refs_7_) | copy-start | bytes 196612
  3.1 8.0 %copy-start.11 = (bf16[128,192]{1,0:T(8,128)(2,1)S(1)}, bf16[128,192]{1,0:T(8,128)(2,1)}, u32[]{:S(2)}) copy-start(bf16[128,192]{1,0:T(8,128)(2,1)} %constant.29.clone.refs_6_) | copy-start | bytes 147460
  3.1 8.0 %copy-start.12 = (bf16[64,384]{1,0:T(8,128)(2,1)S(1)}, bf16[64,384]{1,0:T(8,128)(2,1)}, u32[]{:S(2)}) copy-start(bf16[64,384]{1,0:T(8,128)(2,1)} %constant.38.clone.refs_11_) | copy-start | bytes 147460
  3.3 6.7 %collective-permute-start.1 = (f32[32,256]{1,0:T(8,128)S(1)}, f32[32,256]{1,0:T(8,128)S(1)}, u32[]{:S(2)}, u32[]{:S(2)}) collective-permute-start(f32[32,256]{1,0:T(8,128)S(1)} %get-tuple-element.23), channel_id=1, source_target_pairs={{0,1},{1,0},{2,3},{3,2},{4,5},{5,4},{6,7},{7,6},{8,9},{9,8},{10,11... | collective-permute-start | bytes 98312 | tf_op jit(solution)/shard_map/ppermute | solution.py:372
  3.9 7.3 %collective-permute-start.2 = (f32[32,256]{1,0:T(8,128)S(1)}, f32[32,256]{1,0:T(8,128)S(1)}, u32[]{:S(2)}, u32[]{:S(2)}) collective-permute-start(f32[32,256]{1,0:T(8,128)S(1)} %get-tuple-element.16.refs_6_), channel_id=1, source_target_pairs={{0,15},{1,2},{2,1},{3,4},{4,3},{5,6},{6,5},{7,8},{8,7},{9,10},{10,... | collective-permute-start | bytes 98312 | tf_op jit(solution)/shard_map/ppermute | solution.py:372
  9.5 6.1 %collective-permute-start = (f32[32,256]{1,0:T(8,128)S(1)}, f32[32,256]{1,0:T(8,128)S(1)}, u32[]{:S(2)}, u32[]{:S(2)}) collective-permute-start(f32[32,256]{1,0:T(8,128)S(1)} %get-tuple-element.22), channel_id=1, source_target_pairs={{15,0},{0,14},{14,15},{1,2},{2,3},{3,1},{4,5},{5,4},{6,7},{7,6},{8... | collective-permute-start | bytes 98312 | tf_op jit(solution)/shard_map/ppermute | solution.py:372
  15.6 10.4 %copy-start = (bf16[256,256]{1,0:T(8,128)(2,1)S(1)}, bf16[256,256]{1,0:T(8,128)(2,1)}, u32[]{:S(2)}) copy-start(bf16[256,256]{1,0:T(8,128)(2,1)} %constant.32.clone.refs_2_.fwd_l) | copy-start | bytes 393220
  15.6 10.4 %copy-start.1 = (bf16[256,256]{1,0:T(8,128)(2,1)S(1)}, bf16[256,256]{1,0:T(8,128)(2,1)}, u32[]{:S(2)}) copy-start(bf16[256,256]{1,0:T(8,128)(2,1)} %constant.31.clone.refs_1_.fwd_h) | copy-start | bytes 393220
  15.6 10.4 %copy-start.2 = (bf16[128,192]{1,0:T(8,128)(2,1)S(1)}, bf16[128,192]{1,0:T(8,128)(2,1)}, u32[]{:S(2)}) copy-start(bf16[128,192]{1,0:T(8,128)(2,1)} %constant.26.clone.rows_b) | copy-start | bytes 147460
  19.4 1.8 %collective-permute-start.5 = (f32[32,256]{1,0:T(8,128)S(1)}, f32[32,256]{1,0:T(8,128)S(1)}, u32[]{:S(2)}, u32[]{:S(2)}) collective-permute-start(f32[32,256]{1,0:T(8,128)S(1)} %get-tuple-element.28.own), channel_id=1, source_target_pairs={{0,15},{1,0},{2,1},{3,2},{4,3},{5,4},{6,5},{7,6},{8,7},{9,8},{10,9... | collective-permute-start | bytes 98312 | tf_op jit(solution)/shard_map/ppermute | solution.py:372
  19.6 1.6 %collective-permute-start.4 = (f32[32,256]{1,0:T(8,128)S(1)}, f32[32,256]{1,0:T(8,128)S(1)}, u32[]{:S(2)}, u32[]{:S(2)}) collective-permute-start(f32[32,256]{1,0:T(8,128)S(1)} %get-tuple-element.28.own), channel_id=1, source_target_pairs={{0,1},{1,0},{2,3},{3,2},{4,5},{5,4},{6,7},{7,6},{8,9},{9,8},{10,11... | collective-permute-start | bytes 98312 | tf_op jit(solution)/shard_map/ppermute | solution.py:372
  19.9 6.0 %collective-permute-start.3 = (f32[32,256]{1,0:T(8,128)S(1)}, f32[32,256]{1,0:T(8,128)S(1)}, u32[]{:S(2)}, u32[]{:S(2)}) collective-permute-start(f32[32,256]{1,0:T(8,128)S(1)} %get-tuple-element.26.refs_15_), channel_id=1, source_target_pairs={{15,0},{0,1},{1,2},{2,15},{3,4},{4,3},{5,6},{6,5},{7,8},{8,7},{9,1... | collective-permute-start | bytes 98312 | tf_op jit(solution)/shard_map/ppermute | solution.py:372

commit v6 on v5

--- a/solution.py
+++ b/solution.py
@@ -181,10 +181,7 @@
 ):
     mask, fwd_h, fwd_l, proj_h, proj_l, weights, sems = scratch
     columns = quarters(mask)
-    masks = [
-        pltpu.make_async_copy(mask_hbm.at[:, cols], mask.at[:, cols], sems.at[0, i])
-        for i, cols in enumerate(columns)
-    ]
+    masks = [pltpu.make_async_copy(mask_hbm, mask, sems.at[0, 0])]
     tables = [
         pltpu.make_async_copy(fwd_h_hbm, fwd_h, sems.at[1, 0]),
         pltpu.make_async_copy(fwd_l_hbm, fwd_l, sems.at[1, 1]),
@@ -194,11 +191,20 @@
         pltpu.make_async_copy(proj_h_hbm, proj_h, sems.at[2, 0]),
         pltpu.make_async_copy(proj_l_hbm, proj_l, sems.at[2, 1]),
     ]
-    for copy in [masks[0], *tables, *masks[1:], *last]:
+    for copy in [*masks, *tables, *last]:
         copy.start()
     spectra = None
     for i, cols in enumerate(columns):
-        masks[i].wait()
+        if i == 0:
+            last[0].wait()
+            kernels, width = share_out.shape
+            whole = weights[0]
+            for k in range(1, kernels):
+                whole = whole + weights[k]
+            rows = [jnp.full((1, width), weights[k], F32) for k in range(kernels)]
+            share_out[...] = jnp.concatenate(rows, axis=0) / jnp.full((kernels, width), whole, F32)
+        if i == 0:
+            masks[0].wait()
         transmit = jnp.tanh(mask[:, cols])
         slope_out[:, cols] = 1.0 - transmit * transmit
         pieces = split(transmit)
@@ -207,14 +213,8 @@
                 copy.wait()
         term = quarter_turn(dot3(pieces, (fwd_h[...], fwd_l[...])), -i)
         spectra = term if spectra is None else spectra + term
-    for copy in last:
+    for copy in last[1:]:
         copy.wait()
-    kernels, width = share_out.shape
-    whole = weights[0]
-    for k in range(1, kernels):
-        whole = whole + weights[k]
-    rows = [jnp.full((1, width), weights[k], F32) for k in range(kernels)]
-    share_out[...] = jnp.concatenate(rows, axis=0) / jnp.full((kernels, width), whole, F32)
     parts = dot3((proj_h[...], proj_l[...]), split(turn(spectra, -1)))
     half = parts.shape[0] // 2
     return parts[:half], parts[half:]
@@ -329,14 +329,11 @@
         refs[1][...] = grad_in[...]
 
 
-def gradient_kernel(
-    own, before_even, before_odd, after, slope, rows_b, fwd_h, fwd_l, out_hbm, out, sems
-):
+def gradient(own, before, after, slope, rows_b, fwd_h, fwd_l, out_hbm, out, sems):
     half = out.shape[0] // 2
     sign = alternate(own.shape)
-    before = jnp.where(is_odd(), before_odd[...], before_even[...])
     low = stack_turned(own[...] + sign * before)
-    high = stack_turned(own[...] + sign * after[...])
+    high = stack_turned(own[...] + sign * after)
     merged = jnp.concatenate([dot(rows_b[:half], low), dot(rows_b[half:], high)], axis=0)
     sent = []
     for i, cols in enumerate(quarters(out)):
@@ -346,6 +343,19 @@
         sent[-1].start()
     for copy in sent:
         copy.wait()
+
+
+def gradient_first(own, before, after, *refs):
+    @pl.when(is_first())
+    def _():
+        gradient(own, before[...], after[...], *refs)
+
+
+def gradient_second(own, before_even, before_odd, after, slope, rows_b, fwd_h, fwd_l, _, *refs):
+    @pl.when(jnp.logical_not(is_first()))
+    def _():
+        before = jnp.where(is_odd(), before_odd[...], before_even[...])
+        gradient(own, before, after[...], slope, rows_b, fwd_h, fwd_l, *refs)
 
 
 VMEM = pl.BlockSpec(memory_space=pltpu.VMEM)
@@ -385,8 +395,8 @@
     last = count - 1
     ends = [(last, 0), (0, last - 1), (last - 1, last), (1, 2), (2, 3), (3, 1)]
     wrap1_pairs = ends + near_pairs[4 : last - 1]
-    wrap2_pairs = [(last, 0), (0, 1), (1, 2), (2, last)] + far_pairs[3:last]
-    down_pairs = [(i, (i - 1) % count) for i in range(count)]
+    up_pairs = [(i, (i + 1) % count) for i in range(count)]
+    down_pairs = [(j, i) for i, j in up_pairs]
     pair, full, wide = (freq_rows, 2 * freq_cols), (strip_rows, columns), (kernels, 2 * freq_cols)
     area = strip_rows * columns
 
@@ -426,23 +436,25 @@
         image_first, [full, pair], [own, far, near, *rest], work, held,
         in_specs=specs, out_specs=[HBM, VMEM],
     )
-    grad_before_even = permute(grad, wrap2_pairs)
+    grad_after_first = permute(grad, near_pairs)
+    grad_before_even = permute(grad, up_pairs)
     resist, grad = call(
         image_second, [full, pair], [own, far_first, near, *rest, resist, grad], work, held,
         in_specs=specs + [HBM, VMEM], out_specs=[HBM, VMEM], aliases={14: 0},
     )
     grad_after = permute(grad, down_pairs)
     grad_before_odd = permute(grad, near_pairs)
+    rest = [slope, tables["back_rows"], *tables["forward"]]
+    held = [pltpu.VMEM(full, F32), pltpu.SemaphoreType.DMA((QUARTERS,))]
+    work = 6 * area * 2 * freq_cols
     (gradient,) = call(
-        gradient_kernel,
-        [full],
-        [
-            grad, grad_before_even, grad_before_odd, grad_after, slope,
-            tables["back_rows"], *tables["forward"],
-        ],
-        6 * area * 2 * freq_cols,
-        [pltpu.VMEM(full, F32), pltpu.SemaphoreType.DMA((QUARTERS,))],
+        gradient_first, [full], [grad, grad_before_even, grad_after_first, *rest], work, held,
         out_specs=[HBM],
+    )
+    (gradient,) = call(
+        gradient_second, [full],
+        [grad, grad_before_even, grad_before_odd, grad_after, *rest, gradient], work, held,
+        in_specs=[VMEM] * 8 + [HBM], out_specs=[HBM], aliases={8: 0},
     )
     return (resist, gradient)
 

time: 27.6 us -> 22.4 us (0.81)
  waiting for transfers between devices: 11.3 us -> 5.74 us
  starting transfers between devices: 7.43 us -> 8.21 us
  Pallas kernels: 7.83 us -> 7.36 us
    ppermute x6 -> x7, waiting for transfers between devices: 11.3 us -> 5.74 us  [permute(): return lax.ppermute(value, 'tiles', pairs)]
    ppermute x6 -> x7, starting transfers between devices: 7.43 us -> 8.21 us  [permute(): return lax.ppermute(value, 'tiles', pairs)]
    pallas_call x5 -> x6, Pallas kernels: 7.83 us -> 7.36 us  [call(): pl.pallas_call(kernel, out_shape=shapes, in_specs=in_specs or [VMEM] * le...]
  transfers between devices with their start and end apart: 6 -> 7, of which waited for: 4 -> 3; matrix products, arithmetic and copies ran while one was open for 0% -> 0% of each run, Pallas kernels for 0% -> 24%
where the time goes in v6:
time: 22.4 us; the launch traced here: 22.2 us
  starting transfers between devices  8.21 us (37%)
  Pallas kernels  7.36 us (33%)
  waiting for transfers between devices  5.74 us (26%)
  between operations  0.83 us (4%)
    ppermute x7, starting transfers between devices, permute(): return lax.ppermute(value, 'tiles', pairs)  8.21 us
    pallas_call x6, Pallas kernels, call(): pl.pallas_call(kernel, out_shape=shapes, in_specs=in_specs or [VMEM] * le...  7.36 us
    ppermute x7, waiting for transfers between devices, permute(): return lax.ppermute(value, 'tiles', pairs)  5.74 us
  transfers between devices with their start and end apart: 7, of which 3 were waited for; matrix products, arithmetic and copies ran while one was open for 0% of the time, Pallas kernels for 24%

profile of v6, /device:TPU:0, one launch (start us, length us, event | category | flops | bytes accessed | tf_op | source)
XLA Modules:
  0.0 22.2 jit_solution(10228972708957493452)
XLA Ops:
  0.6 1.9 %shard_map.176 = (f32[32,256]{1,0:T(8,128)S(1)}, f32[32,256]{1,0:T(8,128)S(1)}, f32[32,256]{1,0:T(8,128)S(1)}, f32[16,256]{1,0:T(8,128)S(1)}, f32[128,1024]{1,0:T(8,128)S(1)}) custom-call(f32[128,1024]{1,0:T(8,128)} %refs_0_.3, bf16[256,256]{1,0:T(8,128)(2,1)} %constant.31.clone.refs_1_.refs_2_.fwd_h, bf16[256,256]{1,0:T(8,128)(2,1)} %constant.32.clone.refs_2_.refs_3_.fwd_l, ...), custom_call_target="tpu_custom_call" | custom-call | flops 2013265920 | bytes 1491008 | tf_op jit(solution)/shard_map/pallas_call | solution.py:369
  2.5 0.0 copy-start.3
  2.5 0.0 copy-start.5
  2.6 0.0 copy-start.6
  2.6 0.0 copy-start.7
  2.6 0.0 copy-start.8
  2.6 0.0 copy-start.9
  2.6 0.0 copy-start.10
  2.6 0.0 copy-start.11
  2.6 0.0 copy-start.12
  2.6 0.1 shard_map.177
  2.8 0.6 %collective-permute-start.1 = (f32[32,256]{1,0:T(8,128)S(1)}, f32[32,256]{1,0:T(8,128)S(1)}, u32[]{:S(2)}, u32[]{:S(2)}) collective-permute-start(f32[32,256]{1,0:T(8,128)S(1)} %get-tuple-element.23), channel_id=1, source_target_pairs={{0,1},{1,0},{2,3},{3,2},{4,5},{5,4},{6,7},{7,6},{8,9},{9,8},{10,11... | collective-permute-start | bytes 98312 | tf_op jit(solution)/shard_map/ppermute | solution.py:382
  3.3 5.7 %collective-permute-start.2 = (f32[32,256]{1,0:T(8,128)S(1)}, f32[32,256]{1,0:T(8,128)S(1)}, u32[]{:S(2)}, u32[]{:S(2)}) collective-permute-start(f32[32,256]{1,0:T(8,128)S(1)} %get-tuple-element.16.refs_6_), channel_id=1, source_target_pairs={{0,15},{1,2},{2,1},{3,4},{4,3},{5,6},{6,5},{7,8},{8,7},{9,10},{10,... | collective-permute-start | bytes 98312 | tf_op jit(solution)/shard_map/ppermute | solution.py:382
  9.0 0.5 %collective-permute-start = (f32[32,256]{1,0:T(8,128)S(1)}, f32[32,256]{1,0:T(8,128)S(1)}, u32[]{:S(2)}, u32[]{:S(2)}) collective-permute-start(f32[32,256]{1,0:T(8,128)S(1)} %get-tuple-element.22), channel_id=1, source_target_pairs={{15,0},{0,14},{14,15},{1,2},{2,3},{3,1},{4,5},{5,4},{6,7},{7,6},{8... | collective-permute-start | bytes 98312 | tf_op jit(solution)/shard_map/ppermute | solution.py:382
  9.5 1.1 %collective-permute-done.2.refs_1_ = f32[32,256]{1,0:T(8,128)S(1)} collective-permute-done((f32[32,256]{1,0:T(8,128)S(1)}, f32[32,256]{1,0:T(8,128)S(1)}, u32[]{:S(2)}, u32[]{:S(2)}) %collective-permute-start.2) | collective-permute-done | bytes 32800 | tf_op jit(solution)/shard_map/ppermute | solution.py:382
  10.7 0.9 %collective-permute-start.6 = (f32[32,256]{1,0:T(8,128)S(1)}, f32[32,256]{1,0:T(8,128)S(1)}, u32[]{:S(2)}, u32[]{:S(2)}) collective-permute-start(f32[32,256]{1,0:T(8,128)S(1)} %get-tuple-element.26.refs_15_), channel_id=1, source_target_pairs={{0,1},{1,0},{2,3},{3,2},{4,5},{5,4},{6,7},{7,6},{8,9},{9,8},{10,11... | collective-permute-start | bytes 98312 | tf_op jit(solution)/shard_map/ppermute | solution.py:382
  11.6 0.1 collective-permute-start.3
  11.6 3.4 %collective-permute-done.refs_1_ = f32[32,256]{1,0:T(8,128)S(1)} collective-permute-done((f32[32,256]{1,0:T(8,128)S(1)}, f32[32,256]{1,0:T(8,128)S(1)}, u32[]{:S(2)}, u32[]{:S(2)}) %collective-permute-start) | collective-permute-done | bytes 32800 | tf_op jit(solution)/shard_map/ppermute | solution.py:382
  15.0 3.8 %shard_map.179 = (f32[128,1024]{1,0:T(8,128)}, f32[32,256]{1,0:T(8,128)S(1)}) custom-call(f32[32,256]{1,0:T(8,128)S(1)} %get-tuple-element.21.refs_0_, f32[32,256]{1,0:T(8,128)S(1)} %collective-permute-done.refs_1_, f32[32,256]{1,0:T(8,128)S(1)} %collective-permute-done.1.refs_2_, ...), custom_call_target="tpu_custom_call", output_to_operand_aliasing={{0}: (14, {})} | custom-call | flops 1610612736 | bytes 4063232 | tf_op jit(solution)/shard_map/pallas_call | solution.py:369
  18.8 0.4 %collective-permute-start.5 = (f32[32,256]{1,0:T(8,128)S(1)}, f32[32,256]{1,0:T(8,128)S(1)}, u32[]{:S(2)}, u32[]{:S(2)}) collective-permute-start(f32[32,256]{1,0:T(8,128)S(1)} %get-tuple-element.28.own), channel_id=1, source_target_pairs={{1,0},{2,1},{3,2},{4,3},{5,4},{6,5},{7,6},{8,7},{9,8},{10,9},{11,1... | collective-permute-start | bytes 98312 | tf_op jit(solution)/shard_map/ppermute | solution.py:382
  19.2 0.2 collective-permute-start.4
  19.4 1.2 %collective-permute-done.3.before.before_even = f32[32,256]{1,0:T(8,128)S(1)} collective-permute-done((f32[32,256]{1,0:T(8,128)S(1)}, f32[32,256]{1,0:T(8,128)S(1)}, u32[]{:S(2)}, u32[]{:S(2)}) %collective-permute-start.3) | collective-permute-done | bytes 32800 | tf_op jit(solution)/shard_map/ppermute | solution.py:382
  20.6 1.5 %shard_map.180._ = f32[128,1024]{1,0:T(8,128)} custom-call(f32[32,256]{1,0:T(8,128)S(1)} %get-tuple-element.28.own, f32[32,256]{1,0:T(8,128)S(1)} %collective-permute-done.3.before.before_even, f32[32,256]{1,0:T(8,128)S(1)} %collective-permute-done.6.after, f32[128,1024]{1,0:T(8,128)S(1)} %get-tuple-element.29.refs_0_.slope, bf16[128,192]{1,0:T(8,128)(2,1)S(1)} %copy-done.2, ...), custom_call_target="tpu_custom_call" | custom-call | flops 201326592 | bytes 1458176 | tf_op jit(solution)/shard_map/pallas_call | solution.py:369
  22.2 0.1 shard_map.181
  (22 shorter events, 0.1 us)
Async XLA Ops:
  2.5 8.1 %copy-start.3 = (f32[2,16,32,128]{3,2,1,0:T(8,128)S(1)}, f32[2,16,32,128]{3,2,1,0:T(8,128)}, u32[]{:S(2)}) copy-start(f32[2,16,32,128]{3,2,1,0:T(8,128)} %refs_3_.6) | copy-start | bytes 1572868
  2.5 8.1 %copy-start.4 = (s32[128,1024]{1,0:T(8,128)S(1)}, s32[128,1024]{1,0:T(8,128)}, u32[]{:S(2)}) copy-start(s32[128,1024]{1,0:T(8,128)} %refs_5_.7) | copy-start | bytes 1572868
  2.5 8.1 %copy-start.5 = (bf16[256,1024]{1,0:T(8,128)(2,1)S(1)}, bf16[256,1024]{1,0:T(8,128)(2,1)}, u32[]{:S(2)}) copy-start(bf16[256,1024]{1,0:T(8,128)(2,1)} %constant.36.clone.refs_13_) | copy-start | bytes 1572868
  2.6 8.1 %copy-start.6 = (bf16[256,1024]{1,0:T(8,128)(2,1)S(1)}, bf16[256,1024]{1,0:T(8,128)(2,1)}, u32[]{:S(2)}) copy-start(bf16[256,1024]{1,0:T(8,128)(2,1)} %constant.35.clone.refs_12_) | copy-start | bytes 1572868
  2.6 8.1 %copy-start.7 = (bf16[256,512]{1,0:T(8,128)(2,1)S(1)}, bf16[256,512]{1,0:T(8,128)(2,1)}, u32[]{:S(2)}) copy-start(bf16[256,512]{1,0:T(8,128)(2,1)} %constant.28.clone.refs_9_) | copy-start | bytes 786436
  2.6 8.0 %copy-start.8 = (bf16[256,512]{1,0:T(8,128)(2,1)S(1)}, bf16[256,512]{1,0:T(8,128)(2,1)}, u32[]{:S(2)}) copy-start(bf16[256,512]{1,0:T(8,128)(2,1)} %constant.27.clone.refs_8_) | copy-start | bytes 786436
  2.6 8.0 %copy-start.9 = (bf16[128,192]{1,0:T(8,128)(2,1)S(1)}, bf16[128,192]{1,0:T(8,128)(2,1)}, u32[]{:S(2)}) copy-start(bf16[128,192]{1,0:T(8,128)(2,1)} %constant.37.clone.refs_10_) | copy-start | bytes 147460
  2.6 8.0 %copy-start.10 = (bf16[128,256]{1,0:T(8,128)(2,1)S(1)}, bf16[128,256]{1,0:T(8,128)(2,1)}, u32[]{:S(2)}) copy-start(bf16[128,256]{1,0:T(8,128)(2,1)} %constant.30.clone.refs_7_) | copy-start | bytes 196612
  2.6 8.0 %copy-start.11 = (bf16[128,192]{1,0:T(8,128)(2,1)S(1)}, bf16[128,192]{1,0:T(8,128)(2,1)}, u32[]{:S(2)}) copy-start(bf16[128,192]{1,0:T(8,128)(2,1)} %constant.29.clone.refs_6_) | copy-start | bytes 147460
  2.6 8.0 %copy-start.12 = (bf16[64,384]{1,0:T(8,128)(2,1)S(1)}, bf16[64,384]{1,0:T(8,128)(2,1)}, u32[]{:S(2)}) copy-start(bf16[64,384]{1,0:T(8,128)(2,1)} %constant.38.clone.refs_11_) | copy-start | bytes 147460
  2.8 6.7 %collective-permute-start.1 = (f32[32,256]{1,0:T(8,128)S(1)}, f32[32,256]{1,0:T(8,128)S(1)}, u32[]{:S(2)}, u32[]{:S(2)}) collective-permute-start(f32[32,256]{1,0:T(8,128)S(1)} %get-tuple-element.23), channel_id=1, source_target_pairs={{0,1},{1,0},{2,3},{3,2},{4,5},{5,4},{6,7},{7,6},{8,9},{9,8},{10,11... | collective-permute-start | bytes 98312 | tf_op jit(solution)/shard_map/ppermute | solution.py:382
  3.3 7.3 %collective-permute-start.2 = (f32[32,256]{1,0:T(8,128)S(1)}, f32[32,256]{1,0:T(8,128)S(1)}, u32[]{:S(2)}, u32[]{:S(2)}) collective-permute-start(f32[32,256]{1,0:T(8,128)S(1)} %get-tuple-element.16.refs_6_), channel_id=1, source_target_pairs={{0,15},{1,2},{2,1},{3,4},{4,3},{5,6},{6,5},{7,8},{8,7},{9,10},{10,... | collective-permute-start | bytes 98312 | tf_op jit(solution)/shard_map/ppermute | solution.py:382
  9.0 6.0 %collective-permute-start = (f32[32,256]{1,0:T(8,128)S(1)}, f32[32,256]{1,0:T(8,128)S(1)}, u32[]{:S(2)}, u32[]{:S(2)}) collective-permute-start(f32[32,256]{1,0:T(8,128)S(1)} %get-tuple-element.22), channel_id=1, source_target_pairs={{15,0},{0,14},{14,15},{1,2},{2,3},{3,1},{4,5},{5,4},{6,7},{7,6},{8... | collective-permute-start | bytes 98312 | tf_op jit(solution)/shard_map/ppermute | solution.py:382
  10.7 8.7 %collective-permute-start.6 = (f32[32,256]{1,0:T(8,128)S(1)}, f32[32,256]{1,0:T(8,128)S(1)}, u32[]{:S(2)}, u32[]{:S(2)}) collective-permute-start(f32[32,256]{1,0:T(8,128)S(1)} %get-tuple-element.26.refs_15_), channel_id=1, source_target_pairs={{0,1},{1,0},{2,3},{3,2},{4,5},{5,4},{6,7},{7,6},{8,9},{9,8},{10,11... | collective-permute-start | bytes 98312 | tf_op jit(solution)/shard_map/ppermute | solution.py:382
  11.6 9.1 %collective-permute-start.3 = (f32[32,256]{1,0:T(8,128)S(1)}, f32[32,256]{1,0:T(8,128)S(1)}, u32[]{:S(2)}, u32[]{:S(2)}) collective-permute-start(f32[32,256]{1,0:T(8,128)S(1)} %get-tuple-element.26.refs_15_), channel_id=1, source_target_pairs={{0,1},{1,2},{2,3},{3,4},{4,5},{5,6},{6,7},{7,8},{8,9},{9,10},{10,1... | collective-permute-start | bytes 98312 | tf_op jit(solution)/shard_map/ppermute | solution.py:382
  15.0 5.6 %copy-start = (bf16[256,256]{1,0:T(8,128)(2,1)S(1)}, bf16[256,256]{1,0:T(8,128)(2,1)}, u32[]{:S(2)}) copy-start(bf16[256,256]{1,0:T(8,128)(2,1)} %constant.32.clone.refs_2_.refs_3_.fwd_l) | copy-start | bytes 393220
  15.0 5.6 %copy-start.1 = (bf16[256,256]{1,0:T(8,128)(2,1)S(1)}, bf16[256,256]{1,0:T(8,128)(2,1)}, u32[]{:S(2)}) copy-start(bf16[256,256]{1,0:T(8,128)(2,1)} %constant.31.clone.refs_1_.refs_2_.fwd_h) | copy-start | bytes 393220
  15.0 5.6 %copy-start.2 = (bf16[128,192]{1,0:T(8,128)(2,1)S(1)}, bf16[128,192]{1,0:T(8,128)(2,1)}, u32[]{:S(2)}) copy-start(bf16[128,192]{1,0:T(8,128)(2,1)} %constant.26.clone.refs_1_.rows_b) | copy-start | bytes 147460
  18.8 3.3 %collective-permute-start.5 = (f32[32,256]{1,0:T(8,128)S(1)}, f32[32,256]{1,0:T(8,128)S(1)}, u32[]{:S(2)}, u32[]{:S(2)}) collective-permute-start(f32[32,256]{1,0:T(8,128)S(1)} %get-tuple-element.28.own), channel_id=1, source_target_pairs={{1,0},{2,1},{3,2},{4,3},{5,4},{6,5},{7,6},{8,7},{9,8},{10,9},{11,1... | collective-permute-start | bytes 98312 | tf_op jit(solution)/shard_map/ppermute | solution.py:382
  19.2 3.0 %collective-permute-start.4 = (f32[32,256]{1,0:T(8,128)S(1)}, f32[32,256]{1,0:T(8,128)S(1)}, u32[]{:S(2)}, u32[]{:S(2)}) collective-permute-start(f32[32,256]{1,0:T(8,128)S(1)} %get-tuple-element.28.own), channel_id=1, source_target_pairs={{0,1},{1,0},{2,3},{3,2},{4,5},{5,4},{6,7},{7,6},{8,9},{9,8},{10,11... | collective-permute-start | bytes 98312 | tf_op jit(solution)/shard_map/ppermute | solution.py:382

commit v7 on v6

--- a/solution.py
+++ b/solution.py
@@ -335,14 +335,15 @@
     low = stack_turned(own[...] + sign * before)
     high = stack_turned(own[...] + sign * after)
     merged = jnp.concatenate([dot(rows_b[:half], low), dot(rows_b[half:], high)], axis=0)
-    sent = []
+    parts = [quarter_turn(merged, i) for i in range(QUARTERS)]
+    pieces = split(jnp.concatenate(parts, axis=0))
+    terms = dot3_t(pieces, (fwd_h[...], fwd_l[...]))
+    rows = out.shape[0]
     for i, cols in enumerate(quarters(out)):
-        pieces = split(quarter_turn(merged, i))
-        out[:, cols] = slope[:, cols] * dot3_t(pieces, (fwd_h[...], fwd_l[...]))
-        sent.append(pltpu.make_async_copy(out.at[:, cols], out_hbm.at[:, cols], sems.at[i]))
-        sent[-1].start()
-    for copy in sent:
-        copy.wait()
+        out[:, cols] = slope[:, cols] * terms[i * rows : (i + 1) * rows]
+    sent = pltpu.make_async_copy(out, out_hbm, sems.at[0])
+    sent.start()
+    sent.wait()
 
 
 def gradient_first(own, before, after, *refs):

time: 22.4 us -> 22.2 us (level)
  transfers between devices with their start and end apart: 7 -> 7, of which waited for: 3 -> 3; matrix products, arithmetic and copies ran while one was open for 0% -> 0% of each run, Pallas kernels for 24% -> 23%
where the time goes in v7:
time: 22.2 us; the launch traced here: 22.1 us
  starting transfers between devices  8.21 us (37%)
  Pallas kernels  7.22 us (33%)
  waiting for transfers between devices  5.74 us (26%)
  between operations  0.83 us (4%)
    ppermute x7, starting transfers between devices, permute(): return lax.ppermute(value, 'tiles', pairs)  8.21 us
    pallas_call x6, Pallas kernels, call(): pl.pallas_call(kernel, out_shape=shapes, in_specs=in_specs or [VMEM] * le...  7.22 us
    ppermute x7, waiting for transfers between devices, permute(): return lax.ppermute(value, 'tiles', pairs)  5.74 us
  transfers between devices with their start and end apart: 7, of which 3 were waited for; matrix products, arithmetic and copies ran while one was open for 0% of the time, Pallas kernels for 23%

profile of v7, /device:TPU:0, one launch (start us, length us, event | category | flops | bytes accessed | tf_op | source)
XLA Modules:
  0.0 22.1 jit_solution(15134716953967880869)
XLA Ops:
  0.6 1.9 %shard_map.176 = (f32[32,256]{1,0:T(8,128)S(1)}, f32[32,256]{1,0:T(8,128)S(1)}, f32[32,256]{1,0:T(8,128)S(1)}, f32[16,256]{1,0:T(8,128)S(1)}, f32[128,1024]{1,0:T(8,128)S(1)}) custom-call(f32[128,1024]{1,0:T(8,128)} %refs_0_.3, bf16[256,256]{1,0:T(8,128)(2,1)} %constant.31.clone.refs_1_.refs_2_.fwd_h, bf16[256,256]{1,0:T(8,128)(2,1)} %constant.32.clone.refs_2_.refs_3_.fwd_l, ...), custom_call_target="tpu_custom_call" | custom-call | flops 2013265920 | bytes 1491008 | tf_op jit(solution)/shard_map/pallas_call | solution.py:370
  2.5 0.0 copy-start.3
  2.5 0.0 copy-start.5
  2.6 0.0 copy-start.6
  2.6 0.0 copy-start.7
  2.6 0.0 copy-start.8
  2.6 0.0 copy-start.9
  2.6 0.0 copy-start.10
  2.6 0.0 copy-start.11
  2.6 0.0 copy-start.12
  2.6 0.1 shard_map.177
  2.8 0.6 %collective-permute-start.1 = (f32[32,256]{1,0:T(8,128)S(1)}, f32[32,256]{1,0:T(8,128)S(1)}, u32[]{:S(2)}, u32[]{:S(2)}) collective-permute-start(f32[32,256]{1,0:T(8,128)S(1)} %get-tuple-element.23), channel_id=1, source_target_pairs={{0,1},{1,0},{2,3},{3,2},{4,5},{5,4},{6,7},{7,6},{8,9},{9,8},{10,11... | collective-permute-start | bytes 98312 | tf_op jit(solution)/shard_map/ppermute | solution.py:383
  3.3 5.7 %collective-permute-start.2 = (f32[32,256]{1,0:T(8,128)S(1)}, f32[32,256]{1,0:T(8,128)S(1)}, u32[]{:S(2)}, u32[]{:S(2)}) collective-permute-start(f32[32,256]{1,0:T(8,128)S(1)} %get-tuple-element.16.refs_6_), channel_id=1, source_target_pairs={{0,15},{1,2},{2,1},{3,4},{4,3},{5,6},{6,5},{7,8},{8,7},{9,10},{10,... | collective-permute-start | bytes 98312 | tf_op jit(solution)/shard_map/ppermute | solution.py:383
  9.0 0.5 %collective-permute-start = (f32[32,256]{1,0:T(8,128)S(1)}, f32[32,256]{1,0:T(8,128)S(1)}, u32[]{:S(2)}, u32[]{:S(2)}) collective-permute-start(f32[32,256]{1,0:T(8,128)S(1)} %get-tuple-element.22), channel_id=1, source_target_pairs={{15,0},{0,14},{14,15},{1,2},{2,3},{3,1},{4,5},{5,4},{6,7},{7,6},{8... | collective-permute-start | bytes 98312 | tf_op jit(solution)/shard_map/ppermute | solution.py:383
  9.5 1.1 %collective-permute-done.2.refs_1_ = f32[32,256]{1,0:T(8,128)S(1)} collective-permute-done((f32[32,256]{1,0:T(8,128)S(1)}, f32[32,256]{1,0:T(8,128)S(1)}, u32[]{:S(2)}, u32[]{:S(2)}) %collective-permute-start.2) | collective-permute-done | bytes 32800 | tf_op jit(solution)/shard_map/ppermute | solution.py:383
  10.7 0.9 %collective-permute-start.6 = (f32[32,256]{1,0:T(8,128)S(1)}, f32[32,256]{1,0:T(8,128)S(1)}, u32[]{:S(2)}, u32[]{:S(2)}) collective-permute-start(f32[32,256]{1,0:T(8,128)S(1)} %get-tuple-element.26.refs_15_), channel_id=1, source_target_pairs={{0,1},{1,0},{2,3},{3,2},{4,5},{5,4},{6,7},{7,6},{8,9},{9,8},{10,11... | collective-permute-start | bytes 98312 | tf_op jit(solution)/shard_map/ppermute | solution.py:383
  11.6 0.1 collective-permute-start.3
  11.6 3.4 %collective-permute-done.refs_1_ = f32[32,256]{1,0:T(8,128)S(1)} collective-permute-done((f32[32,256]{1,0:T(8,128)S(1)}, f32[32,256]{1,0:T(8,128)S(1)}, u32[]{:S(2)}, u32[]{:S(2)}) %collective-permute-start) | collective-permute-done | bytes 32800 | tf_op jit(solution)/shard_map/ppermute | solution.py:383
  15.0 3.8 %shard_map.179 = (f32[128,1024]{1,0:T(8,128)}, f32[32,256]{1,0:T(8,128)S(1)}) custom-call(f32[32,256]{1,0:T(8,128)S(1)} %get-tuple-element.21.refs_0_, f32[32,256]{1,0:T(8,128)S(1)} %collective-permute-done.refs_1_, f32[32,256]{1,0:T(8,128)S(1)} %collective-permute-done.1.refs_2_, ...), custom_call_target="tpu_custom_call", output_to_operand_aliasing={{0}: (14, {})} | custom-call | flops 1610612736 | bytes 4063232 | tf_op jit(solution)/shard_map/pallas_call | solution.py:370
  18.8 0.4 %collective-permute-start.5 = (f32[32,256]{1,0:T(8,128)S(1)}, f32[32,256]{1,0:T(8,128)S(1)}, u32[]{:S(2)}, u32[]{:S(2)}) collective-permute-start(f32[32,256]{1,0:T(8,128)S(1)} %get-tuple-element.28.own), channel_id=1, source_target_pairs={{1,0},{2,1},{3,2},{4,3},{5,4},{6,5},{7,6},{8,7},{9,8},{10,9},{11,1... | collective-permute-start | bytes 98312 | tf_op jit(solution)/shard_map/ppermute | solution.py:383
  19.2 0.2 collective-permute-start.4
  19.4 1.2 %collective-permute-done.3.before.before_even = f32[32,256]{1,0:T(8,128)S(1)} collective-permute-done((f32[32,256]{1,0:T(8,128)S(1)}, f32[32,256]{1,0:T(8,128)S(1)}, u32[]{:S(2)}, u32[]{:S(2)}) %collective-permute-start.3) | collective-permute-done | bytes 32800 | tf_op jit(solution)/shard_map/ppermute | solution.py:383
  20.6 1.3 %shard_map.180._ = f32[128,1024]{1,0:T(8,128)} custom-call(f32[32,256]{1,0:T(8,128)S(1)} %get-tuple-element.28.own, f32[32,256]{1,0:T(8,128)S(1)} %collective-permute-done.3.before.before_even, f32[32,256]{1,0:T(8,128)S(1)} %collective-permute-done.6.after, f32[128,1024]{1,0:T(8,128)S(1)} %get-tuple-element.29.refs_0_.slope, bf16[128,192]{1,0:T(8,128)(2,1)S(1)} %copy-done.2, ...), custom_call_target="tpu_custom_call" | custom-call | flops 201326592 | bytes 1458176 | tf_op jit(solution)/shard_map/pallas_call | solution.py:370
  22.0 0.1 shard_map.181
  (22 shorter events, 0.1 us)
Async XLA Ops:
  2.5 8.1 %copy-start.3 = (f32[2,16,32,128]{3,2,1,0:T(8,128)S(1)}, f32[2,16,32,128]{3,2,1,0:T(8,128)}, u32[]{:S(2)}) copy-start(f32[2,16,32,128]{3,2,1,0:T(8,128)} %refs_3_.6) | copy-start | bytes 1572868
  2.5 8.1 %copy-start.4 = (s32[128,1024]{1,0:T(8,128)S(1)}, s32[128,1024]{1,0:T(8,128)}, u32[]{:S(2)}) copy-start(s32[128,1024]{1,0:T(8,128)} %refs_5_.7) | copy-start | bytes 1572868
  2.5 8.1 %copy-start.5 = (bf16[256,1024]{1,0:T(8,128)(2,1)S(1)}, bf16[256,1024]{1,0:T(8,128)(2,1)}, u32[]{:S(2)}) copy-start(bf16[256,1024]{1,0:T(8,128)(2,1)} %constant.36.clone.refs_13_) | copy-start | bytes 1572868
  2.6 8.1 %copy-start.6 = (bf16[256,1024]{1,0:T(8,128)(2,1)S(1)}, bf16[256,1024]{1,0:T(8,128)(2,1)}, u32[]{:S(2)}) copy-start(bf16[256,1024]{1,0:T(8,128)(2,1)} %constant.35.clone.refs_12_) | copy-start | bytes 1572868
  2.6 8.1 %copy-start.7 = (bf16[256,512]{1,0:T(8,128)(2,1)S(1)}, bf16[256,512]{1,0:T(8,128)(2,1)}, u32[]{:S(2)}) copy-start(bf16[256,512]{1,0:T(8,128)(2,1)} %constant.28.clone.refs_9_) | copy-start | bytes 786436
  2.6 8.0 %copy-start.8 = (bf16[256,512]{1,0:T(8,128)(2,1)S(1)}, bf16[256,512]{1,0:T(8,128)(2,1)}, u32[]{:S(2)}) copy-start(bf16[256,512]{1,0:T(8,128)(2,1)} %constant.27.clone.refs_8_) | copy-start | bytes 786436
  2.6 8.0 %copy-start.9 = (bf16[128,192]{1,0:T(8,128)(2,1)S(1)}, bf16[128,192]{1,0:T(8,128)(2,1)}, u32[]{:S(2)}) copy-start(bf16[128,192]{1,0:T(8,128)(2,1)} %constant.37.clone.refs_10_) | copy-start | bytes 147460
  2.6 8.0 %copy-start.10 = (bf16[128,256]{1,0:T(8,128)(2,1)S(1)}, bf16[128,256]{1,0:T(8,128)(2,1)}, u32[]{:S(2)}) copy-start(bf16[128,256]{1,0:T(8,128)(2,1)} %constant.30.clone.refs_7_) | copy-start | bytes 196612
  2.6 8.0 %copy-start.11 = (bf16[128,192]{1,0:T(8,128)(2,1)S(1)}, bf16[128,192]{1,0:T(8,128)(2,1)}, u32[]{:S(2)}) copy-start(bf16[128,192]{1,0:T(8,128)(2,1)} %constant.29.clone.refs_6_) | copy-start | bytes 147460
  2.6 8.0 %copy-start.12 = (bf16[64,384]{1,0:T(8,128)(2,1)S(1)}, bf16[64,384]{1,0:T(8,128)(2,1)}, u32[]{:S(2)}) copy-start(bf16[64,384]{1,0:T(8,128)(2,1)} %constant.38.clone.refs_11_) | copy-start | bytes 147460
  2.8 6.7 %collective-permute-start.1 = (f32[32,256]{1,0:T(8,128)S(1)}, f32[32,256]{1,0:T(8,128)S(1)}, u32[]{:S(2)}, u32[]{:S(2)}) collective-permute-start(f32[32,256]{1,0:T(8,128)S(1)} %get-tuple-element.23), channel_id=1, source_target_pairs={{0,1},{1,0},{2,3},{3,2},{4,5},{5,4},{6,7},{7,6},{8,9},{9,8},{10,11... | collective-permute-start | bytes 98312 | tf_op jit(solution)/shard_map/ppermute | solution.py:383
  3.3 7.3 %collective-permute-start.2 = (f32[32,256]{1,0:T(8,128)S(1)}, f32[32,256]{1,0:T(8,128)S(1)}, u32[]{:S(2)}, u32[]{:S(2)}) collective-permute-start(f32[32,256]{1,0:T(8,128)S(1)} %get-tuple-element.16.refs_6_), channel_id=1, source_target_pairs={{0,15},{1,2},{2,1},{3,4},{4,3},{5,6},{6,5},{7,8},{8,7},{9,10},{10,... | collective-permute-start | bytes 98312 | tf_op jit(solution)/shard_map/ppermute | solution.py:383
  9.0 6.0 %collective-permute-start = (f32[32,256]{1,0:T(8,128)S(1)}, f32[32,256]{1,0:T(8,128)S(1)}, u32[]{:S(2)}, u32[]{:S(2)}) collective-permute-start(f32[32,256]{1,0:T(8,128)S(1)} %get-tuple-element.22), channel_id=1, source_target_pairs={{15,0},{0,14},{14,15},{1,2},{2,3},{3,1},{4,5},{5,4},{6,7},{7,6},{8... | collective-permute-start | bytes 98312 | tf_op jit(solution)/shard_map/ppermute | solution.py:383
  10.7 8.7 %collective-permute-start.6 = (f32[32,256]{1,0:T(8,128)S(1)}, f32[32,256]{1,0:T(8,128)S(1)}, u32[]{:S(2)}, u32[]{:S(2)}) collective-permute-start(f32[32,256]{1,0:T(8,128)S(1)} %get-tuple-element.26.refs_15_), channel_id=1, source_target_pairs={{0,1},{1,0},{2,3},{3,2},{4,5},{5,4},{6,7},{7,6},{8,9},{9,8},{10,11... | collective-permute-start | bytes 98312 | tf_op jit(solution)/shard_map/ppermute | solution.py:383
  11.6 9.1 %collective-permute-start.3 = (f32[32,256]{1,0:T(8,128)S(1)}, f32[32,256]{1,0:T(8,128)S(1)}, u32[]{:S(2)}, u32[]{:S(2)}) collective-permute-start(f32[32,256]{1,0:T(8,128)S(1)} %get-tuple-element.26.refs_15_), channel_id=1, source_target_pairs={{0,1},{1,2},{2,3},{3,4},{4,5},{5,6},{6,7},{7,8},{8,9},{9,10},{10,1... | collective-permute-start | bytes 98312 | tf_op jit(solution)/shard_map/ppermute | solution.py:383
  15.0 5.6 %copy-start = (bf16[256,256]{1,0:T(8,128)(2,1)S(1)}, bf16[256,256]{1,0:T(8,128)(2,1)}, u32[]{:S(2)}) copy-start(bf16[256,256]{1,0:T(8,128)(2,1)} %constant.32.clone.refs_2_.refs_3_.fwd_l) | copy-start | bytes 393220
  15.0 5.6 %copy-start.1 = (bf16[256,256]{1,0:T(8,128)(2,1)S(1)}, bf16[256,256]{1,0:T(8,128)(2,1)}, u32[]{:S(2)}) copy-start(bf16[256,256]{1,0:T(8,128)(2,1)} %constant.31.clone.refs_1_.refs_2_.fwd_h) | copy-start | bytes 393220
  15.0 5.6 %copy-start.2 = (bf16[128,192]{1,0:T(8,128)(2,1)S(1)}, bf16[128,192]{1,0:T(8,128)(2,1)}, u32[]{:S(2)}) copy-start(bf16[128,192]{1,0:T(8,128)(2,1)} %constant.26.clone.refs_1_.rows_b) | copy-start | bytes 147460
  18.8 3.2 %collective-permute-start.5 = (f32[32,256]{1,0:T(8,128)S(1)}, f32[32,256]{1,0:T(8,128)S(1)}, u32[]{:S(2)}, u32[]{:S(2)}) collective-permute-start(f32[32,256]{1,0:T(8,128)S(1)} %get-tuple-element.28.own), channel_id=1, source_target_pairs={{1,0},{2,1},{3,2},{4,3},{5,4},{6,5},{7,6},{8,7},{9,8},{10,9},{11,1... | collective-permute-start | bytes 98312 | tf_op jit(solution)/shard_map/ppermute | solution.py:383
  19.2 2.8 %collective-permute-start.4 = (f32[32,256]{1,0:T(8,128)S(1)}, f32[32,256]{1,0:T(8,128)S(1)}, u32[]{:S(2)}, u32[]{:S(2)}) collective-permute-start(f32[32,256]{1,0:T(8,128)S(1)} %get-tuple-element.28.own), channel_id=1, source_target_pairs={{0,1},{1,0},{2,3},{3,2},{4,5},{5,4},{6,7},{7,6},{8,9},{9,8},{10,11... | collective-permute-start | bytes 98312 | tf_op jit(solution)/shard_map/ppermute | solution.py:383

commit v8 on v7

--- a/solution.py
+++ b/solution.py
@@ -193,26 +193,26 @@
     ]
     for copy in [*masks, *tables, *last]:
         copy.start()
-    spectra = None
-    for i, cols in enumerate(columns):
-        if i == 0:
-            last[0].wait()
-            kernels, width = share_out.shape
-            whole = weights[0]
-            for k in range(1, kernels):
-                whole = whole + weights[k]
-            rows = [jnp.full((1, width), weights[k], F32) for k in range(kernels)]
-            share_out[...] = jnp.concatenate(rows, axis=0) / jnp.full((kernels, width), whole, F32)
-        if i == 0:
-            masks[0].wait()
+    last[0].wait()
+    kernels, width = share_out.shape
+    whole = weights[0]
+    for k in range(1, kernels):
+        whole = whole + weights[k]
+    rows = [jnp.full((1, width), weights[k], F32) for k in range(kernels)]
+    share_out[...] = jnp.concatenate(rows, axis=0) / jnp.full((kernels, width), whole, F32)
+    masks[0].wait()
+    rows = []
+    for cols in columns:
         transmit = jnp.tanh(mask[:, cols])
         slope_out[:, cols] = 1.0 - transmit * transmit
-        pieces = split(transmit)
-        if i == 0:
-            for copy in tables:
-                copy.wait()
-        term = quarter_turn(dot3(pieces, (fwd_h[...], fwd_l[...])), -i)
-        spectra = term if spectra is None else spectra + term
+        rows.append(transmit)
+    for copy in tables:
+        copy.wait()
+    terms = dot3(split(jnp.concatenate(rows, axis=0)), (fwd_h[...], fwd_l[...]))
+    count = mask.shape[0]
+    spectra = terms[:count]
+    for i in range(1, QUARTERS):
+        spectra = spectra + quarter_turn(terms[i * count : (i + 1) * count], -i)
     for copy in last[1:]:
         copy.wait()
     parts = dot3((proj_h[...], proj_l[...]), split(turn(spectra, -1)))

time: 22.2 us -> 22.3 us (level)
  no operation moved by 1% of the time
where the time goes in v8:
time: 22.3 us; the launch traced here: 22.1 us
  starting transfers between devices  8.22 us (37%)
  Pallas kernels  7.23 us (32%)
  waiting for transfers between devices  5.76 us (26%)
  between operations  0.83 us (4%)
    ppermute x7, starting transfers between devices, permute(): return lax.ppermute(value, 'tiles', pairs)  8.22 us
    pallas_call x6, Pallas kernels, call(): pl.pallas_call(kernel, out_shape=shapes, in_specs=in_specs or [VMEM] * le...  7.23 us
    ppermute x7, waiting for transfers between devices, permute(): return lax.ppermute(value, 'tiles', pairs)  5.76 us
  transfers between devices with their start and end apart: 7, of which 3 were waited for; matrix products, arithmetic and copies ran while one was open for 0% of the time, Pallas kernels for 23%

profile of v8, /device:TPU:0, one launch (start us, length us, event | category | flops | bytes accessed | tf_op | source)
XLA Modules:
  0.0 22.1 jit_solution(11272855498180478784)
XLA Ops:
  0.6 1.9 %shard_map.176 = (f32[32,256]{1,0:T(8,128)S(1)}, f32[32,256]{1,0:T(8,128)S(1)}, f32[32,256]{1,0:T(8,128)S(1)}, f32[16,256]{1,0:T(8,128)S(1)}, f32[128,1024]{1,0:T(8,128)S(1)}) custom-call(f32[128,1024]{1,0:T(8,128)} %refs_0_.3, bf16[256,256]{1,0:T(8,128)(2,1)} %constant.31.clone.refs_1_.refs_2_.fwd_h, bf16[256,256]{1,0:T(8,128)(2,1)} %constant.32.clone.refs_2_.refs_3_.fwd_l, ...), custom_call_target="tpu_custom_call" | custom-call | flops 2013265920 | bytes 1491008 | tf_op jit(solution)/shard_map/pallas_call | solution.py:370
  2.5 0.0 copy-start.3
  2.6 0.0 copy-start.5
  2.6 0.0 copy-start.6
  2.6 0.0 copy-start.7
  2.6 0.0 copy-start.8
  2.6 0.0 copy-start.9
  2.6 0.0 copy-start.10
  2.6 0.0 copy-start.11
  2.7 0.0 copy-start.12
  2.7 0.1 shard_map.177
  2.8 0.6 %collective-permute-start.1 = (f32[32,256]{1,0:T(8,128)S(1)}, f32[32,256]{1,0:T(8,128)S(1)}, u32[]{:S(2)}, u32[]{:S(2)}) collective-permute-start(f32[32,256]{1,0:T(8,128)S(1)} %get-tuple-element.23), channel_id=1, source_target_pairs={{0,1},{1,0},{2,3},{3,2},{4,5},{5,4},{6,7},{7,6},{8,9},{9,8},{10,11... | collective-permute-start | bytes 98312 | tf_op jit(solution)/shard_map/ppermute | solution.py:383
  3.4 5.7 %collective-permute-start.2 = (f32[32,256]{1,0:T(8,128)S(1)}, f32[32,256]{1,0:T(8,128)S(1)}, u32[]{:S(2)}, u32[]{:S(2)}) collective-permute-start(f32[32,256]{1,0:T(8,128)S(1)} %get-tuple-element.16.refs_6_), channel_id=1, source_target_pairs={{0,15},{1,2},{2,1},{3,4},{4,3},{5,6},{6,5},{7,8},{8,7},{9,10},{10,... | collective-permute-start | bytes 98312 | tf_op jit(solution)/shard_map/ppermute | solution.py:383
  9.0 0.5 %collective-permute-start = (f32[32,256]{1,0:T(8,128)S(1)}, f32[32,256]{1,0:T(8,128)S(1)}, u32[]{:S(2)}, u32[]{:S(2)}) collective-permute-start(f32[32,256]{1,0:T(8,128)S(1)} %get-tuple-element.22), channel_id=1, source_target_pairs={{15,0},{0,14},{14,15},{1,2},{2,3},{3,1},{4,5},{5,4},{6,7},{7,6},{8... | collective-permute-start | bytes 98312 | tf_op jit(solution)/shard_map/ppermute | solution.py:383
  9.5 1.1 %collective-permute-done.2.refs_1_ = f32[32,256]{1,0:T(8,128)S(1)} collective-permute-done((f32[32,256]{1,0:T(8,128)S(1)}, f32[32,256]{1,0:T(8,128)S(1)}, u32[]{:S(2)}, u32[]{:S(2)}) %collective-permute-start.2) | collective-permute-done | bytes 32800 | tf_op jit(solution)/shard_map/ppermute | solution.py:383
  10.7 0.9 %collective-permute-start.6 = (f32[32,256]{1,0:T(8,128)S(1)}, f32[32,256]{1,0:T(8,128)S(1)}, u32[]{:S(2)}, u32[]{:S(2)}) collective-permute-start(f32[32,256]{1,0:T(8,128)S(1)} %get-tuple-element.26.refs_15_), channel_id=1, source_target_pairs={{0,1},{1,0},{2,3},{3,2},{4,5},{5,4},{6,7},{7,6},{8,9},{9,8},{10,11... | collective-permute-start | bytes 98312 | tf_op jit(solution)/shard_map/ppermute | solution.py:383
  11.6 0.1 collective-permute-start.3
  11.7 3.4 %collective-permute-done.refs_1_ = f32[32,256]{1,0:T(8,128)S(1)} collective-permute-done((f32[32,256]{1,0:T(8,128)S(1)}, f32[32,256]{1,0:T(8,128)S(1)}, u32[]{:S(2)}, u32[]{:S(2)}) %collective-permute-start) | collective-permute-done | bytes 32800 | tf_op jit(solution)/shard_map/ppermute | solution.py:383
  15.1 3.8 %shard_map.179 = (f32[128,1024]{1,0:T(8,128)}, f32[32,256]{1,0:T(8,128)S(1)}) custom-call(f32[32,256]{1,0:T(8,128)S(1)} %get-tuple-element.21.refs_0_, f32[32,256]{1,0:T(8,128)S(1)} %collective-permute-done.refs_1_, f32[32,256]{1,0:T(8,128)S(1)} %collective-permute-done.1.refs_2_, ...), custom_call_target="tpu_custom_call", output_to_operand_aliasing={{0}: (14, {})} | custom-call | flops 1610612736 | bytes 4063232 | tf_op jit(solution)/shard_map/pallas_call | solution.py:370
  18.8 0.4 %collective-permute-start.5 = (f32[32,256]{1,0:T(8,128)S(1)}, f32[32,256]{1,0:T(8,128)S(1)}, u32[]{:S(2)}, u32[]{:S(2)}) collective-permute-start(f32[32,256]{1,0:T(8,128)S(1)} %get-tuple-element.28.own), channel_id=1, source_target_pairs={{1,0},{2,1},{3,2},{4,3},{5,4},{6,5},{7,6},{8,7},{9,8},{10,9},{11,1... | collective-permute-start | bytes 98312 | tf_op jit(solution)/shard_map/ppermute | solution.py:383
  19.2 0.2 collective-permute-start.4
  19.4 1.3 %collective-permute-done.3.before.before_even = f32[32,256]{1,0:T(8,128)S(1)} collective-permute-done((f32[32,256]{1,0:T(8,128)S(1)}, f32[32,256]{1,0:T(8,128)S(1)}, u32[]{:S(2)}, u32[]{:S(2)}) %collective-permute-start.3) | collective-permute-done | bytes 32800 | tf_op jit(solution)/shard_map/ppermute | solution.py:383
  20.7 1.3 %shard_map.180._ = f32[128,1024]{1,0:T(8,128)} custom-call(f32[32,256]{1,0:T(8,128)S(1)} %get-tuple-element.28.own, f32[32,256]{1,0:T(8,128)S(1)} %collective-permute-done.3.before.before_even, f32[32,256]{1,0:T(8,128)S(1)} %collective-permute-done.6.after, f32[128,1024]{1,0:T(8,128)S(1)} %get-tuple-element.29.refs_0_.slope, bf16[128,192]{1,0:T(8,128)(2,1)S(1)} %copy-done.2, ...), custom_call_target="tpu_custom_call" | custom-call | flops 201326592 | bytes 1458176 | tf_op jit(solution)/shard_map/pallas_call | solution.py:370
  22.1 0.1 shard_map.181
  (22 shorter events, 0.1 us)
Async XLA Ops:
  2.5 8.1 %copy-start.3 = (f32[2,16,32,128]{3,2,1,0:T(8,128)S(1)}, f32[2,16,32,128]{3,2,1,0:T(8,128)}, u32[]{:S(2)}) copy-start(f32[2,16,32,128]{3,2,1,0:T(8,128)} %refs_3_.6) | copy-start | bytes 1572868
  2.6 8.1 %copy-start.4 = (s32[128,1024]{1,0:T(8,128)S(1)}, s32[128,1024]{1,0:T(8,128)}, u32[]{:S(2)}) copy-start(s32[128,1024]{1,0:T(8,128)} %refs_5_.7) | copy-start | bytes 1572868
  2.6 8.1 %copy-start.5 = (bf16[256,1024]{1,0:T(8,128)(2,1)S(1)}, bf16[256,1024]{1,0:T(8,128)(2,1)}, u32[]{:S(2)}) copy-start(bf16[256,1024]{1,0:T(8,128)(2,1)} %constant.36.clone.refs_13_) | copy-start | bytes 1572868
  2.6 8.1 %copy-start.6 = (bf16[256,1024]{1,0:T(8,128)(2,1)S(1)}, bf16[256,1024]{1,0:T(8,128)(2,1)}, u32[]{:S(2)}) copy-start(bf16[256,1024]{1,0:T(8,128)(2,1)} %constant.35.clone.refs_12_) | copy-start | bytes 1572868
  2.6 8.1 %copy-start.7 = (bf16[256,512]{1,0:T(8,128)(2,1)S(1)}, bf16[256,512]{1,0:T(8,128)(2,1)}, u32[]{:S(2)}) copy-start(bf16[256,512]{1,0:T(8,128)(2,1)} %constant.28.clone.refs_9_) | copy-start | bytes 786436
  2.6 8.0 %copy-start.8 = (bf16[256,512]{1,0:T(8,128)(2,1)S(1)}, bf16[256,512]{1,0:T(8,128)(2,1)}, u32[]{:S(2)}) copy-start(bf16[256,512]{1,0:T(8,128)(2,1)} %constant.27.clone.refs_8_) | copy-start | bytes 786436
  2.6 8.0 %copy-start.9 = (bf16[128,192]{1,0:T(8,128)(2,1)S(1)}, bf16[128,192]{1,0:T(8,128)(2,1)}, u32[]{:S(2)}) copy-start(bf16[128,192]{1,0:T(8,128)(2,1)} %constant.37.clone.refs_10_) | copy-start | bytes 147460
  2.6 8.0 %copy-start.10 = (bf16[128,256]{1,0:T(8,128)(2,1)S(1)}, bf16[128,256]{1,0:T(8,128)(2,1)}, u32[]{:S(2)}) copy-start(bf16[128,256]{1,0:T(8,128)(2,1)} %constant.30.clone.refs_7_) | copy-start | bytes 196612
  2.6 8.0 %copy-start.11 = (bf16[128,192]{1,0:T(8,128)(2,1)S(1)}, bf16[128,192]{1,0:T(8,128)(2,1)}, u32[]{:S(2)}) copy-start(bf16[128,192]{1,0:T(8,128)(2,1)} %constant.29.clone.refs_6_) | copy-start | bytes 147460
  2.7 8.0 %copy-start.12 = (bf16[64,384]{1,0:T(8,128)(2,1)S(1)}, bf16[64,384]{1,0:T(8,128)(2,1)}, u32[]{:S(2)}) copy-start(bf16[64,384]{1,0:T(8,128)(2,1)} %constant.38.clone.refs_11_) | copy-start | bytes 147460
  2.8 6.7 %collective-permute-start.1 = (f32[32,256]{1,0:T(8,128)S(1)}, f32[32,256]{1,0:T(8,128)S(1)}, u32[]{:S(2)}, u32[]{:S(2)}) collective-permute-start(f32[32,256]{1,0:T(8,128)S(1)} %get-tuple-element.23), channel_id=1, source_target_pairs={{0,1},{1,0},{2,3},{3,2},{4,5},{5,4},{6,7},{7,6},{8,9},{9,8},{10,11... | collective-permute-start | bytes 98312 | tf_op jit(solution)/shard_map/ppermute | solution.py:383
  3.4 7.3 %collective-permute-start.2 = (f32[32,256]{1,0:T(8,128)S(1)}, f32[32,256]{1,0:T(8,128)S(1)}, u32[]{:S(2)}, u32[]{:S(2)}) collective-permute-start(f32[32,256]{1,0:T(8,128)S(1)} %get-tuple-element.16.refs_6_), channel_id=1, source_target_pairs={{0,15},{1,2},{2,1},{3,4},{4,3},{5,6},{6,5},{7,8},{8,7},{9,10},{10,... | collective-permute-start | bytes 98312 | tf_op jit(solution)/shard_map/ppermute | solution.py:383
  9.0 6.0 %collective-permute-start = (f32[32,256]{1,0:T(8,128)S(1)}, f32[32,256]{1,0:T(8,128)S(1)}, u32[]{:S(2)}, u32[]{:S(2)}) collective-permute-start(f32[32,256]{1,0:T(8,128)S(1)} %get-tuple-element.22), channel_id=1, source_target_pairs={{15,0},{0,14},{14,15},{1,2},{2,3},{3,1},{4,5},{5,4},{6,7},{7,6},{8... | collective-permute-start | bytes 98312 | tf_op jit(solution)/shard_map/ppermute | solution.py:383
  10.7 8.7 %collective-permute-start.6 = (f32[32,256]{1,0:T(8,128)S(1)}, f32[32,256]{1,0:T(8,128)S(1)}, u32[]{:S(2)}, u32[]{:S(2)}) collective-permute-start(f32[32,256]{1,0:T(8,128)S(1)} %get-tuple-element.26.refs_15_), channel_id=1, source_target_pairs={{0,1},{1,0},{2,3},{3,2},{4,5},{5,4},{6,7},{7,6},{8,9},{9,8},{10,11... | collective-permute-start | bytes 98312 | tf_op jit(solution)/shard_map/ppermute | solution.py:383
  11.6 9.1 %collective-permute-start.3 = (f32[32,256]{1,0:T(8,128)S(1)}, f32[32,256]{1,0:T(8,128)S(1)}, u32[]{:S(2)}, u32[]{:S(2)}) collective-permute-start(f32[32,256]{1,0:T(8,128)S(1)} %get-tuple-element.26.refs_15_), channel_id=1, source_target_pairs={{0,1},{1,2},{2,3},{3,4},{4,5},{5,6},{6,7},{7,8},{8,9},{9,10},{10,1... | collective-permute-start | bytes 98312 | tf_op jit(solution)/shard_map/ppermute | solution.py:383
  15.1 5.6 %copy-start = (bf16[256,256]{1,0:T(8,128)(2,1)S(1)}, bf16[256,256]{1,0:T(8,128)(2,1)}, u32[]{:S(2)}) copy-start(bf16[256,256]{1,0:T(8,128)(2,1)} %constant.32.clone.refs_2_.refs_3_.fwd_l) | copy-start | bytes 393220
  15.1 5.6 %copy-start.1 = (bf16[256,256]{1,0:T(8,128)(2,1)S(1)}, bf16[256,256]{1,0:T(8,128)(2,1)}, u32[]{:S(2)}) copy-start(bf16[256,256]{1,0:T(8,128)(2,1)} %constant.31.clone.refs_1_.refs_2_.fwd_h) | copy-start | bytes 393220
  15.1 5.6 %copy-start.2 = (bf16[128,192]{1,0:T(8,128)(2,1)S(1)}, bf16[128,192]{1,0:T(8,128)(2,1)}, u32[]{:S(2)}) copy-start(bf16[128,192]{1,0:T(8,128)(2,1)} %constant.26.clone.refs_1_.rows_b) | copy-start | bytes 147460
  18.8 3.2 %collective-permute-start.5 = (f32[32,256]{1,0:T(8,128)S(1)}, f32[32,256]{1,0:T(8,128)S(1)}, u32[]{:S(2)}, u32[]{:S(2)}) collective-permute-start(f32[32,256]{1,0:T(8,128)S(1)} %get-tuple-element.28.own), channel_id=1, source_target_pairs={{1,0},{2,1},{3,2},{4,3},{5,4},{6,5},{7,6},{8,7},{9,8},{10,9},{11,1... | collective-permute-start | bytes 98312 | tf_op jit(solution)/shard_map/ppermute | solution.py:383
  19.2 2.8 %collective-permute-start.4 = (f32[32,256]{1,0:T(8,128)S(1)}, f32[32,256]{1,0:T(8,128)S(1)}, u32[]{:S(2)}, u32[]{:S(2)}) collective-permute-start(f32[32,256]{1,0:T(8,128)S(1)} %get-tuple-element.28.own), channel_id=1, source_target_pairs={{0,1},{1,0},{2,3},{3,2},{4,5},{5,4},{6,7},{7,6},{8,9},{9,8},{10,11... | collective-permute-start | bytes 98312 | tf_op jit(solution)/shard_map/ppermute | solution.py:383
